TPU v7x, 256 devices: a whole 4x4x8 slice. The times are simulated.
256 devices in a mesh: section: 4 (over z_lo), dp: 32 (over x, y, core), tensor: 2 (over z_hi).
Axes of the slice: x: 4, y: 4, z: 8 (z_hi: 2, z_lo: 4; z = z_hi * 4 + z_lo), core: 2. Of those that a mesh axis runs over, the one named last changes fastest.
Arguments:
- inputs: bfloat16 [2, 4096, 768], P(None, 'dp'), may hold values from -6 to 6
- out_grads: bfloat16 [2, 4096, 768], P(None, 'dp'), may hold values from -6 to 6
- norm_gain: float32 [4, 768], P('section'), may hold values from 0.1 to 1.9
- up_weight: bfloat16 [4, 768, 3072], P('section', None, 'tensor'), may hold values from -0.21875 to 0.21875
- down_weight: bfloat16 [4, 3072, 768], P('section', 'tensor'), may hold values from -0.109375 to 0.109375
- prior_up_grad: bfloat16 [32, 4, 768, 3072], P('dp', 'section', None, 'tensor'), may hold values from -6 to 6
- prior_down_grad: bfloat16 [32, 4, 3072, 768], P('dp', 'section', 'tensor'), may hold values from -6 to 6
- master_up: float32 [4, 768, 3072], P('section', 'dp', 'tensor'), may hold values from -0.3 to 0.3
- master_down: float32 [4, 3072, 768], P('section', ('tensor', 'dp')), may hold values from -0.3 to 0.3
Outputs:
- layer_outputs: bfloat16 [4, 2, 4096, 768], P('section', None, 'dp')
- input_grads: bfloat16 [4, 2, 4096, 768], P('section', None, 'dp')
- new_up: float32 [4, 768, 3072], P('section', 'dp', 'tensor')
- new_down: float32 [4, 3072, 768], P('section', ('tensor', 'dp'))
All inputs are finite; a program needn't handle non-finite values.
Results may differ from a plain program's by a relative error of at most 0.019.
Values may be sent and summed in bfloat16 or wider, within the bound.
No kernel may reach another device: no remote copies, remote signals or barrier semaphores. Data moves between devices by JAX's collectives and lax.ppermute only.
A program may use at most 128 MiB of HBM per device.

v0:
```python
import jax
import jax.numpy as jnp
from jax import lax
from jax.sharding import PartitionSpec as P

eps_norm = 1e-05
gelu_coef = 0.7978845608028654
learning_rate = 0.05


def from_everyone(value, axis):
    copies = jnp.broadcast_to(value, (lax.axis_size(axis), *value.shape))
    return lax.all_to_all(copies, axis, split_axis=0, concat_axis=0, tiled=True)


def taken_together(value, axis):
    everything = from_everyone(value, axis)
    return jnp.sum(everything.astype(jnp.float32), axis=0)


def total_of_pieces(value, axis):
    blocks = lax.all_gather(value, axis).astype(jnp.float32)
    return blocks.sum(axis=0)


def cut_along(value, dim, devices):
    before, after = (value.shape[:dim], value.shape[dim + 1 :])
    return jnp.moveaxis(value.reshape(*before, devices, -1, *after), dim, 0)


def sum_together(arrays, axis, dims):
    devices = lax.axis_size(axis)
    blocks = [cut_along(a, dim, devices) for a, dim in zip(arrays, dims)]
    lines = jnp.concatenate([b.reshape(devices, -1) for b in blocks], axis=1)
    width = max(16, -(-lines.shape[1] // 1024) * 8)
    lines = jnp.pad(lines, ((0, 0), (0, width * 128 - lines.shape[1]))).reshape(-1, 128)
    flat, at, finished = (lax.psum_scatter(lines, axis, tiled=True).reshape(-1), 0, [])
    for b in blocks:
        part = b[0]
        finished.append(flat[at : at + part.size].reshape(part.shape))
        at += part.size
    return tuple(finished)


def shifted(value, axis, steps):
    count = lax.axis_size(axis)
    initial, last = (max(0, -steps), min(count, count - steps))
    return lax.ppermute(value, axis, [(source, source + steps) for source in range(initial, last)])


def gelu_tanh(value):
    inner = jnp.tanh(gelu_coef * (value + 0.044715 * value * value * value))
    return 0.5 * value * (1.0 + inner)


def gelu_slope(value):
    inner = jnp.tanh(gelu_coef * (value + 0.044715 * value * value * value))
    return 0.5 * (1.0 + inner) + 0.5 * value * (1.0 - inner * inner) * gelu_coef * (
        1.0 + 3.0 * 0.044715 * value * value
    )


def apply_norm(layer_entry_input, gain_vector):
    values = layer_entry_input.astype(jnp.float32)
    center = jnp.mean(values, axis=-1, keepdims=True)
    centered_rows = values - center
    spread = jnp.mean(centered_rows * centered_rows, axis=-1, keepdims=True)
    inverse_scale = lax.rsqrt(spread + eps_norm)
    standardized_input = centered_rows * inverse_scale
    return (
        (standardized_input * gain_vector).astype(jnp.bfloat16),
        standardized_input,
        inverse_scale,
    )


def layer_forward(layer_entry_input, gain_vector, w_up, w_down):
    normalized_rows, standardized_input, inverse_scale = apply_norm(layer_entry_input, gain_vector)
    upper = jnp.dot(normalized_rows, w_up, preferred_element_type=jnp.float32)
    active = gelu_tanh(upper).astype(jnp.bfloat16)
    partial_value = jnp.dot(active, w_down, preferred_element_type=jnp.float32)
    mixed = taken_together(partial_value.astype(jnp.bfloat16), "tensor").astype(jnp.float32)
    return (layer_entry_input.astype(jnp.float32) + mixed).astype(jnp.bfloat16)


def norm_gradient_pass(
    normalized_gradient, upstream_gradient, gain_vector, standardized_input, inverse_scale
):
    rescaled_rows = normalized_gradient * gain_vector
    leading_operand = jnp.mean(rescaled_rows, axis=-1, keepdims=True)
    trailing_operand = jnp.mean(rescaled_rows * standardized_input, axis=-1, keepdims=True)
    final_output = upstream_gradient.astype(jnp.float32) + inverse_scale * (
        rescaled_rows - leading_operand - standardized_input * trailing_operand
    )
    return final_output.astype(jnp.bfloat16)


def layer_backward(layer_entry_input, upstream_gradient, gain_vector, w_up, w_down):
    normalized_rows, standardized_input, inverse_scale = apply_norm(layer_entry_input, gain_vector)
    upper = jnp.dot(normalized_rows, w_up, preferred_element_type=jnp.float32)
    grad_act = lax.dot_general(
        upstream_gradient, w_down, (((1,), (1,)), ((), ())), preferred_element_type=jnp.float32
    )
    grad_up = (grad_act * gelu_slope(upper)).astype(jnp.bfloat16)
    partial_value = lax.dot_general(
        grad_up, w_up, (((1,), (1,)), ((), ())), preferred_element_type=jnp.float32
    )
    normalized_gradient = total_of_pieces(partial_value.astype(jnp.bfloat16), "tensor").astype(
        jnp.float32
    )
    return norm_gradient_pass(
        normalized_gradient, upstream_gradient, gain_vector, standardized_input, inverse_scale
    )


def store_row(buffer, row_value, slot_index, in_range):
    previous = lax.dynamic_index_in_dim(buffer, slot_index, 0, keepdims=False)
    chosen = jnp.where(in_range, row_value, previous)
    return lax.dynamic_update_index_in_dim(buffer, chosen, slot_index, 0)


def local(
    inputs,
    out_grads,
    norm_gain,
    up_weight,
    down_weight,
    prior_up_grad,
    prior_down_grad,
    master_up,
    master_down,
):
    totals = tuple(
        (
            part.astype(jnp.float32)
            for part in sum_together(
                (
                    prior_up_grad.astype(jnp.float32).astype(jnp.bfloat16),
                    prior_down_grad.astype(jnp.float32).astype(jnp.bfloat16),
                ),
                "dp",
                (2, 2),
            )
        )
    )
    up_total = totals[0][0]
    down_total = totals[1][0]
    new_up = master_up - learning_rate * up_total
    new_down = master_down - learning_rate * down_total
    sections = lax.axis_size("section")
    section_index = lax.axis_index("section")
    micro_count = inputs.shape[0]
    tick_count = micro_count + sections - 1
    gain_vector = norm_gain[0]
    w_up = up_weight[0]
    w_down = down_weight[0]
    stashed = jnp.zeros_like(inputs)
    produced = jnp.zeros_like(inputs)
    carried = jnp.zeros(inputs.shape[1:], jnp.bfloat16)
    for tick in range(tick_count):
        fresh_rows = inputs[min(tick, micro_count - 1)]
        layer_entry_input = jnp.where(section_index == 0, fresh_rows, carried)
        layer_out = layer_forward(layer_entry_input, gain_vector, w_up, w_down)
        micro_index = tick - section_index
        in_range = (micro_index >= 0) & (micro_index < micro_count)
        slot_index = jnp.clip(micro_index, 0, micro_count - 1)
        stashed = store_row(stashed, layer_entry_input, slot_index, in_range)
        produced = store_row(produced, layer_out, slot_index, in_range)
        if tick + 1 < tick_count:
            carried = shifted(layer_out, "section", 1)
    grads_done = jnp.zeros_like(inputs)
    carried_grad = jnp.zeros(inputs.shape[1:], jnp.bfloat16)
    for tick in range(tick_count):
        seed_grad = out_grads[min(tick, micro_count - 1)]
        upstream_gradient = jnp.where(section_index == sections - 1, seed_grad, carried_grad)
        micro_index = tick - (sections - 1 - section_index)
        in_range = (micro_index >= 0) & (micro_index < micro_count)
        slot_index = jnp.clip(micro_index, 0, micro_count - 1)
        layer_entry_input = lax.dynamic_index_in_dim(stashed, slot_index, 0, keepdims=False)
        input_grad = layer_backward(layer_entry_input, upstream_gradient, gain_vector, w_up, w_down)
        grads_done = store_row(grads_done, input_grad, slot_index, in_range)
        if tick + 1 < tick_count:
            carried_grad = shifted(input_grad, "section", -1)
    return (produced[None], grads_done[None], new_up, new_down)


def solution(mesh):
    placed = (
        P(None, "dp", None),
        P(None, "dp", None),
        P("section", None),
        P("section", None, "tensor"),
        P("section", "tensor", None),
        P("dp", "section", None, "tensor"),
        P("dp", "section", "tensor", None),
        P("section", "dp", "tensor"),
        P("section", ("tensor", "dp"), None),
    )
    return jax.shard_map(
        local,
        mesh=mesh,
        in_specs=placed,
        out_specs=(
            P("section", None, "dp", None),
            P("section", None, "dp", None),
            P("section", "dp", "tensor"),
            P("section", ("tensor", "dp"), None),
        ),
        check_vma=False,
    )
```

profile of v0, /device:TPU:6, one launch (start us, length us, event | category | flops | bytes accessed | tf_op | source)
XLA Modules:
  0.0 314.5 jit_solution(1875935882690995203)
XLA Ops:
  13.9 8.5 %all-to-all-start = ((bf16[2,128,768]{2,1,0:T(8,128)(2,1)}), bf16[2,128,768]{2,1,0:T(8,128)(2,1)S(1)}, u32[]{:S(2)}, u32[]{:S(2)}) async-start(bf16[2,128,768]{2,1,0:T(8,128)(2,1)} %broadcast_in_dim.91), calls=%async_computation | async-start | bytes 786432 | tf_op jit(solution)/shard_map/all_to_all | solution.py:13
  22.3 13.8 %all-to-all-done = bf16[2,128,768]{2,1,0:T(8,128)(2,1)S(1)} async-done(((bf16[2,128,768]{2,1,0:T(8,128)(2,1)}), bf16[2,128,768]{2,1,0:T(8,128)(2,1)S(1)}, u32[]{:S(2)}, u32[]{:S(2)}) %all-to-all-start) | async-done | bytes 393248 | tf_op jit(solution)/shard_map/all_to_all | solution.py:13
  36.9 4.4 %collective-permute-start = (bf16[128,768]{1,0:T(8,128)(2,1)S(1)}, bf16[128,768]{1,0:T(8,128)(2,1)}, u32[]{:S(2)}, u32[]{:S(2)}) collective-permute-start(bf16[128,768]{1,0:T(8,128)(2,1)S(1)} %fusion.239), channel_id=1, source_target_pairs={{0,64},{64,128},{128,192},{1,65},{65,129},{129,193},{2,66},{66,130... | collective-permute-start | bytes 589832 | tf_op jit(solution)/shard_map/ppermute | solution.py:48
  56.2 13.0 %all-to-all-done.1 = bf16[2,128,768]{2,1,0:T(8,128)(2,1)} async-done(((bf16[2,128,768]{2,1,0:T(8,128)(2,1)}), bf16[2,128,768]{2,1,0:T(8,128)(2,1)}, u32[]{:S(2)}, u32[]{:S(2)}) %all-to-all-start.1) | async-done | bytes 393248 | tf_op jit(solution)/shard_map/all_to_all | solution.py:13
  72.1 4.5 %collective-permute-start.1 = (bf16[128,768]{1,0:T(8,128)(2,1)}, bf16[128,768]{1,0:T(8,128)(2,1)}, u32[]{:S(2)}, u32[]{:S(2)}) collective-permute-start(bf16[128,768]{1,0:T(8,128)(2,1)} %get-tuple-element.42), channel_id=1, source_target_pairs={{0,64},{64,128},{128,192},{1,65},{65,129},{129,193},{2,66},{66,130... | collective-permute-start | bytes 589832 | tf_op jit(solution)/shard_map/ppermute | solution.py:48
  91.0 13.3 %all-to-all-done.2 = bf16[2,128,768]{2,1,0:T(8,128)(2,1)} async-done(((bf16[2,128,768]{2,1,0:T(8,128)(2,1)}), bf16[2,128,768]{2,1,0:T(8,128)(2,1)}, u32[]{:S(2)}, u32[]{:S(2)}) %all-to-all-start.2) | async-done | bytes 393248 | tf_op jit(solution)/shard_map/all_to_all | solution.py:13
  124.4 4.4 %reshape_transpose_reshape.6 = bf16[32,36864]{1,0:T(8,128)(2,1)} reshape(bf16[1,1,768,1536]{3,2,1,0:T(8,128)(2,1)} %param.14) | data formatting | bytes 4718592 | tf_op jit(solution)/shard_map/reshape;transpose;reshape | solution.py:34
  128.8 4.3 %reshape_transpose_reshape.7 = bf16[32,36864]{1,0:T(8,128)(2,1)} reshape(bf16[1,1,1536,768]{3,2,1,0:T(8,128)(2,1)} %param.15) | data formatting | bytes 4718592 | tf_op jit(solution)/shard_map/reshape;transpose;reshape | solution.py:34
  133.8 4.7 %all-to-all-done.3 = bf16[2,128,768]{2,1,0:T(8,128)(2,1)} async-done(((bf16[2,128,768]{2,1,0:T(8,128)(2,1)}), bf16[2,128,768]{2,1,0:T(8,128)(2,1)}, u32[]{:S(2)}, u32[]{:S(2)}) %all-to-all-start.3) | async-done | bytes 393248 | tf_op jit(solution)/shard_map/all_to_all | solution.py:13
  141.3 5.5 %collective-permute-start.3 = (bf16[128,768]{1,0:T(8,128)(2,1)}, bf16[128,768]{1,0:T(8,128)(2,1)}, u32[]{:S(2)}, u32[]{:S(2)}) collective-permute-start(bf16[128,768]{1,0:T(8,128)(2,1)} %get-tuple-element.38), channel_id=1, source_target_pairs={{0,64},{64,128},{128,192},{1,65},{65,129},{129,193},{2,66},{66,130... | collective-permute-start | bytes 589832 | tf_op jit(solution)/shard_map/ppermute | solution.py:48
  146.8 4.8 %pad_maximum_fusion = bf16[32,73728]{1,0:T(8,128)(2,1)} fusion(bf16[32,36864]{1,0:T(8,128)(2,1)} %reshape_transpose_reshape.7, bf16[32,36864]{1,0:T(8,128)(2,1)} %reshape_transpose_reshape.6), kind=kLoop, calls=%fused_computation | loop fusion | flops 9437184 | bytes 9437184 | tf_op jit(solution)/shard_map/concatenate | solution.py:34
  151.7 6.0 %reshape.451 = bf16[18432,128]{1,0:T(8,128)(2,1)} reshape(bf16[32,73728]{1,0:T(8,128)(2,1)} %pad_maximum_fusion) | data formatting | bytes 9437184 | tf_op jit(solution)/shard_map/reshape | solution.py:36
  176.6 14.0 %all-gather = bf16[256,768]{1,0:T(8,128)(2,1)S(1)} all-gather(bf16[128,768]{1,0:T(8,128)(2,1)} %fusion.60), channel_id=2, replica_groups=mesh['section'=4,'dp'=32,'tensor'=2] {'tensor'}, dimensions={0}, use_global_device_ids=true | all-gather | bytes 589824 | tf_op jit(solution)/shard_map/all_gather | solution.py:22
  202.5 4.4 %fusion.65 = bf16[128,768]{1,0:T(8,128)(2,1)} fusion(bf16[1,768,1536]{2,1,0:T(8,128)(2,1)S(1)} %copy-done, bf16[1,1536,768]{2,1,0:T(8,128)(2,1)} %param.13, f32[128,1536]{1,0:T(8,128)} %fusion.34, bf16[128,768]{1,0:T(8,128)(2,1)} %collective-permute-done.4, pred[]{:T(512)S(6)} %eq.5, bf16[2,128,768]{2,1,0:T(8,128)(2,1)} %param.10), kind=kOutput, calls=%fused_computation.72 | convolution fusion | flops 607911936 | bytes 6094849 | tf_op jit(solution)/shard_map/dot_general | solution.py:105
  206.9 11.0 %all-gather.1 = bf16[256,768]{1,0:T(8,128)(2,1)S(1)} all-gather(bf16[128,768]{1,0:T(8,128)(2,1)} %fusion.65), channel_id=3, replica_groups=mesh['section'=4,'dp'=32,'tensor'=2] {'tensor'}, dimensions={0}, use_global_device_ids=true | all-gather | bytes 589824 | tf_op jit(solution)/shard_map/all_gather | solution.py:22
  223.7 8.0 %collective-permute-done.5 = bf16[128,768]{1,0:T(8,128)(2,1)} collective-permute-done((bf16[128,768]{1,0:T(8,128)(2,1)S(1)}, bf16[128,768]{1,0:T(8,128)(2,1)}, u32[]{:S(2)}, u32[]{:S(2)}) %collective-permute-start.5) | collective-permute-done | bytes 196640 | tf_op jit(solution)/shard_map/ppermute | solution.py:48
  231.7 4.4 %fusion.70 = bf16[128,768]{1,0:T(8,128)(2,1)} fusion(bf16[1,768,1536]{2,1,0:T(8,128)(2,1)S(1)} %copy-done, bf16[1,1536,768]{2,1,0:T(8,128)(2,1)} %param.13, f32[128,1536]{1,0:T(8,128)} %fusion.30, bf16[128,768]{1,0:T(8,128)(2,1)} %collective-permute-done.5, pred[]{:T(512)S(6)} %eq.5, bf16[2,128,768]{2,1,0:T(8,128)(2,1)} %param.10), kind=kOutput, calls=%fused_computation.73 | convolution fusion | flops 607911936 | bytes 6094849 | tf_op jit(solution)/shard_map/dot_general | solution.py:105
  236.1 11.5 %all-gather.2 = bf16[256,768]{1,0:T(8,128)(2,1)S(1)} all-gather(bf16[128,768]{1,0:T(8,128)(2,1)} %fusion.70), channel_id=4, replica_groups=mesh['section'=4,'dp'=32,'tensor'=2] {'tensor'}, dimensions={0}, use_global_device_ids=true | all-gather | bytes 589824 | tf_op jit(solution)/shard_map/all_gather | solution.py:22
  253.8 6.2 %collective-permute-done.6 = bf16[128,768]{1,0:T(8,128)(2,1)} collective-permute-done((bf16[128,768]{1,0:T(8,128)(2,1)}, bf16[128,768]{1,0:T(8,128)(2,1)}, u32[]{:S(2)}, u32[]{:S(2)}) %collective-permute-start.6) | collective-permute-done | bytes 196640 | tf_op jit(solution)/shard_map/ppermute | solution.py:48
  260.0 4.4 %fusion.75 = bf16[128,768]{1,0:T(8,128)(2,1)} fusion(bf16[1,768,1536]{2,1,0:T(8,128)(2,1)S(1)} %copy-done, bf16[1,1536,768]{2,1,0:T(8,128)(2,1)} %param.13, f32[128,1536]{1,0:T(8,128)} %fusion.26, bf16[128,768]{1,0:T(8,128)(2,1)} %collective-permute-done.6, pred[]{:T(512)S(6)} %eq.5, bf16[2,128,768]{2,1,0:T(8,128)(2,1)} %param.10), kind=kOutput, calls=%fused_computation.74 | convolution fusion | flops 607911936 | bytes 6094849 | tf_op jit(solution)/shard_map/dot_general | solution.py:105
  264.4 12.4 %all-gather.3 = bf16[256,768]{1,0:T(8,128)(2,1)S(1)} all-gather(bf16[128,768]{1,0:T(8,128)(2,1)} %fusion.75), channel_id=5, replica_groups=mesh['section'=4,'dp'=32,'tensor'=2] {'tensor'}, dimensions={0}, use_global_device_ids=true | all-gather | bytes 589824 | tf_op jit(solution)/shard_map/all_gather | solution.py:22
  281.5 4.8 %collective-permute-done.7 = bf16[128,768]{1,0:T(8,128)(2,1)} collective-permute-done((bf16[128,768]{1,0:T(8,128)(2,1)S(1)}, bf16[128,768]{1,0:T(8,128)(2,1)}, u32[]{:S(2)}, u32[]{:S(2)}) %collective-permute-start.7) | collective-permute-done | bytes 196640 | tf_op jit(solution)/shard_map/ppermute | solution.py:48
  286.2 4.4 %fusion.80 = bf16[128,768]{1,0:T(8,128)(2,1)} fusion(bf16[1,768,1536]{2,1,0:T(8,128)(2,1)S(1)} %copy-done, bf16[1,1536,768]{2,1,0:T(8,128)(2,1)} %param.13, f32[128,1536]{1,0:T(8,128)} %fusion.22, bf16[128,768]{1,0:T(8,128)(2,1)} %collective-permute-done.7, pred[]{:T(512)S(6)} %eq.5, bf16[2,128,768]{2,1,0:T(8,128)(2,1)} %param.10), kind=kOutput, calls=%fused_computation.75 | convolution fusion | flops 607911936 | bytes 6094849 | tf_op jit(solution)/shard_map/dot_general | solution.py:105
  290.6 10.7 %all-gather.4 = bf16[256,768]{1,0:T(8,128)(2,1)S(1)} all-gather(bf16[128,768]{1,0:T(8,128)(2,1)} %fusion.80), channel_id=6, replica_groups=mesh['section'=4,'dp'=32,'tensor'=2] {'tensor'}, dimensions={0}, use_global_device_ids=true | all-gather | bytes 589824 | tf_op jit(solution)/shard_map/all_gather | solution.py:22
  (181 shorter events, 116.3 us)
Async XLA Ops:
  10.2 25.9 %copy-start.1 = (bf16[2,128,768]{2,1,0:T(8,128)(2,1)S(1)}, bf16[2,128,768]{2,1,0:T(8,128)(2,1)}, u32[]{:S(2)}) copy-start(bf16[2,128,768]{2,1,0:T(8,128)(2,1)} %param.9) | copy-start | bytes 1179652
  13.9 22.3 %all-to-all-start = ((bf16[2,128,768]{2,1,0:T(8,128)(2,1)}), bf16[2,128,768]{2,1,0:T(8,128)(2,1)S(1)}, u32[]{:S(2)}, u32[]{:S(2)}) async-start(bf16[2,128,768]{2,1,0:T(8,128)(2,1)} %broadcast_in_dim.91), calls=%async_computation | async-start | bytes 786432 | tf_op jit(solution)/shard_map/all_to_all | solution.py:13
  36.9 7.1 %collective-permute-start = (bf16[128,768]{1,0:T(8,128)(2,1)S(1)}, bf16[128,768]{1,0:T(8,128)(2,1)}, u32[]{:S(2)}, u32[]{:S(2)}) collective-permute-start(bf16[128,768]{1,0:T(8,128)(2,1)S(1)} %fusion.239), channel_id=1, source_target_pairs={{0,64},{64,128},{128,192},{1,65},{65,129},{129,193},{2,66},{66,130... | collective-permute-start | bytes 589832 | tf_op jit(solution)/shard_map/ppermute | solution.py:48
  51.3 17.9 %all-to-all-start.1 = ((bf16[2,128,768]{2,1,0:T(8,128)(2,1)}), bf16[2,128,768]{2,1,0:T(8,128)(2,1)}, u32[]{:S(2)}, u32[]{:S(2)}) async-start(bf16[2,128,768]{2,1,0:T(8,128)(2,1)} %broadcast_in_dim.92), calls=%async_computation.1 | async-start | bytes 786432 | tf_op jit(solution)/shard_map/all_to_all | solution.py:13
  72.1 8.0 %collective-permute-start.1 = (bf16[128,768]{1,0:T(8,128)(2,1)}, bf16[128,768]{1,0:T(8,128)(2,1)}, u32[]{:S(2)}, u32[]{:S(2)}) collective-permute-start(bf16[128,768]{1,0:T(8,128)(2,1)} %get-tuple-element.42), channel_id=1, source_target_pairs={{0,64},{64,128},{128,192},{1,65},{65,129},{129,193},{2,66},{66,130... | collective-permute-start | bytes 589832 | tf_op jit(solution)/shard_map/ppermute | solution.py:48
  86.2 18.1 %all-to-all-start.2 = ((bf16[2,128,768]{2,1,0:T(8,128)(2,1)}), bf16[2,128,768]{2,1,0:T(8,128)(2,1)}, u32[]{:S(2)}, u32[]{:S(2)}) async-start(bf16[2,128,768]{2,1,0:T(8,128)(2,1)} %broadcast_in_dim.94), calls=%async_computation.2 | async-start | bytes 786432 | tf_op jit(solution)/shard_map/all_to_all | solution.py:13
  107.2 6.9 %collective-permute-start.2 = (bf16[128,768]{1,0:T(8,128)(2,1)}, bf16[128,768]{1,0:T(8,128)(2,1)}, u32[]{:S(2)}, u32[]{:S(2)}) collective-permute-start(bf16[128,768]{1,0:T(8,128)(2,1)} %get-tuple-element.40), channel_id=1, source_target_pairs={{0,64},{64,128},{128,192},{1,65},{65,129},{129,193},{2,66},{66,130... | collective-permute-start | bytes 589832 | tf_op jit(solution)/shard_map/ppermute | solution.py:48
  120.2 18.3 %all-to-all-start.3 = ((bf16[2,128,768]{2,1,0:T(8,128)(2,1)}), bf16[2,128,768]{2,1,0:T(8,128)(2,1)}, u32[]{:S(2)}, u32[]{:S(2)}) async-start(bf16[2,128,768]{2,1,0:T(8,128)(2,1)} %broadcast_in_dim.96), calls=%async_computation.3 | async-start | bytes 786432 | tf_op jit(solution)/shard_map/all_to_all | solution.py:13
  124.3 179.1 %reduce-scatter.2.cloned.1.call-start = ((), (), s32[]{:S(2)}) async-start(), calls=%async_computation.6 | async-start | bytes 4866048 | tf_op jit(solution)/shard_map/reduce_scatter | solution.py:37
  141.3 17.2 %collective-permute-start.3 = (bf16[128,768]{1,0:T(8,128)(2,1)}, bf16[128,768]{1,0:T(8,128)(2,1)}, u32[]{:S(2)}, u32[]{:S(2)}) collective-permute-start(bf16[128,768]{1,0:T(8,128)(2,1)} %get-tuple-element.38), channel_id=1, source_target_pairs={{0,64},{64,128},{128,192},{1,65},{65,129},{129,193},{2,66},{66,130... | collective-permute-start | bytes 589832 | tf_op jit(solution)/shard_map/ppermute | solution.py:48
  166.7 84.6 %all-to-all-start.4 = ((bf16[2,128,768]{2,1,0:T(8,128)(2,1)}), bf16[2,128,768]{2,1,0:T(8,128)(2,1)}, u32[]{:S(2)}, u32[]{:S(2)}) async-start(bf16[2,128,768]{2,1,0:T(8,128)(2,1)} %broadcast_in_dim.99), calls=%async_computation.4 | async-start | bytes 786432 | tf_op jit(solution)/shard_map/all_to_all | solution.py:13
  176.6 15.9 %copy-start.17 = (f32[128]{0:T(128)S(1)}, f32[128]{0:T(128)}, u32[]{:S(2)}) copy-start(f32[128]{0:T(128)} %copy-done.16) | copy-start | bytes 1540
  176.6 16.2 %copy-start.3 = (bf16[2,128,768]{2,1,0:T(8,128)(2,1)S(1)}, bf16[2,128,768]{2,1,0:T(8,128)(2,1)}, u32[]{:S(2)}) copy-start(bf16[2,128,768]{2,1,0:T(8,128)(2,1)} %param.10) | copy-start | bytes 1179652
  193.7 8.8 %collective-permute-start.4 = (bf16[128,768]{1,0:T(8,128)(2,1)S(1)}, bf16[128,768]{1,0:T(8,128)(2,1)}, u32[]{:S(2)}, u32[]{:S(2)}) collective-permute-start(bf16[128,768]{1,0:T(8,128)(2,1)S(1)} %fusion.253), channel_id=1, source_target_pairs={{64,0},{128,64},{192,128},{65,1},{129,65},{193,129},{66,2},{130,66... | collective-permute-start | bytes 589832 | tf_op jit(solution)/shard_map/ppermute | solution.py:48
  199.9 18.1 %copy-start.15 = (f32[128]{0:T(128)S(1)}, f32[128]{0:T(128)}, u32[]{:S(2)}) copy-start(f32[128]{0:T(128)} %broadcast_multiply_fusion.11) | copy-start | bytes 1540
  220.3 11.5 %collective-permute-start.5 = (bf16[128,768]{1,0:T(8,128)(2,1)S(1)}, bf16[128,768]{1,0:T(8,128)(2,1)}, u32[]{:S(2)}, u32[]{:S(2)}) collective-permute-start(bf16[128,768]{1,0:T(8,128)(2,1)S(1)} %get-tuple-element.28), channel_id=1, source_target_pairs={{64,0},{128,64},{192,128},{65,1},{129,65},{193,129},{66,2},{130,66... | collective-permute-start | bytes 589832 | tf_op jit(solution)/shard_map/ppermute | solution.py:48
  223.7 23.9 %copy-start.23 = (f32[128]{0:T(128)S(1)}, f32[128]{0:T(128)}, u32[]{:S(2)}) copy-start(f32[128]{0:T(128)} %copy-done.22) | copy-start | bytes 1540
  250.0 10.1 %collective-permute-start.6 = (bf16[128,768]{1,0:T(8,128)(2,1)}, bf16[128,768]{1,0:T(8,128)(2,1)}, u32[]{:S(2)}, u32[]{:S(2)}) collective-permute-start(bf16[128,768]{1,0:T(8,128)(2,1)} %get-tuple-element.26), channel_id=1, source_target_pairs={{64,0},{128,64},{192,128},{65,1},{129,65},{193,129},{66,2},{130,66... | collective-permute-start | bytes 589832 | tf_op jit(solution)/shard_map/ppermute | solution.py:48
  253.8 23.1 %copy-start.21 = (f32[128]{0:T(128)S(1)}, f32[128]{0:T(128)}, u32[]{:S(2)}) copy-start(f32[128]{0:T(128)} %copy-done.20) | copy-start | bytes 1540
  264.4 15.4 %copy-start.12 = (bf16[1,2,128,768]{3,2,1,0:T(8,128)(2,1)S(1)}, bf16[1,2,128,768]{3,2,1,0:T(8,128)(2,1)}, u32[]{:S(2)}) copy-start(bf16[1,2,128,768]{3,2,1,0:T(8,128)(2,1)} %copy.22) | copy-start | bytes 1179652
  278.6 7.7 %collective-permute-start.7 = (bf16[128,768]{1,0:T(8,128)(2,1)S(1)}, bf16[128,768]{1,0:T(8,128)(2,1)}, u32[]{:S(2)}, u32[]{:S(2)}) collective-permute-start(bf16[128,768]{1,0:T(8,128)(2,1)S(1)} %get-tuple-element.24), channel_id=1, source_target_pairs={{64,0},{128,64},{192,128},{65,1},{129,65},{193,129},{66,2},{130,66... | collective-permute-start | bytes 589832 | tf_op jit(solution)/shard_map/ppermute | solution.py:48
  281.5 19.9 %copy-start.19 = (f32[128]{0:T(128)S(1)}, f32[128]{0:T(128)}, u32[]{:S(2)}) copy-start(f32[128]{0:T(128)} %broadcast_multiply_fusion.2) | copy-start | bytes 1540
  281.5 19.9 %copy-start.26 = (f32[128]{0:T(128)S(1)}, f32[128]{0:T(128)}, u32[]{:S(2)}) copy-start(f32[128]{0:T(128)} %add_rsqrt_fusion) | copy-start | bytes 1540
  281.5 20.1 %copy-start.4 = (bf16[2,128,768]{2,1,0:T(8,128)(2,1)S(1)}, bf16[2,128,768]{2,1,0:T(8,128)(2,1)}, u32[]{:S(2)}) copy-start(bf16[2,128,768]{2,1,0:T(8,128)(2,1)} %param.10) | copy-start | bytes 1179652
  (17 other events, 102.0 us)
Sparse Core Ops, SparseCore 0:
  157.8 88.6 reduce-scatter.1
where the time goes:
time: 320 us; the launch traced here: 315 us
  waiting for transfers between devices  75.3 us (24%)
  blocking collectives  59.6 us (19%)
  starting transfers between devices  48.8 us (15%)
  matrix products  45.7 us (14%)
  other arithmetic  38.5 us (12%)
  local copies, waits for them, and re-layouts  31.9 us (10%)
  between operations  14.8 us (5%)
    all_gather x5, blocking collectives, total_of_pieces(): blocks = lax.all_gather(value, axis).astype(jnp.float32)  59.6 us
    all_to_all x5, waiting for transfers between devices, from_everyone(): return lax.all_to_all(copies, axis, split_axis=0, concat_axis=0, tiled=True)  44.8 us
    ppermute x8, waiting for transfers between devices, shifted(): lax.ppermute(value, axis, [(source, source + steps) for source in range(i...  30.5 us
    all_to_all x5, starting transfers between devices, from_everyone(): return lax.all_to_all(copies, axis, split_axis=0, concat_axis=0, tiled=True)  25.1 us
    ppermute x8, starting transfers between devices, shifted(): lax.ppermute(value, axis, [(source, source + steps) for source in range(i...  23.6 us
    dot_general x5, matrix products, layer_backward(): lax.dot_general(grad_up, w_up, (((1,), (1,)), ((), ())), preferred_elemen...  21.9 us
    dot_general x5, matrix products, layer_forward(): partial_value = jnp.dot(active, w_down, preferred_element_type=jnp.float32)  16.6 us
    dynamic_update_slice x14, other arithmetic, store_row(): return lax.dynamic_update_index_in_dim(buffer, chosen, slot_index, 0)  13.8 us
  transfers between devices with their start and end apart: 14, of which 11 were waited for; matrix products, arithmetic and copies ran while one was open for 24% of the time, Pallas kernels for 0%

commit v1 on v0

v1 whole, which is shorter than its diff:
```python
import jax
import jax.numpy as jnp
from jax import lax
from jax.sharding import PartitionSpec as P

eps_norm = 1e-05
gelu_coef = 0.7978845608028654
learning_rate = 0.05
bf16 = jnp.bfloat16
f32 = jnp.float32
side = 4
cores = 2


def hand_over(value, source, target, sections):
    axes = ("section", "tensor")
    halves = lax.axis_size("tensor")
    straight = lax.ppermute(
        value, axes, [(source * halves + t, target * halves + t) for t in range(halves)]
    )
    crossed = lax.ppermute(
        value, axes, [(source * halves + t, target * halves + 1 - t) for t in range(halves)]
    )
    return (straight.astype(f32) + crossed.astype(f32)).astype(bf16)


def with_other_half(value):
    other = lax.ppermute(value, "tensor", [(0, 1), (1, 0)])
    return (value.astype(f32) + other.astype(f32)).astype(bf16)


def apply_norm(rows, gain):
    values = rows.astype(f32)
    center = jnp.mean(values, axis=-1, keepdims=True)
    centered = values - center
    spread = jnp.mean(centered * centered, axis=-1, keepdims=True)
    inverse_scale = lax.rsqrt(spread + eps_norm)
    return centered * inverse_scale, inverse_scale


def forward_part(rows, gain, w_up, w_down):
    standardized, _ = apply_norm(rows, gain)
    upper = jnp.dot((standardized * gain).astype(bf16), w_up, preferred_element_type=f32)
    inner = jnp.tanh(gelu_coef * (upper + 0.044715 * upper * upper * upper))
    active = (0.5 * upper * (1.0 + inner)).astype(bf16)
    part = jnp.dot(active, w_down, preferred_element_type=f32)
    return (part + 0.5 * rows.astype(f32)).astype(bf16)


def slope_of(rows, gain, w_up):
    standardized, inverse_scale = apply_norm(rows, gain)
    upper = jnp.dot((standardized * gain).astype(bf16), w_up, preferred_element_type=f32)
    inner = jnp.tanh(gelu_coef * (upper + 0.044715 * upper * upper * upper))
    slope = 0.5 * (1.0 + inner) + 0.5 * upper * (1.0 - inner * inner) * gelu_coef * (
        1.0 + 3.0 * 0.044715 * upper * upper
    )
    return slope, standardized, inverse_scale


def backward_part(grad, slope, standardized, inverse_scale, gain, w_up, w_down):
    across = (((1,), (1,)), ((), ()))
    grad_act = lax.dot_general(grad, w_down, across, preferred_element_type=f32)
    grad_up = (grad_act * slope).astype(bf16)
    part = lax.dot_general(grad_up, w_up, across, preferred_element_type=f32) * gain
    leading = jnp.mean(part, axis=-1, keepdims=True)
    trailing = jnp.mean(part * standardized, axis=-1, keepdims=True)
    moved = inverse_scale * (part - leading - standardized * trailing)
    return (moved + 0.5 * grad.astype(f32)).astype(bf16)


def by_position(axis, move):
    pairs = []
    for x in range(side):
        for y in range(side):
            for core in range(cores):
                place = [x, y, core]
                place[axis] = move(place[axis])
                pairs.append(((x * side + y) * cores + core, (place[0] * side + place[1]) * cores + place[2]))
    return pairs


def near(position):
    return position ^ 1


def wrapped(position):
    return side - 1 - position


def block(value, index):
    return lax.dynamic_index_in_dim(value, index, 0, keepdims=False)


def plus(a, b):
    return (a.astype(f32) + b.astype(f32)).astype(bf16)


def line_sum(value, axis, position, first, second):
    there = first(position)
    sent = jnp.stack([block(value, there), block(value, second(there))])
    got = lax.ppermute(sent, "dp", by_position(axis, first))
    kept = plus(block(value, second(position)), got[1])
    mine = plus(block(value, position), got[0])
    return plus(mine, lax.ppermute(kept, "dp", by_position(axis, second)))


def summed_shards(up, down):
    index = lax.axis_index("dp")
    core, y, x = index % cores, (index // cores) % side, index // (cores * side)
    totals = []
    for value, order in ((up, ((0, x), (1, y))), (down, ((1, y), (0, x)))):
        rows = value.shape[0] // (side * side * cores)
        value = value.reshape(side, side, cores, rows, value.shape[1])
        own = lax.dynamic_index_in_dim(value, core, 2, keepdims=False)
        other = lax.dynamic_index_in_dim(value, 1 - core, 2, keepdims=False)
        value = plus(own, lax.ppermute(other, "dp", by_position(2, lambda c: 1 - c)))
        if order[0][0] == 1:
            value = jnp.swapaxes(value, 0, 1)
        parts = []
        half = rows // 2
        for at, moves in ((0, (near, wrapped)), (half, (wrapped, near))):
            part = value[:, :, at : at + half]
            for axis, position in order:
                part = line_sum(part, axis, position, *moves)
            parts.append(part)
        totals.append(jnp.concatenate(parts, axis=0))
    return totals


def local(
    inputs,
    out_grads,
    norm_gain,
    up_weight,
    down_weight,
    prior_up_grad,
    prior_down_grad,
    master_up,
    master_down,
):
    up_total, down_total = summed_shards(prior_up_grad[0, 0], prior_down_grad[0, 0])
    new_up = master_up - learning_rate * up_total.astype(f32)[None]
    new_down = master_down - learning_rate * down_total.astype(f32)[None]

    sections = lax.axis_size("section")
    section = lax.axis_index("section")
    width = inputs.shape[-1]
    gain = norm_gain[0]
    w_up = up_weight[0]
    w_down = down_weight[0]
    rows = inputs.reshape(-1, width)
    for stage in range(sections - 1):
        part = forward_part(rows, gain, w_up, w_down)
        rows = jnp.where(section == stage + 1, hand_over(part, stage, stage + 1, sections), rows)
    produced = with_other_half(forward_part(rows, gain, w_up, w_down))
    slope, standardized, inverse_scale = slope_of(rows, gain, w_up)
    grad = out_grads.reshape(-1, width)
    for stage in range(sections - 1, 0, -1):
        part = backward_part(grad, slope, standardized, inverse_scale, gain, w_up, w_down)
        grad = jnp.where(section == stage - 1, hand_over(part, stage, stage - 1, sections), grad)
    part = backward_part(grad, slope, standardized, inverse_scale, gain, w_up, w_down)
    grads_done = with_other_half(part)
    shape = (1, *inputs.shape)
    return (produced.reshape(shape), grads_done.reshape(shape), new_up, new_down)


def solution(mesh):
    placed = (
        P(None, "dp", None),
        P(None, "dp", None),
        P("section", None),
        P("section", None, "tensor"),
        P("section", "tensor", None),
        P("dp", "section", None, "tensor"),
        P("dp", "section", "tensor", None),
        P("section", "dp", "tensor"),
        P("section", ("tensor", "dp"), None),
    )
    return jax.shard_map(
        local,
        mesh=mesh,
        in_specs=placed,
        out_specs=(
            P("section", None, "dp", None),
            P("section", None, "dp", None),
            P("section", "dp", "tensor"),
            P("section", ("tensor", "dp"), None),
        ),
        check_vma=False,
    )
```

time: 320 us -> 180 us (0.56); the launches traced: 315 us -> 179 us
  blocking collectives: 59.6 us -> 0 us
  local copies, waits for them, and re-layouts: 31.9 us -> 4.11 us
  waiting for transfers between devices: 75.3 us -> 61 us
  between operations: 14.8 us -> 1.3 us
  matrix products: 45.7 us -> 35.4 us
  other arithmetic: 38.5 us -> 33.3 us
  starting transfers between devices: 48.8 us -> 43.6 us
    all_gather x5 -> x0, blocking collectives: 59.6 us -> none  [total_of_pieces(): blocks = lax.all_gather(value, axis).astype(jnp.float32)]
    all_to_all x5 -> x0, waiting for transfers between devices: 44.8 us -> none  [from_everyone(): return lax.all_to_all(copies, axis, split_axis=0, concat_axis=0, tiled=True)]
    ppermute x8 -> x32, waiting for transfers between devices: 30.5 us -> 61 us  [the longest x6 17.3 us: hand_over(): lax.ppermute(value, axes, [(source * halves + t, target * halves + t) for...]
    all_to_all x5 -> x0, starting transfers between devices: 25.1 us -> none  [from_everyone(): return lax.all_to_all(copies, axis, split_axis=0, concat_axis=0, tiled=True)]
    ppermute x8 -> x32, starting transfers between devices: 23.6 us -> 43.6 us  [the longest x8 13.5 us: line_sum(): got = lax.ppermute(sent, 'dp', by_position(axis, first))]
    convert_element_type x2 -> x20, other arithmetic: 0.25 us -> 19.4 us  [the longest x13 9.4 us: plus(): return (a.astype(f32) + b.astype(f32)).astype(bf16)]
    dynamic_update_slice x14 -> x0, other arithmetic: 13.8 us -> none  [store_row(): return lax.dynamic_update_index_in_dim(buffer, chosen, slot_index, 0)]
    dot_general x15 -> x9, matrix products: 45.7 us -> 35.4 us  [the longest x4 19.5 us: backward_part(): lax.dot_general(grad_up, w_up, across, preferred_element_type=f32) * gain]
  transfers between devices with their start and end apart: 14 -> 32, of which waited for: 11 -> 10; matrix products, arithmetic and copies ran while one was open for 24% -> 26% of each run, Pallas kernels for 0% -> 0%
where the time goes in v1:
time: 180 us; the launch traced here: 179 us
  waiting for transfers between devices  61 us (34%)
  starting transfers between devices  43.6 us (24%)
  matrix products  35.4 us (20%)
  other arithmetic  33.3 us (18%)
  local copies, waits for them, and re-layouts  4.11 us (2%)
    dot_general x4, matrix products, backward_part(): lax.dot_general(grad_up, w_up, across, preferred_element_type=f32) * gain  19.5 us
    ppermute x6, waiting for transfers between devices, hand_over(): lax.ppermute(value, axes, [(source * halves + t, target * halves + t) for...  17.3 us
    ppermute x8, waiting for transfers between devices, line_sum(): got = lax.ppermute(sent, 'dp', by_position(axis, first))  17.2 us
    ppermute x2, waiting for transfers between devices, with_other_half(): other = lax.ppermute(value, 'tensor', [(0, 1), (1, 0)])  14.4 us
    dot_general x4, matrix products, forward_part(): part = jnp.dot(active, w_down, preferred_element_type=f32)  13.9 us
    ppermute x8, starting transfers between devices, line_sum(): got = lax.ppermute(sent, 'dp', by_position(axis, first))  13.5 us
    ppermute x6, starting transfers between devices, hand_over(): lax.ppermute(value, axes, [(source * halves + t, target * halves + 1 - t)...  12.3 us
    ppermute x6, waiting for transfers between devices, hand_over(): lax.ppermute(value, axes, [(source * halves + t, target * halves + 1 - t)...  10.6 us
  transfers between devices with their start and end apart: 32, of which 10 were waited for; matrix products, arithmetic and copies ran while one was open for 26% of the time, Pallas kernels for 0%

profile of v1, /device:TPU:6, one launch (start us, length us, event | category | flops | bytes accessed | tf_op | source)
XLA Modules:
  0.0 178.7 jit_solution(13803498007038432148)
XLA Ops:
  5.1 4.0 %fusion.93 = bf16[256,768]{1,0:T(8,128)(2,1)} fusion(bf16[1,1536,768]{2,1,0:T(8,128)(2,1)} %param.13, bf16[256,768]{1,0:T(8,128)(2,1)S(1)} %bitcast.219, bf16[1,768,1536]{2,1,0:T(8,128)(2,1)S(1)} %copy-done, bf16[256,768]{1,0:T(8,128)(2,1)S(1)} %bitcast.213), kind=kOutput, calls=%fused_computation.77 | convolution fusion | flops 1212284928 | bytes 5898240 | tf_op jit(solution)/shard_map/dot_general | solution.py:46
  9.1 3.8 %collective-permute-start = (bf16[256,768]{1,0:T(8,128)(2,1)}, bf16[256,768]{1,0:T(8,128)(2,1)S(1)}, u32[]{:S(2)}, u32[]{:S(2)}) collective-permute-start(bf16[256,768]{1,0:T(8,128)(2,1)} %fusion.93), channel_id=1, source_target_pairs={{0,64},{1,65},{2,66},{3,67},{4,68},{5,69},{6,70},{7,71},{8,72},{9,... | collective-permute-start | bytes 1179656 | tf_op jit(solution)/shard_map/ppermute | solution.py:18
  13.0 6.8 %collective-permute-start.1 = (bf16[256,768]{1,0:T(8,128)(2,1)}, bf16[256,768]{1,0:T(8,128)(2,1)}, u32[]{:S(2)}, u32[]{:S(2)}) collective-permute-start(bf16[256,768]{1,0:T(8,128)(2,1)} %fusion.93), channel_id=1, source_target_pairs={{0,65},{1,64},{2,67},{3,66},{4,69},{5,68},{6,71},{7,70},{8,73},{9,... | collective-permute-start | bytes 1179656 | tf_op jit(solution)/shard_map/ppermute | solution.py:21
  21.6 6.1 %collective-permute-done.1 = bf16[256,768]{1,0:T(8,128)(2,1)} collective-permute-done((bf16[256,768]{1,0:T(8,128)(2,1)}, bf16[256,768]{1,0:T(8,128)(2,1)}, u32[]{:S(2)}, u32[]{:S(2)}) %collective-permute-start.1) | collective-permute-done | bytes 393248 | tf_op jit(solution)/shard_map/ppermute | solution.py:21
  29.3 4.0 %fusion.90 = bf16[256,768]{1,0:T(8,128)(2,1)} fusion(bf16[1,1536,768]{2,1,0:T(8,128)(2,1)} %param.13, bf16[1,768,1536]{2,1,0:T(8,128)(2,1)S(1)} %copy-done, bf16[256,768]{1,0:T(8,128)(2,1)S(1)} %get-tuple-element.17, f32[768]{0:T(1024)S(1)} %reduce.2, f32[256]{0:T(256)S(1)} %add_rsqrt_fusion.2, f32[256]{0:T(256)S(1)} %broadcast_multiply_fusion.10), kind=kOutput, calls=%fused_computation.76 | convolution fusion | flops 1213267968 | bytes 5510144 | tf_op jit(solution)/shard_map/dot_general | solution.py:46
  36.9 4.0 %fusion.87 = bf16[256,768]{1,0:T(8,128)(2,1)} fusion(bf16[1,1536,768]{2,1,0:T(8,128)(2,1)} %param.13, bf16[1,768,1536]{2,1,0:T(8,128)(2,1)S(1)} %copy-done, bf16[256,768]{1,0:T(8,128)(2,1)S(1)} %get-tuple-element.15, f32[256]{0:T(256)S(1)} %add_rsqrt_fusion.1, f32[256]{0:T(256)S(1)} %broadcast_multiply_fusion.9, f32[768]{0:T(1024)S(1)} %reduce.2), kind=kOutput, calls=%fused_computation.75 | convolution fusion | flops 1213267968 | bytes 5510144 | tf_op jit(solution)/shard_map/dot_general | solution.py:46
  43.2 2.4 %dynamic-slice_bitcast_fusion = bf16[4,4,48,768]{3,2,1,0:T(8,128)(2,1)} fusion(bf16[4,4,2,48,768]{4,3,2,1,0:T(8,128)(2,1)} %bitcast.214, s32[]{:T(128)S(6)} %select_n.130), kind=kLoop, calls=%fused_computation.88 | loop fusion | bytes 2359300 | tf_op jit(solution)/shard_map/jit(dynamic_index_in_dim)/squeeze | solution.py:115
  48.7 2.0 %fusion.26 = f32[256,1536]{1,0:T(8,128)} fusion(bf16[1,768,1536]{2,1,0:T(8,128)(2,1)S(1)} %copy-done, bf16[256,768]{1,0:T(8,128)(2,1)S(1)} %get-tuple-element.13, f32[256]{0:T(256)S(1)} %add_rsqrt_fusion, f32[256]{0:T(256)S(1)} %broadcast_multiply_fusion.8, f32[768]{0:T(1024)S(1)} %reduce.2), kind=kOutput, calls=%fused_computation.37 | convolution fusion | flops 604962816 | bytes 4330496 | tf_op jit(solution)/shard_map/dot_general | solution.py:43
  50.7 4.9 %fusion.253 = (f32[256]{0:T(256)S(1)}, f32[256]{0:T(256)S(1)}, f32[256,768]{1,0:T(8,128)}) fusion(f32[256]{0:T(256)S(1)} %add_rsqrt_fusion, f32[256]{0:T(256)S(1)} %broadcast_multiply_fusion.8, bf16[256,768]{1,0:T(8,128)(2,1)S(1)} %get-tuple-element.13, f32[768]{0:T(1024)S(1)} %reduce.2, bf16[1,768,1536]{2,1,0:T(8,128)(2,1)S(1)} %copy-done, ...), kind=kOutput, calls=%fused_computation.294 | convolution fusion | flops 1216806400 | bytes 7871488 | tf_op jit(solution)/shard_map/dot_general | solution.py:64
  58.5 1.9 %fusion.96 = bf16[4,4,48,768]{3,2,0,1:T(8,128)(2,1)S(1)} fusion(bf16[4,4,48,768]{3,2,1,0:T(8,128)(2,1)} %collective-permute-done.23, bf16[4,4,2,48,768]{4,3,2,1,0:T(8,128)(2,1)} %bitcast.215, s32[]{:T(128)S(6)} %select_n.129), kind=kLoop, calls=%fused_computation.87 | loop fusion | flops 2359296 | bytes 3538948 | tf_op jit(solution)/shard_map/transpose | solution.py:118
  62.4 2.4 %collective-permute-start.28 = (bf16[2,4,24,768]{3,2,1,0:T(8,128)(2,1)S(1)}, bf16[2,4,24,768]{3,2,1,0:T(8,128)(2,1)S(1)}, u32[]{:S(2)}, u32[]{:S(2)}) collective-permute-start(bf16[2,4,24,768]{3,2,1,0:T(8,128)(2,1)S(1)} %pad_maximum_fusion.3), channel_id=1, source_target_pairs={{0,12},{2,14},{4,8},{6,10},{8,4},{10,6},{12,0},{14,2},{16,28},{18,... | collective-permute-start | bytes 884744 | tf_op jit(solution)/shard_map/ppermute | solution.py:101
  69.6 9.5 %collective-permute-done.15 = bf16[2,4,12,1536]{3,2,1,0:T(8,128)(2,1)S(1)} collective-permute-done((bf16[2,4,12,1536]{3,2,1,0:T(8,128)(2,1)S(1)}, bf16[2,4,12,1536]{3,2,1,0:T(8,128)(2,1)S(1)}, u32[]{:S(2)}, u32[]{:S(2)}) %collective-permute-start.15) | collective-permute-done | bytes 294944 | tf_op jit(solution)/shard_map/ppermute | solution.py:101
  84.9 5.0 %collective-permute-done.19 = bf16[2,4,12,1536]{3,2,1,0:T(8,128)(2,1)S(1)} collective-permute-done((bf16[2,4,12,1536]{3,2,1,0:T(8,128)(2,1)S(1)}, bf16[2,4,12,1536]{3,2,1,0:T(8,128)(2,1)S(1)}, u32[]{:S(2)}, u32[]{:S(2)}) %collective-permute-start.19) | collective-permute-done | bytes 294944 | tf_op jit(solution)/shard_map/ppermute | solution.py:101
  92.1 4.9 %fusion.252 = (f32[256]{0:T(256)S(1)}, f32[256]{0:T(256)S(1)}, f32[256,768]{1,0:T(8,128)}) fusion(f32[256]{0:T(256)S(1)} %add_rsqrt_fusion, f32[256]{0:T(256)S(1)} %broadcast_multiply_fusion.8, bf16[256,768]{1,0:T(8,128)(2,1)S(1)} %get-tuple-element.13, f32[768]{0:T(1024)S(1)} %reduce.2, bf16[1,768,1536]{2,1,0:T(8,128)(2,1)S(1)} %copy-done, ...), kind=kOutput, calls=%fused_computation.293 | convolution fusion | flops 1216806400 | bytes 7871488 | tf_op jit(solution)/shard_map/dot_general | solution.py:64
  100.1 2.0 %add_convert_fusion.4 = bf16[256,768]{1,0:T(8,128)(2,1)} fusion(bf16[256,768]{1,0:T(8,128)(2,1)} %collective-permute-done.6, bf16[256,768]{1,0:T(8,128)(2,1)} %fusion.84), kind=kLoop, calls=%fused_computation.144 | loop fusion | flops 786432 | bytes 1179648 | tf_op jit(solution)/shard_map/convert_element_type | solution.py:29
  106.5 2.8 %collective-permute-start.30 = (bf16[2,24,768]{2,1,0:T(8,128)(2,1)S(1)}, bf16[2,24,768]{2,1,0:T(8,128)(2,1)S(1)}, u32[]{:S(2)}, u32[]{:S(2)}) collective-permute-start(bf16[2,24,768]{2,1,0:T(8,128)(2,1)S(1)} %pad_maximum_fusion.7), channel_id=1, source_target_pairs={{0,48},{2,50},{4,52},{6,54},{8,56},{10,58},{12,60},{14,62},{16,32}... | collective-permute-start | bytes 221192 | tf_op jit(solution)/shard_map/ppermute | solution.py:101
  113.1 2.3 %collective-permute-start.21 = (bf16[2,12,1536]{2,1,0:T(8,128)(2,1)S(1)}, bf16[2,12,1536]{2,1,0:T(8,128)(2,1)S(1)}, u32[]{:S(2)}, u32[]{:S(2)}) collective-permute-start(bf16[2,12,1536]{2,1,0:T(8,128)(2,1)S(1)} %pad_maximum_fusion.5), channel_id=1, source_target_pairs={{0,12},{2,14},{4,8},{6,10},{8,4},{10,6},{12,0},{14,2},{16,28},{18,... | collective-permute-start | bytes 221192 | tf_op jit(solution)/shard_map/ppermute | solution.py:101
  116.4 2.6 %collective-permute-done.21 = bf16[2,12,1536]{2,1,0:T(8,128)(2,1)S(1)} collective-permute-done((bf16[2,12,1536]{2,1,0:T(8,128)(2,1)S(1)}, bf16[2,12,1536]{2,1,0:T(8,128)(2,1)S(1)}, u32[]{:S(2)}, u32[]{:S(2)}) %collective-permute-start.21) | collective-permute-done | bytes 73760 | tf_op jit(solution)/shard_map/ppermute | solution.py:101
  119.1 2.4 %collective-permute-start.18 = (bf16[12,1536]{1,0:T(8,128)(2,1)S(1)}, bf16[12,1536]{1,0:T(8,128)(2,1)S(1)}, u32[]{:S(2)}, u32[]{:S(2)}) collective-permute-start(bf16[12,1536]{1,0:T(8,128)(2,1)S(1)} %fusion.219), channel_id=1, source_target_pairs={{0,12},{2,14},{4,8},{6,10},{8,4},{10,6},{12,0},{14,2},{16,28},{18,... | collective-permute-start | bytes 110600 | tf_op jit(solution)/shard_map/ppermute | solution.py:104
  125.2 4.9 %fusion.251 = (f32[256]{0:T(256)S(1)}, f32[256]{0:T(256)S(1)}, f32[256,768]{1,0:T(8,128)}) fusion(f32[256]{0:T(256)S(1)} %add_rsqrt_fusion, f32[256]{0:T(256)S(1)} %broadcast_multiply_fusion.8, bf16[256,768]{1,0:T(8,128)(2,1)S(1)} %get-tuple-element.13, f32[768]{0:T(1024)S(1)} %reduce.2, bf16[1,768,1536]{2,1,0:T(8,128)(2,1)S(1)} %copy-done, ...), kind=kOutput, calls=%fused_computation.292 | convolution fusion | flops 1216806400 | bytes 7871488 | tf_op jit(solution)/shard_map/dot_general | solution.py:64
  135.6 15.5 %collective-permute-done.11 = bf16[256,768]{1,0:T(8,128)(2,1)S(1)} collective-permute-done((bf16[256,768]{1,0:T(8,128)(2,1)S(1)}, bf16[256,768]{1,0:T(8,128)(2,1)S(1)}, u32[]{:S(2)}, u32[]{:S(2)}) %collective-permute-start.11) | collective-permute-done | bytes 393248 | tf_op jit(solution)/shard_map/ppermute | solution.py:18
  151.1 4.4 %collective-permute-done.12 = bf16[256,768]{1,0:T(8,128)(2,1)S(1)} collective-permute-done((bf16[256,768]{1,0:T(8,128)(2,1)S(1)}, bf16[256,768]{1,0:T(8,128)(2,1)S(1)}, u32[]{:S(2)}, u32[]{:S(2)}) %collective-permute-start.12) | collective-permute-done | bytes 393248 | tf_op jit(solution)/shard_map/ppermute | solution.py:21
  155.7 4.9 %fusion.250 = (f32[256]{0:T(256)S(1)}, f32[256]{0:T(256)S(1)}, f32[256,768]{1,0:T(8,128)}) fusion(f32[256]{0:T(256)S(1)} %add_rsqrt_fusion, f32[256]{0:T(256)S(1)} %broadcast_multiply_fusion.8, bf16[256,768]{1,0:T(8,128)(2,1)S(1)} %get-tuple-element.13, f32[768]{0:T(1024)S(1)} %reduce.2, bf16[1,768,1536]{2,1,0:T(8,128)(2,1)S(1)} %copy-done, ...), kind=kOutput, calls=%fused_computation.291 | convolution fusion | flops 1216806400 | bytes 7871488 | tf_op jit(solution)/shard_map/dot_general | solution.py:64
  164.3 13.6 %collective-permute-done.13 = bf16[256,768]{1,0:T(8,128)(2,1)S(1)} collective-permute-done((bf16[256,768]{1,0:T(8,128)(2,1)S(1)}, bf16[256,768]{1,0:T(8,128)(2,1)S(1)}, u32[]{:S(2)}, u32[]{:S(2)}) %collective-permute-start.13) | collective-permute-done | bytes 393248 | tf_op jit(solution)/shard_map/ppermute | solution.py:28
  (175 shorter events, 60.1 us)
Async XLA Ops:
  9.1 12.5 %collective-permute-start = (bf16[256,768]{1,0:T(8,128)(2,1)}, bf16[256,768]{1,0:T(8,128)(2,1)S(1)}, u32[]{:S(2)}, u32[]{:S(2)}) collective-permute-start(bf16[256,768]{1,0:T(8,128)(2,1)} %fusion.93), channel_id=1, source_target_pairs={{0,64},{1,65},{2,66},{3,67},{4,68},{5,69},{6,70},{7,71},{8,72},{9,... | collective-permute-start | bytes 1179656 | tf_op jit(solution)/shard_map/ppermute | solution.py:18
  13.0 14.8 %collective-permute-start.1 = (bf16[256,768]{1,0:T(8,128)(2,1)}, bf16[256,768]{1,0:T(8,128)(2,1)}, u32[]{:S(2)}, u32[]{:S(2)}) collective-permute-start(bf16[256,768]{1,0:T(8,128)(2,1)} %fusion.93), channel_id=1, source_target_pairs={{0,65},{1,64},{2,67},{3,66},{4,69},{5,68},{6,71},{7,70},{8,73},{9,... | collective-permute-start | bytes 1179656 | tf_op jit(solution)/shard_map/ppermute | solution.py:21
  45.5 12.9 %collective-permute-start.23 = (bf16[4,4,48,768]{3,2,1,0:T(8,128)(2,1)}, bf16[4,4,48,768]{3,2,1,0:T(8,128)(2,1)}, u32[]{:S(2)}, u32[]{:S(2)}) collective-permute-start(bf16[4,4,48,768]{3,2,1,0:T(8,128)(2,1)} %dynamic-slice_bitcast_fusion), channel_id=1, source_target_pairs={{0,2},{2,0},{4,6},{6,4},{8,10},{10,8},{12,14},{14,12},{16,18},{18,... | collective-permute-start | bytes 3538952 | tf_op jit(solution)/shard_map/ppermute | solution.py:116
  46.7 20.0 %collective-permute-start.14 = (bf16[4,4,24,1536]{3,2,1,0:T(8,128)(2,1)}, bf16[4,4,24,1536]{3,2,1,0:T(8,128)(2,1)}, u32[]{:S(2)}, u32[]{:S(2)}) collective-permute-start(bf16[4,4,24,1536]{3,2,1,0:T(8,128)(2,1)} %dynamic-slice_bitcast_fusion.1), channel_id=1, source_target_pairs={{0,2},{2,0},{4,6},{6,4},{8,10},{10,8},{12,14},{14,12},{16,18},{18,... | collective-permute-start | bytes 3538952 | tf_op jit(solution)/shard_map/ppermute | solution.py:116
  57.1 34.3 %collective-permute-start.7 = (bf16[256,768]{1,0:T(8,128)(2,1)S(1)}, bf16[256,768]{1,0:T(8,128)(2,1)S(1)}, u32[]{:S(2)}, u32[]{:S(2)}) collective-permute-start(bf16[256,768]{1,0:T(8,128)(2,1)S(1)} %fusion.133), channel_id=1, source_target_pairs={{192,128},{193,129},{194,130},{195,131},{196,132},{197,133},{198,1... | collective-permute-start | bytes 1179656 | tf_op jit(solution)/shard_map/ppermute | solution.py:18
  57.8 34.0 %collective-permute-start.8 = (bf16[256,768]{1,0:T(8,128)(2,1)S(1)}, bf16[256,768]{1,0:T(8,128)(2,1)S(1)}, u32[]{:S(2)}, u32[]{:S(2)}) collective-permute-start(bf16[256,768]{1,0:T(8,128)(2,1)S(1)} %fusion.133), channel_id=1, source_target_pairs={{192,129},{193,128},{194,131},{195,130},{196,133},{197,132},{198,1... | collective-permute-start | bytes 1179656 | tf_op jit(solution)/shard_map/ppermute | solution.py:21
  60.6 19.7 %collective-permute-start.24 = (bf16[2,4,24,768]{3,2,1,0:T(8,128)(2,1)S(1)}, bf16[2,4,24,768]{3,2,1,0:T(8,128)(2,1)S(1)}, u32[]{:S(2)}, u32[]{:S(2)}) collective-permute-start(bf16[2,4,24,768]{3,2,1,0:T(8,128)(2,1)S(1)} %pad_maximum_fusion.2), channel_id=1, source_target_pairs={{0,4},{2,6},{4,0},{6,2},{8,12},{10,14},{12,8},{14,10},{16,20},{18,... | collective-permute-start | bytes 884744 | tf_op jit(solution)/shard_map/ppermute | solution.py:101
  62.4 20.2 %collective-permute-start.28 = (bf16[2,4,24,768]{3,2,1,0:T(8,128)(2,1)S(1)}, bf16[2,4,24,768]{3,2,1,0:T(8,128)(2,1)S(1)}, u32[]{:S(2)}, u32[]{:S(2)}) collective-permute-start(bf16[2,4,24,768]{3,2,1,0:T(8,128)(2,1)S(1)} %pad_maximum_fusion.3), channel_id=1, source_target_pairs={{0,12},{2,14},{4,8},{6,10},{8,4},{10,6},{12,0},{14,2},{16,28},{18,... | collective-permute-start | bytes 884744 | tf_op jit(solution)/shard_map/ppermute | solution.py:101
  68.6 10.5 %collective-permute-start.15 = (bf16[2,4,12,1536]{3,2,1,0:T(8,128)(2,1)S(1)}, bf16[2,4,12,1536]{3,2,1,0:T(8,128)(2,1)S(1)}, u32[]{:S(2)}, u32[]{:S(2)}) collective-permute-start(bf16[2,4,12,1536]{3,2,1,0:T(8,128)(2,1)S(1)} %pad_maximum_fusion), channel_id=1, source_target_pairs={{0,16},{2,18},{4,20},{6,22},{8,24},{10,26},{12,28},{14,30},{16,0},... | collective-permute-start | bytes 884744 | tf_op jit(solution)/shard_map/ppermute | solution.py:101
  79.1 10.8 %collective-permute-start.19 = (bf16[2,4,12,1536]{3,2,1,0:T(8,128)(2,1)S(1)}, bf16[2,4,12,1536]{3,2,1,0:T(8,128)(2,1)S(1)}, u32[]{:S(2)}, u32[]{:S(2)}) collective-permute-start(bf16[2,4,12,1536]{3,2,1,0:T(8,128)(2,1)S(1)} %pad_maximum_fusion.1), channel_id=1, source_target_pairs={{0,48},{2,50},{4,52},{6,54},{8,56},{10,58},{12,60},{14,62},{16,32}... | collective-permute-start | bytes 884744 | tf_op jit(solution)/shard_map/ppermute | solution.py:101
  80.3 19.1 %collective-permute-start.6 = (bf16[256,768]{1,0:T(8,128)(2,1)}, bf16[256,768]{1,0:T(8,128)(2,1)}, u32[]{:S(2)}, u32[]{:S(2)}) collective-permute-start(bf16[256,768]{1,0:T(8,128)(2,1)} %fusion.84), channel_id=1, source_target_pairs={{0,1},{1,0},{2,3},{3,2},{4,5},{5,4},{6,7},{7,6},{8,9},{9,8},{10,11... | collective-permute-start | bytes 1179656 | tf_op jit(solution)/shard_map/ppermute | solution.py:28
  82.5 19.5 %collective-permute-start.25 = (bf16[4,24,768]{2,1,0:T(8,128)(2,1)}, bf16[4,24,768]{2,1,0:T(8,128)(2,1)}, u32[]{:S(2)}, u32[]{:S(2)}) collective-permute-start(bf16[4,24,768]{2,1,0:T(8,128)(2,1)} %fusion.211), channel_id=1, source_target_pairs={{0,12},{2,14},{4,8},{6,10},{8,4},{10,6},{12,0},{14,2},{16,28},{18,... | collective-permute-start | bytes 442376 | tf_op jit(solution)/shard_map/ppermute | solution.py:104
  89.9 14.0 %collective-permute-start.29 = (bf16[4,24,768]{2,1,0:T(8,128)(2,1)}, bf16[4,24,768]{2,1,0:T(8,128)(2,1)}, u32[]{:S(2)}, u32[]{:S(2)}) collective-permute-start(bf16[4,24,768]{2,1,0:T(8,128)(2,1)} %fusion.213), channel_id=1, source_target_pairs={{0,4},{2,6},{4,0},{6,2},{8,12},{10,14},{12,8},{14,10},{16,20},{18,... | collective-permute-start | bytes 442376 | tf_op jit(solution)/shard_map/ppermute | solution.py:104
  91.3 15.1 %collective-permute-start.16 = (bf16[4,12,1536]{2,1,0:T(8,128)(2,1)}, bf16[4,12,1536]{2,1,0:T(8,128)(2,1)}, u32[]{:S(2)}, u32[]{:S(2)}) collective-permute-start(bf16[4,12,1536]{2,1,0:T(8,128)(2,1)} %fusion.207), channel_id=1, source_target_pairs={{0,48},{2,50},{4,52},{6,54},{8,56},{10,58},{12,60},{14,62},{16,32}... | collective-permute-start | bytes 442376 | tf_op jit(solution)/shard_map/ppermute | solution.py:104
  91.8 18.7 %collective-permute-start.20 = (bf16[4,12,1536]{2,1,0:T(8,128)(2,1)}, bf16[4,12,1536]{2,1,0:T(8,128)(2,1)}, u32[]{:S(2)}, u32[]{:S(2)}) collective-permute-start(bf16[4,12,1536]{2,1,0:T(8,128)(2,1)} %fusion.209), channel_id=1, source_target_pairs={{0,16},{2,18},{4,20},{6,22},{8,24},{10,26},{12,28},{14,30},{16,0},... | collective-permute-start | bytes 442376 | tf_op jit(solution)/shard_map/ppermute | solution.py:104
  99.4 25.6 %collective-permute-start.10 = (bf16[256,768]{1,0:T(8,128)(2,1)S(1)}, bf16[256,768]{1,0:T(8,128)(2,1)S(1)}, u32[]{:S(2)}, u32[]{:S(2)}) collective-permute-start(bf16[256,768]{1,0:T(8,128)(2,1)S(1)} %fusion.138), channel_id=1, source_target_pairs={{128,65},{129,64},{130,67},{131,66},{132,69},{133,68},{134,71},{13... | collective-permute-start | bytes 1179656 | tf_op jit(solution)/shard_map/ppermute | solution.py:21
  102.0 23.0 %collective-permute-start.9 = (bf16[256,768]{1,0:T(8,128)(2,1)S(1)}, bf16[256,768]{1,0:T(8,128)(2,1)S(1)}, u32[]{:S(2)}, u32[]{:S(2)}) collective-permute-start(bf16[256,768]{1,0:T(8,128)(2,1)S(1)} %fusion.138), channel_id=1, source_target_pairs={{128,64},{129,65},{130,66},{131,67},{132,68},{133,69},{134,70},{13... | collective-permute-start | bytes 1179656 | tf_op jit(solution)/shard_map/ppermute | solution.py:18
  104.0 9.1 %collective-permute-start.26 = (bf16[2,24,768]{2,1,0:T(8,128)(2,1)S(1)}, bf16[2,24,768]{2,1,0:T(8,128)(2,1)S(1)}, u32[]{:S(2)}, u32[]{:S(2)}) collective-permute-start(bf16[2,24,768]{2,1,0:T(8,128)(2,1)S(1)} %pad_maximum_fusion.6), channel_id=1, source_target_pairs={{0,16},{2,18},{4,20},{6,22},{8,24},{10,26},{12,28},{14,30},{16,0},... | collective-permute-start | bytes 221192 | tf_op jit(solution)/shard_map/ppermute | solution.py:101
  106.5 9.0 %collective-permute-start.30 = (bf16[2,24,768]{2,1,0:T(8,128)(2,1)S(1)}, bf16[2,24,768]{2,1,0:T(8,128)(2,1)S(1)}, u32[]{:S(2)}, u32[]{:S(2)}) collective-permute-start(bf16[2,24,768]{2,1,0:T(8,128)(2,1)S(1)} %pad_maximum_fusion.7), channel_id=1, source_target_pairs={{0,48},{2,50},{4,52},{6,54},{8,56},{10,58},{12,60},{14,62},{16,32}... | collective-permute-start | bytes 221192 | tf_op jit(solution)/shard_map/ppermute | solution.py:101
  115.5 6.6 %collective-permute-start.27 = (bf16[24,768]{1,0:T(8,128)(2,1)S(1)}, bf16[24,768]{1,0:T(8,128)(2,1)S(1)}, u32[]{:S(2)}, u32[]{:S(2)}) collective-permute-start(bf16[24,768]{1,0:T(8,128)(2,1)S(1)} %fusion.225), channel_id=1, source_target_pairs={{0,48},{2,50},{4,52},{6,54},{8,56},{10,58},{12,60},{14,62},{16,32}... | collective-permute-start | bytes 110600 | tf_op jit(solution)/shard_map/ppermute | solution.py:104
  122.1 12.1 %collective-permute-start.22 = (bf16[12,1536]{1,0:T(8,128)(2,1)}, bf16[12,1536]{1,0:T(8,128)(2,1)}, u32[]{:S(2)}, u32[]{:S(2)}) collective-permute-start(bf16[12,1536]{1,0:T(8,128)(2,1)} %fusion.221), channel_id=1, source_target_pairs={{0,4},{2,6},{4,0},{6,2},{8,12},{10,14},{12,8},{14,10},{16,20},{18,... | collective-permute-start | bytes 110600 | tf_op jit(solution)/shard_map/ppermute | solution.py:104
  131.5 19.6 %collective-permute-start.11 = (bf16[256,768]{1,0:T(8,128)(2,1)S(1)}, bf16[256,768]{1,0:T(8,128)(2,1)S(1)}, u32[]{:S(2)}, u32[]{:S(2)}) collective-permute-start(bf16[256,768]{1,0:T(8,128)(2,1)S(1)} %fusion.143), channel_id=1, source_target_pairs={{64,0},{65,1},{66,2},{67,3},{68,4},{69,5},{70,6},{71,7},{72,8},{73... | collective-permute-start | bytes 1179656 | tf_op jit(solution)/shard_map/ppermute | solution.py:18
  132.8 22.7 %collective-permute-start.12 = (bf16[256,768]{1,0:T(8,128)(2,1)S(1)}, bf16[256,768]{1,0:T(8,128)(2,1)S(1)}, u32[]{:S(2)}, u32[]{:S(2)}) collective-permute-start(bf16[256,768]{1,0:T(8,128)(2,1)S(1)} %fusion.143), channel_id=1, source_target_pairs={{64,1},{65,0},{66,3},{67,2},{68,5},{69,4},{70,7},{71,6},{72,9},{73... | collective-permute-start | bytes 1179656 | tf_op jit(solution)/shard_map/ppermute | solution.py:21
  162.1 15.7 %collective-permute-start.13 = (bf16[256,768]{1,0:T(8,128)(2,1)S(1)}, bf16[256,768]{1,0:T(8,128)(2,1)S(1)}, u32[]{:S(2)}, u32[]{:S(2)}) collective-permute-start(bf16[256,768]{1,0:T(8,128)(2,1)S(1)} %fusion.148), channel_id=1, source_target_pairs={{0,1},{1,0},{2,3},{3,2},{4,5},{5,4},{6,7},{7,6},{8,9},{9,8},{10,11... | collective-permute-start | bytes 1179656 | tf_op jit(solution)/shard_map/ppermute | solution.py:28
  (34 other events, 259.1 us)

commit v2 on v1

v2 whole, which is shorter than its diff:
```python
from functools import partial

import jax
import jax.numpy as jnp
from jax import lax
from jax.experimental import pallas as pl
from jax.experimental.pallas import tpu as pltpu
from jax.sharding import PartitionSpec as P


eps_norm = 1e-05
gelu_coef = 0.7978845608028654
learning_rate = 0.05
bf16 = jnp.bfloat16
f32 = jnp.float32
side = 4
cores = 2


def hand_over(value, source, target):
    axes = ("section", "tensor")
    halves = lax.axis_size("tensor")
    straight = lax.ppermute(
        value, axes, [(source * halves + t, target * halves + t) for t in range(halves)]
    )
    crossed = lax.ppermute(
        value, axes, [(source * halves + t, target * halves + 1 - t) for t in range(halves)]
    )
    return straight, crossed


def handed(value, moves):
    halves = lax.axis_size("tensor")
    return lax.ppermute(
        value, ("section", "tensor"), [(a * halves + t, b * halves + u) for (a, t), (b, u) in moves]
    )


chunk = 512


def apply_norm(values):
    center = jnp.mean(values, axis=-1, keepdims=True)
    centered = values - center
    spread = jnp.mean(centered * centered, axis=-1, keepdims=True)
    inverse_scale = lax.rsqrt(spread + eps_norm)
    return centered * inverse_scale, inverse_scale


def plus(a, b):
    return (a.astype(f32) + b.astype(f32)).astype(bf16)


def chosen(stage, straight, crossed, kept):
    return jnp.where(lax.axis_index("section") == stage, plus(straight[...], crossed[...]), kept[...])


def up_of(normed, w_up, at):
    return jnp.dot(normed, w_up[:, at : at + chunk], preferred_element_type=f32)


def curve(upper):
    square = upper * upper
    return jnp.tanh(gelu_coef * (upper + 0.044715 * square * upper)), square


def down_part(rows, act, w_down):
    part = jnp.dot(act[...], w_down[...], preferred_element_type=f32)
    return (part + 0.5 * rows.astype(f32)).astype(bf16)


def forward_body(stage, straight, crossed, kept, gain, w_up, w_down, rows_out, part_out, act):
    rows = chosen(stage, straight, crossed, kept)
    rows_out[...] = rows
    standardized, _ = apply_norm(rows.astype(f32))
    normed = (standardized * gain[...]).astype(bf16)
    for at in range(0, act.shape[1], chunk):
        upper = up_of(normed, w_up, at)
        inner, _ = curve(upper)
        act[:, at : at + chunk] = (0.5 * upper * (1.0 + inner)).astype(bf16)
    part_out[...] = down_part(rows, act, w_down)


def first_body(kept, gain, w_up, w_down, part_out, up_here, down_here, act, came):
    hidden = act.shape[1]
    loads = []
    for i, at in enumerate(range(0, hidden, chunk)):
        here = pl.ds(at, chunk)
        loads.append(pltpu.make_async_copy(w_up.at[:, here], up_here.at[:, here], came.at[i]))
    loads.append(pltpu.make_async_copy(w_down, down_here, came.at[len(loads)]))
    for load in loads:
        load.start()
    rows = kept[...]
    standardized, _ = apply_norm(rows.astype(f32))
    normed = (standardized * gain[...]).astype(bf16)
    for i, at in enumerate(range(0, hidden, chunk)):
        loads[i].wait()
        upper = up_of(normed, up_here, at)
        inner, _ = curve(upper)
        act[:, at : at + chunk] = (0.5 * upper * (1.0 + inner)).astype(bf16)
    loads[-1].wait()
    part_out[...] = down_part(rows, act, down_here)


def grad_part(grad, pushed, standardized, inverse_scale, gain, w_up):
    part = lax.dot_general(pushed[...], w_up[...], across, preferred_element_type=f32) * gain
    leading = jnp.mean(part, axis=-1, keepdims=True)
    trailing = jnp.mean(part * standardized, axis=-1, keepdims=True)
    moved = inverse_scale * (part - leading - standardized * trailing)
    return (moved + 0.5 * grad.astype(f32)).astype(bf16)


across = (((1,), (1,)), ((), ()))


def turn_body(stage, straight, crossed, kept, grad_in, gain, w_up, w_down, rows_out, act, slope, part_out, pushed):
    rows = chosen(stage, straight, crossed, kept)
    rows_out[...] = rows
    standardized, inverse_scale = apply_norm(rows.astype(f32))
    normed = (standardized * gain[...]).astype(bf16)
    grad = grad_in[...]
    for at in range(0, act.shape[1], chunk):
        here = slice(at, at + chunk)
        upper = up_of(normed, w_up, at)
        inner, square = curve(upper)
        act[:, here] = (0.5 * upper * (1.0 + inner)).astype(bf16)
        rise = 0.5 * (1.0 + inner) + 0.5 * upper * (1.0 - inner * inner) * gelu_coef * (
            1.0 + 3.0 * 0.044715 * square
        )
        slope[:, here] = rise
        grad_act = lax.dot_general(grad, w_down[here, :], across, preferred_element_type=f32)
        pushed[:, here] = (grad_act * rise).astype(bf16)
    part_out[...] = grad_part(grad, pushed, standardized, inverse_scale, gain[...], w_up)


def mix_body(last, rows, act, w_down, part_out):
    part = down_part(rows[...], act, w_down)
    part_out[...] = jnp.where(lax.axis_index("section") == last, part, rows[...])


def produced_body(last, mixed, back, swapped, out):
    section = lax.axis_index("section")
    other = jnp.where(section == last - 1, swapped[...], back[...])
    out[...] = jnp.where(section == last, plus(mixed[...], back[...]), other)


def grads_body(part, other, swapped, *rest):
    *backs, out = rest
    section = lax.axis_index("section")
    value = swapped[...]
    for at, back in enumerate(backs):
        value = jnp.where(section == at + 1, back[...], value)
    out[...] = jnp.where(section == 0, plus(part[...], other[...]), value)


def backward_body(stage, last, straight, crossed, kept, rows, slope, gain, w_up, w_down, grad_out, part_out, *more):
    *swap_out, pushed = more
    grad = chosen(stage, straight, crossed, kept)
    grad_out[...] = grad
    if swap_out:
        swap_out[0][...] = jnp.where(lax.axis_index("section") == last, rows[...], grad)
    for at in range(0, pushed.shape[1], chunk):
        here = slice(at, at + chunk)
        grad_act = lax.dot_general(grad, w_down[here, :], across, preferred_element_type=f32)
        pushed[:, here] = (grad_act * slope[:, here]).astype(bf16)
    standardized, inverse_scale = apply_norm(rows[...].astype(f32))
    part_out[...] = grad_part(grad, pushed, standardized, inverse_scale, gain[...], w_up)


def held(*arrays):
    return [(array, "held") for array in arrays]


def kernel(body, outs, operands, scratch=(), plain=False):
    spaces = {"held": pltpu.VMEM, "copied": pltpu.VMEM, "far": pltpu.HBM}
    in_vmem = pl.BlockSpec(memory_space=pltpu.VMEM)
    return pl.pallas_call(
        body,
        out_shape=[(jax.ShapeDtypeStruct if plain else pltpu.VMEM)(shape, dtype) for shape, dtype in outs],
        in_specs=[pl.BlockSpec(memory_space=spaces[where]) for _, where in operands],
        out_specs=[in_vmem] * len(outs),
        scratch_shapes=list(scratch),
        compiler_params=pltpu.CompilerParams(vmem_limit_bytes=16 * 2**20),
    )(
        *(
            pltpu.with_memory_space_constraint(array, spaces[where]) if where in ("held", "far") else array
            for array, where in operands
        )
    )


def by_position(axis, move):
    pairs = []
    for x in range(side):
        for y in range(side):
            for core in range(cores):
                place = [x, y, core]
                place[axis] = move(place[axis])
                pairs.append(((x * side + y) * cores + core, (place[0] * side + place[1]) * cores + place[2]))
    return pairs


def near(position):
    return position ^ 1


def wrapped(position):
    return side - 1 - position


def after(values, event):
    return lax.optimization_barrier((values, event))[0]


def my_core():
    return lax.rem(lax.axis_index("dp"), cores)


def my_places(axis):
    chip = lax.div(lax.axis_index("dp"), cores)
    own = lax.rem(chip, side) if axis else lax.div(chip, side)
    beside = near(own)
    return own, wrapped(own), beside, wrapped(beside)


def split_body(up, down, own, other, came):
    mine = my_core()
    rows, columns = up.shape[3], own.shape[-1]
    copies = []
    for to, core in ((own, mine), (other, cores - 1 - mine)):
        for part in range(up.shape[4] // columns):
            source = up.at[:, :, core, :, pl.ds(part * columns, columns)]
            copies.append((source, to.at[0, :, :, pl.ds(part * rows, rows), :]))
        copies.append((down.at[:, :, core], to.at[1]))
    copies = [pltpu.make_async_copy(a, b, came.at[i]) for i, (a, b) in enumerate(copies)]
    for copy in copies:
        copy.start()
    for copy in copies:
        copy.wait()


def halved_body(own, got, up_kept, up_sent, down_kept, down_sent):
    places = my_places(0), my_places(1)
    for line in range(side):
        for at, (kept, sent) in enumerate(((up_kept, up_sent), (down_kept, down_sent))):
            for slot in range(4):
                place = places[at][slot]
                block = (at, place, line) if at == 0 else (at, line, place)
                to = kept if slot < 2 else sent
                to[slot % 2, line] = plus(own[block], got[block])


def paired_body(up_kept, up_got, down_kept, down_got, up_mine, up_sent, down_mine, down_sent):
    for kept, got, mine, sent in ((up_kept, up_got, up_mine, up_sent), (down_kept, down_got, down_mine, down_sent)):
        mine[...] = plus(kept[0], got[0])
        sent[...] = plus(kept[1], got[1])


def crossing_body(up_mine, up_got, down_mine, down_got, up_kept, up_sent, down_kept, down_sent):
    places = my_places(1), my_places(0)
    for at, (mine, got, kept, sent) in enumerate(
        ((up_mine, up_got, up_kept, up_sent), (down_mine, down_got, down_kept, down_sent))
    ):
        for slot in range(4):
            place = places[at][slot]
            to = kept if slot < 2 else sent
            to[slot % 2] = plus(mine[place], got[place])


def settled_body(up_mine, up_got, down_mine, down_got, master_up, master_down, new_up, new_down):
    rows, columns = master_up.shape[0], up_mine.shape[1]
    for part in range(master_up.shape[1] // columns):
        here, there = slice(part * rows, (part + 1) * rows), slice(part * columns, (part + 1) * columns)
        total = up_mine[here, :].astype(f32) + up_got[here, :].astype(f32)
        new_up[:, there] = master_up[:, there] - learning_rate * total
    total = down_mine[...].astype(f32) + down_got[...].astype(f32)
    new_down[...] = master_down[...] - learning_rate * total


def local(
    inputs,
    out_grads,
    norm_gain,
    up_weight,
    down_weight,
    prior_up_grad,
    prior_down_grad,
    master_up,
    master_down,
):
    turn = 0

    def move(part, source, target):
        fresh = hand_over(part, source, target)
        return summing(part, fresh)

    columns = down_weight.shape[2]
    shape = (down_weight.shape[1] // (side * side * cores), columns)
    whole, pair, line, two = (2, side, side, *shape), (2, side, *shape), (side, *shape), (2, *shape)
    axes = ((0, 1), (1, 0))
    state, gots = None, None

    def summing(event, arrivals):
        nonlocal turn, state, gots
        if turn == 0:
            up = prior_up_grad.reshape(side, side, cores, -1, prior_up_grad.shape[-1])
            down = prior_down_grad.reshape(side, side, cores, *shape)
            loads = pltpu.SemaphoreType.DMA((2 * (up.shape[-1] // columns + 1),))
            up, down = after((up, down), event)
            own, other = kernel(split_body, [(whole, bf16)] * 2, [(up, "far"), (down, "far")], [loads])
            gate = other
            state = [own]
            gots = [lax.ppermute(other, "dp", by_position(2, lambda c: 1 - c))]
        else:
            read = [array for both in zip(state, gots) for array in both]
            read = held(*after(read, event))
            if turn == 1:
                made = kernel(halved_body, [(pair, bf16)] * 4, read)
            elif turn == 2:
                made = kernel(paired_body, [(line, bf16)] * 4, read)
            elif turn == 3:
                made = kernel(crossing_body, [(two, bf16)] * 4, read)
            elif turn == 4:
                made = kernel(paired_body, [(shape, bf16)] * 4, read)
            else:
                masters = [(master_up[0], "copied"), (master_down[0], "copied")]
                outs = [(master_up.shape[1:], f32), (master_down.shape[1:], f32)]
                made = kernel(settled_body, outs, [*read, *masters], plain=True)
            gate = made
            if turn < 5:
                state = [made[0], made[2]]
                moved = near if turn % 2 else wrapped
                gots = [
                    lax.ppermute(made[2 * at + 1], "dp", by_position(axes[at][(turn - 1) // 2], moved))
                    for at in range(2)
                ]
            else:
                state = made
        turn += 1
        return after(arrivals, gate)

    sections = lax.axis_size("section")
    last, both = sections - 1, range(lax.axis_size("tensor"))
    width = inputs.shape[-1]
    gain, w_up, w_down = norm_gain, up_weight[0], down_weight[0]
    rows, grad = inputs.reshape(-1, width), out_grads.reshape(-1, width)
    count, hidden = rows.shape[0], w_up.shape[1]
    narrow, wide, broad = ((count, width), bf16), ((count, hidden), bf16), ((count, hidden), f32)
    scratch = [pltpu.VMEM((count, hidden), bf16)]
    loads = pltpu.SemaphoreType.DMA((hidden // chunk + 1,))
    part, up_here, down_here = kernel(
        first_body,
        [narrow, (w_up.shape, bf16), (w_down.shape, bf16)],
        [(rows, "copied"), (gain, "copied"), (w_up, "far"), (w_down, "far")],
        [*scratch, loads],
    )
    weights = [(gain, "copied"), *held(up_here, down_here)]
    kept = (rows, "copied")

    for stage in range(1, last):
        fresh = move(part, stage - 1, stage)
        rows, part = kernel(partial(forward_body, stage), [narrow, narrow], [*held(*fresh), kept, *weights], scratch)
        kept = (rows, "held")
    fresh = move(part, last - 1, last)
    rows, act, slope, part = kernel(
        partial(turn_body, last),
        [narrow, wide, broad, narrow],
        [*held(*fresh), kept, (grad, "copied"), *weights],
        scratch,
    )
    kept = (grad, "copied")
    backs = []
    for stage in range(last - 1, -1, -1):
        fresh = move(part, stage + 1, stage)
        if stage == last - 1:
            (mixed,) = kernel(partial(mix_body, last), [narrow], held(rows, act, down_here))
            back = handed(
                mixed,
                [((last, t), (last, 1 - t)) for t in both]
                + [((s + 1, t), (s, t)) for s in range(last - 1) for t in both],
            )
        grad, part, *swap = kernel(
            partial(backward_body, stage, last),
            [narrow] * (3 if stage == last - 1 else 2),
            [*held(*fresh), kept, *held(rows, slope), *weights],
            scratch,
        )
        kept = (grad, "held")
        if swap:
            swapped = handed(
                swap[0],
                [((last, t), (last - 1, t)) for t in both] + [((last - 1, 1 - t), (last, t)) for t in both],
            )
        else:
            backs.append(handed(grad, [((stage, 1 - t), (stage + 1, t)) for t in both]))
    other = handed(part, [((0, t), (0, 1 - t)) for t in both])
    (produced,) = kernel(partial(produced_body, last), [narrow], held(mixed, back, swapped), plain=True)
    (grads_done,) = kernel(grads_body, [narrow], held(part, other, swapped, *backs[::-1]), plain=True)
    new_up, new_down = state[0][None], state[1][None]
    shape = (1, *inputs.shape)
    return (produced.reshape(shape), grads_done.reshape(shape), new_up, new_down)


def solution(mesh):
    placed = (
        P(None, "dp", None),
        P(None, "dp", None),
        P("section", None),
        P("section", None, "tensor"),
        P("section", "tensor", None),
        P("dp", "section", None, "tensor"),
        P("dp", "section", "tensor", None),
        P("section", "dp", "tensor"),
        P("section", ("tensor", "dp"), None),
    )
    return jax.shard_map(
        local,
        mesh=mesh,
        in_specs=placed,
        out_specs=(
            P("section", None, "dp", None),
            P("section", None, "dp", None),
            P("section", "dp", "tensor"),
            P("section", ("tensor", "dp"), None),
        ),
        check_vma=False,
    )
```

time: 180 us -> 143 us (0.79)
  matrix products: 35.4 us -> 0 us
  other arithmetic: 33.3 us -> 0 us
  Pallas kernels: 0 us -> 22.9 us
  waiting for transfers between devices: 61 us -> 73.8 us
  starting transfers between devices: 43.6 us -> 40.9 us
  local copies, waits for them, and re-layouts: 4.11 us -> 1.7 us
    dot_general x9 -> x0, matrix products: 35.4 us -> none  [the longest x4 19.5 us: backward_part(): lax.dot_general(grad_up, w_up, across, preferred_element_type=f32) * gain]
    pallas_call x0 -> x16, Pallas kernels: none -> 22.9 us  [kernel(): pl.pallas_call(body, out_shape=[(jax.ShapeDtypeStruct if plain else pltpu...]
    convert_element_type x20 -> x0, other arithmetic: 19.4 us -> none  [the longest x13 9.4 us: plus(): return (a.astype(f32) + b.astype(f32)).astype(bf16)]
    ppermute x6, waiting for transfers between devices: 17.3 us -> 30.4 us  [hand_over(): lax.ppermute(value, axes, [(source * halves + t, target * halves + t) for...]
    reduce_sum x8 -> x0, other arithmetic: 6.99 us -> none  [the longest x4 5.02 us: apply_norm(): center = jnp.mean(values, axis=-1, keepdims=True)]
    ppermute x6, waiting for transfers between devices: 10.6 us -> 6.14 us  [hand_over(): lax.ppermute(value, axes, [(source * halves + t, target * halves + 1 - t)...]
    ppermute x20 -> x14, waiting for transfers between devices: 33.1 us -> 37.3 us  [the longest x8 20.5 us: summing(): lax.ppermute(made[2 * at + 1], 'dp', by_position(axes[at][(turn - 1) // 2...]
    squeeze x2 -> x0, local copies, waits for them, and re-layouts: 3.5 us -> none  [summed_shards(): other = lax.dynamic_index_in_dim(value, 1 - core, 2, keepdims=False)]
  transfers between devices with their start and end apart: 32 -> 26, of which waited for: 10 -> 12; matrix products, arithmetic and copies ran while one was open for 26% -> 0% of each run, Pallas kernels for 0% -> 7%
where the time goes in v2:
time: 143 us; the launch traced here: 140 us
  waiting for transfers between devices  73.8 us (52%)
  starting transfers between devices  40.9 us (29%)
  Pallas kernels  22.9 us (16%)
  local copies, waits for them, and re-layouts  1.7 us (1%)
    ppermute x6, waiting for transfers between devices, hand_over(): lax.ppermute(value, axes, [(source * halves + t, target * halves + t) for...  30.4 us
    pallas_call x16, Pallas kernels, kernel(): pl.pallas_call(body, out_shape=[(jax.ShapeDtypeStruct if plain else pltpu...  22.9 us
    ppermute x8, waiting for transfers between devices, summing(): lax.ppermute(made[2 * at + 1], 'dp', by_position(axes[at][(turn - 1) // 2...  20.5 us
    ppermute x5, waiting for transfers between devices, handed(): lax.ppermute(value, ('section', 'tensor'), [(a * halves + t, b * halves +...  16.8 us
    ppermute x8, starting transfers between devices, summing(): lax.ppermute(made[2 * at + 1], 'dp', by_position(axes[at][(turn - 1) // 2...  12.3 us
    ppermute x5, starting transfers between devices, handed(): lax.ppermute(value, ('section', 'tensor'), [(a * halves + t, b * halves +...  10.2 us
    ppermute x6, starting transfers between devices, hand_over(): lax.ppermute(value, axes, [(source * halves + t, target * halves + 1 - t)...  10.2 us
    ppermute x6, starting transfers between devices, hand_over(): lax.ppermute(value, axes, [(source * halves + t, target * halves + t) for...  8.14 us
  transfers between devices with their start and end apart: 26, of which 12 were waited for; matrix products, arithmetic and copies ran while one was open for 0% of the time, Pallas kernels for 7%

profile of v2, /device:TPU:6, one launch (start us, length us, event | category | flops | bytes accessed | tf_op | source)
XLA Modules:
  0.0 140.3 jit_solution(1727696440530758233)
XLA Ops:
  2.3 3.7 %shard_map.120 = (bf16[256,768]{1,0:T(8,128)(2,1)S(1)}, bf16[768,1536]{1,0:T(8,128)(2,1)S(1)}, bf16[1536,768]{1,0:T(8,128)(2,1)S(1)}) custom-call(bf16[256,768]{1,0:T(8,128)(2,1)S(1)} %bitcast.14, f32[1,768]{1,0:T(1,128)S(1)} %copy-done.2, bf16[768,1536]{1,0:T(8,128)(2,1)} %bitcast.20, bf16[1536,768]{1,0:T(8,128)(2,1)} %bitcast.21), custom_call_target="tpu_custom_call" | custom-call | tf_op jit(solution)/shard_map/pallas_call | solution.py:177
  6.0 2.4 %shard_map.121 = (bf16[2,4,4,48,768]{4,3,2,1,0:T(8,128)(2,1)S(1)}, bf16[2,4,4,48,768]{4,3,2,1,0:T(8,128)(2,1)S(1)}) custom-call(bf16[4,4,2,24,1536]{4,3,2,1,0:T(8,128)(2,1)} %bitcast.18, bf16[4,4,2,48,768]{4,3,2,1,0:T(8,128)(2,1)} %bitcast.19), custom_call_target="tpu_custom_call" | custom-call | tf_op jit(solution)/shard_map/pallas_call | solution.py:177
  8.5 3.8 %collective-permute-start = (bf16[256,768]{1,0:T(8,128)(2,1)S(1)}, bf16[256,768]{1,0:T(8,128)(2,1)S(1)}, u32[]{:S(2)}, u32[]{:S(2)}) collective-permute-start(bf16[256,768]{1,0:T(8,128)(2,1)S(1)} %get-tuple-element.74), channel_id=1, source_target_pairs={{0,64},{1,65},{2,66},{3,67},{4,68},{5,69},{6,70},{7,71},{8,72},{9,... | collective-permute-start | bytes 1179656 | tf_op jit(solution)/shard_map/ppermute | solution.py:23
  12.4 6.1 %collective-permute-start.1 = (bf16[256,768]{1,0:T(8,128)(2,1)S(1)}, bf16[256,768]{1,0:T(8,128)(2,1)S(1)}, u32[]{:S(2)}, u32[]{:S(2)}) collective-permute-start(bf16[256,768]{1,0:T(8,128)(2,1)S(1)} %get-tuple-element.74), channel_id=1, source_target_pairs={{0,65},{1,64},{2,67},{3,66},{4,69},{5,68},{6,71},{7,70},{8,73},{9,... | collective-permute-start | bytes 1179656 | tf_op jit(solution)/shard_map/ppermute | solution.py:26
  18.5 2.9 %collective-permute-done.straight = bf16[256,768]{1,0:T(8,128)(2,1)S(1)} collective-permute-done((bf16[256,768]{1,0:T(8,128)(2,1)S(1)}, bf16[256,768]{1,0:T(8,128)(2,1)S(1)}, u32[]{:S(2)}, u32[]{:S(2)}) %collective-permute-start) | collective-permute-done | bytes 393248 | tf_op jit(solution)/shard_map/ppermute | solution.py:23
  21.4 6.1 %collective-permute-done.1.crossed = bf16[256,768]{1,0:T(8,128)(2,1)S(1)} collective-permute-done((bf16[256,768]{1,0:T(8,128)(2,1)S(1)}, bf16[256,768]{1,0:T(8,128)(2,1)S(1)}, u32[]{:S(2)}, u32[]{:S(2)}) %collective-permute-start.1) | collective-permute-done | bytes 393248 | tf_op jit(solution)/shard_map/ppermute | solution.py:26
  27.5 1.9 %shard_map.122 = (bf16[256,768]{1,0:T(8,128)(2,1)S(1)}, bf16[256,768]{1,0:T(8,128)(2,1)S(1)}) custom-call(bf16[256,768]{1,0:T(8,128)(2,1)S(1)} %collective-permute-done.straight, bf16[256,768]{1,0:T(8,128)(2,1)S(1)} %collective-permute-done.1.crossed, bf16[256,768]{1,0:T(8,128)(2,1)S(1)} %bitcast.15, f32[1,768]{1,0:T(1,128)S(1)} %copy-done.2, ...), custom_call_target="tpu_custom_call" | custom-call | tf_op jit(solution)/shard_map/pallas_call | solution.py:177
  32.4 1.6 %collective-permute-start.8 = (bf16[2,4,48,768]{3,2,1,0:T(8,128)(2,1)S(1)}, bf16[2,4,48,768]{3,2,1,0:T(8,128)(2,1)S(1)}, u32[]{:S(2)}, u32[]{:S(2)}) collective-permute-start(bf16[2,4,48,768]{3,2,1,0:T(8,128)(2,1)S(1)} %get-tuple-element.89), channel_id=1, source_target_pairs={{0,4},{2,6},{4,0},{6,2},{8,12},{10,14},{12,8},{14,10},{16,20},{18,... | collective-permute-start | bytes 1769480 | tf_op jit(solution)/shard_map/ppermute | solution.py:334
  34.0 1.9 %shard_map.124 = (bf16[256,768]{1,0:T(8,128)(2,1)S(1)}, bf16[256,768]{1,0:T(8,128)(2,1)S(1)}) custom-call(bf16[256,768]{1,0:T(8,128)(2,1)S(1)} %collective-permute-done.2.straight, bf16[256,768]{1,0:T(8,128)(2,1)S(1)} %collective-permute-done.3.crossed, bf16[256,768]{1,0:T(8,128)(2,1)S(1)} %get-tuple-element.92.kept, f32[1,768]{1,0:T(1,128)S(1)} %copy-done.3, ...), custom_call_target="tpu_custom_call" | custom-call | tf_op jit(solution)/shard_map/pallas_call | solution.py:177
  37.4 9.0 %collective-permute-done.7.up_got = bf16[2,4,48,768]{3,2,1,0:T(8,128)(2,1)S(1)} collective-permute-done((bf16[2,4,48,768]{3,2,1,0:T(8,128)(2,1)S(1)}, bf16[2,4,48,768]{3,2,1,0:T(8,128)(2,1)S(1)}, u32[]{:S(2)}, u32[]{:S(2)}) %collective-permute-start.7) | collective-permute-done | bytes 589856 | tf_op jit(solution)/shard_map/ppermute | solution.py:334
  47.3 2.9 %shard_map.126 = (bf16[256,768]{1,0:T(8,128)(2,1)S(1)}, bf16[256,1536]{1,0:T(8,128)(2,1)S(1)}, f32[256,1536]{1,0:T(8,128)S(1)}, bf16[256,768]{1,0:T(8,128)(2,1)S(1)}) custom-call(bf16[256,768]{1,0:T(8,128)(2,1)S(1)} %collective-permute-done.5.straight, bf16[256,768]{1,0:T(8,128)(2,1)S(1)} %collective-permute-done.6.crossed, ...), custom_call_target="tpu_custom_call" | custom-call | tf_op jit(solution)/shard_map/pallas_call | solution.py:177
  52.8 3.0 %collective-permute-start.13 = (bf16[4,48,768]{2,1,0:T(8,128)(2,1)S(1)}, bf16[4,48,768]{2,1,0:T(8,128)(2,1)S(1)}, u32[]{:S(2)}, u32[]{:S(2)}) collective-permute-start(bf16[4,48,768]{2,1,0:T(8,128)(2,1)S(1)} %get-tuple-element.101), channel_id=1, source_target_pairs={{0,12},{2,14},{4,8},{6,10},{8,4},{10,6},{12,0},{14,2},{16,28},{18,... | collective-permute-start | bytes 884744 | tf_op jit(solution)/shard_map/ppermute | solution.py:334
  55.9 4.5 %collective-permute-done.12.up_got = bf16[4,48,768]{2,1,0:T(8,128)(2,1)S(1)} collective-permute-done((bf16[4,48,768]{2,1,0:T(8,128)(2,1)S(1)}, bf16[4,48,768]{2,1,0:T(8,128)(2,1)S(1)}, u32[]{:S(2)}, u32[]{:S(2)}) %collective-permute-start.12) | collective-permute-done | bytes 294944 | tf_op jit(solution)/shard_map/ppermute | solution.py:334
  61.4 1.9 %shard_map.129 = (bf16[256,768]{1,0:T(8,128)(2,1)S(1)}, bf16[256,768]{1,0:T(8,128)(2,1)S(1)}, bf16[256,768]{1,0:T(8,128)(2,1)S(1)}) custom-call(bf16[256,768]{1,0:T(8,128)(2,1)S(1)} %collective-permute-done.10.straight, bf16[256,768]{1,0:T(8,128)(2,1)S(1)} %collective-permute-done.11.crossed, bf16[256,768]{1,0:T(8,128)(2,1)S(1)} %bitcast.13, ...), custom_call_target="tpu_custom_call" | custom-call | tf_op jit(solution)/shard_map/pallas_call | solution.py:177
  65.7 4.2 %collective-permute-done.17.up_got = bf16[2,48,768]{2,1,0:T(8,128)(2,1)S(1)} collective-permute-done((bf16[2,48,768]{2,1,0:T(8,128)(2,1)S(1)}, bf16[2,48,768]{2,1,0:T(8,128)(2,1)S(1)}, u32[]{:S(2)}, u32[]{:S(2)}) %collective-permute-start.17) | collective-permute-done | bytes 147488 | tf_op jit(solution)/shard_map/ppermute | solution.py:334
  70.6 1.9 %shard_map.132 = (bf16[256,768]{1,0:T(8,128)(2,1)S(1)}, bf16[256,768]{1,0:T(8,128)(2,1)S(1)}) custom-call(bf16[256,768]{1,0:T(8,128)(2,1)S(1)} %collective-permute-done.15.straight, bf16[256,768]{1,0:T(8,128)(2,1)S(1)} %collective-permute-done.16.crossed, bf16[256,768]{1,0:T(8,128)(2,1)S(1)} %get-tuple-element.131.kept, ...), custom_call_target="tpu_custom_call" | custom-call | tf_op jit(solution)/shard_map/pallas_call | solution.py:177
  72.5 1.4 %collective-permute-start.19 = (bf16[256,768]{1,0:T(8,128)(2,1)S(1)}, bf16[256,768]{1,0:T(8,128)(2,1)S(1)}, u32[]{:S(2)}, u32[]{:S(2)}) collective-permute-start(bf16[256,768]{1,0:T(8,128)(2,1)S(1)} %get-tuple-element.132), channel_id=1, source_target_pairs={{64,0},{65,1},{66,2},{67,3},{68,4},{69,5},{70,6},{71,7},{72,8},{73... | collective-permute-start | bytes 1179656 | tf_op jit(solution)/shard_map/ppermute | solution.py:23
  75.2 2.5 %collective-permute-start.21 = (bf16[48,768]{1,0:T(8,128)(2,1)S(1)}, bf16[48,768]{1,0:T(8,128)(2,1)S(1)}, u32[]{:S(2)}, u32[]{:S(2)}) collective-permute-start(bf16[48,768]{1,0:T(8,128)(2,1)S(1)} %get-tuple-element.126), channel_id=1, source_target_pairs={{0,12},{2,14},{4,8},{6,10},{8,4},{10,6},{12,0},{14,2},{16,28},{18,... | collective-permute-start | bytes 221192 | tf_op jit(solution)/shard_map/ppermute | solution.py:334
  77.7 2.1 %collective-permute-start.22 = (bf16[48,768]{1,0:T(8,128)(2,1)S(1)}, bf16[48,768]{1,0:T(8,128)(2,1)S(1)}, u32[]{:S(2)}, u32[]{:S(2)}) collective-permute-start(bf16[48,768]{1,0:T(8,128)(2,1)S(1)} %get-tuple-element.128), channel_id=1, source_target_pairs={{0,48},{2,50},{4,52},{6,54},{8,56},{10,58},{12,60},{14,62},{16,32}... | collective-permute-start | bytes 221192 | tf_op jit(solution)/shard_map/ppermute | solution.py:334
  84.7 27.5 %collective-permute-done.19.straight = bf16[256,768]{1,0:T(8,128)(2,1)S(1)} collective-permute-done((bf16[256,768]{1,0:T(8,128)(2,1)S(1)}, bf16[256,768]{1,0:T(8,128)(2,1)S(1)}, u32[]{:S(2)}, u32[]{:S(2)}) %collective-permute-start.19) | collective-permute-done | bytes 393248 | tf_op jit(solution)/shard_map/ppermute | solution.py:23
  112.2 1.9 %shard_map.134 = (bf16[256,768]{1,0:T(8,128)(2,1)S(1)}, bf16[256,768]{1,0:T(8,128)(2,1)S(1)}) custom-call(bf16[256,768]{1,0:T(8,128)(2,1)S(1)} %collective-permute-done.19.straight, bf16[256,768]{1,0:T(8,128)(2,1)S(1)} %collective-permute-done.20.crossed, bf16[256,768]{1,0:T(8,128)(2,1)S(1)} %get-tuple-element.141.kept, ...), custom_call_target="tpu_custom_call" | custom-call | tf_op jit(solution)/shard_map/pallas_call | solution.py:177
  114.1 6.2 %collective-permute-start.23 = (bf16[256,768]{1,0:T(8,128)(2,1)S(1)}, bf16[256,768]{1,0:T(8,128)(2,1)S(1)}, u32[]{:S(2)}, u32[]{:S(2)}) collective-permute-start(bf16[256,768]{1,0:T(8,128)(2,1)S(1)} %get-tuple-element.142.part), channel_id=1, source_target_pairs={{0,1},{1,0},{2,3},{3,2},{4,5},{5,4},{6,7},{7,6},{8,9},{9,8},{10,11... | collective-permute-start | bytes 1179656 | tf_op jit(solution)/shard_map/ppermute | solution.py:34
  121.7 7.4 %collective-permute-done.9.back = bf16[256,768]{1,0:T(8,128)(2,1)S(1)} collective-permute-done((bf16[256,768]{1,0:T(8,128)(2,1)S(1)}, bf16[256,768]{1,0:T(8,128)(2,1)S(1)}, u32[]{:S(2)}, u32[]{:S(2)}) %collective-permute-start.9) | collective-permute-done | bytes 393248 | tf_op jit(solution)/shard_map/ppermute | solution.py:34
  130.0 9.4 %collective-permute-done.24.rest_0_ = bf16[256,768]{1,0:T(8,128)(2,1)S(1)} collective-permute-done((bf16[256,768]{1,0:T(8,128)(2,1)S(1)}, bf16[256,768]{1,0:T(8,128)(2,1)S(1)}, u32[]{:S(2)}, u32[]{:S(2)}) %collective-permute-start.24) | collective-permute-done | bytes 393248 | tf_op jit(solution)/shard_map/ppermute | solution.py:34
  (56 shorter events, 23.1 us)
Async XLA Ops:
  8.4 22.4 %collective-permute-start.4 = (bf16[2,4,4,48,768]{4,3,2,1,0:T(8,128)(2,1)S(1)}, bf16[2,4,4,48,768]{4,3,2,1,0:T(8,128)(2,1)S(1)}, u32[]{:S(2)}, u32[]{:S(2)}) collective-permute-start(bf16[2,4,4,48,768]{4,3,2,1,0:T(8,128)(2,1)S(1)} %get-tuple-element.77), channel_id=1, source_target_pairs={{0,2},{2,0},{4,6},{6,4},{8,10},{10,8},{12,14},{14,12},{16,18},{18,... | collective-permute-start | bytes 7077896 | tf_op jit(solution)/shard_map/ppermute | solution.py:313
  8.5 12.8 %collective-permute-start = (bf16[256,768]{1,0:T(8,128)(2,1)S(1)}, bf16[256,768]{1,0:T(8,128)(2,1)S(1)}, u32[]{:S(2)}, u32[]{:S(2)}) collective-permute-start(bf16[256,768]{1,0:T(8,128)(2,1)S(1)} %get-tuple-element.74), channel_id=1, source_target_pairs={{0,64},{1,65},{2,66},{3,67},{4,68},{5,69},{6,70},{7,71},{8,72},{9,... | collective-permute-start | bytes 1179656 | tf_op jit(solution)/shard_map/ppermute | solution.py:23
  12.4 15.1 %collective-permute-start.1 = (bf16[256,768]{1,0:T(8,128)(2,1)S(1)}, bf16[256,768]{1,0:T(8,128)(2,1)S(1)}, u32[]{:S(2)}, u32[]{:S(2)}) collective-permute-start(bf16[256,768]{1,0:T(8,128)(2,1)S(1)} %get-tuple-element.74), channel_id=1, source_target_pairs={{0,65},{1,64},{2,67},{3,66},{4,69},{5,68},{6,71},{7,70},{8,73},{9,... | collective-permute-start | bytes 1179656 | tf_op jit(solution)/shard_map/ppermute | solution.py:26
  31.4 14.9 %collective-permute-start.7 = (bf16[2,4,48,768]{3,2,1,0:T(8,128)(2,1)S(1)}, bf16[2,4,48,768]{3,2,1,0:T(8,128)(2,1)S(1)}, u32[]{:S(2)}, u32[]{:S(2)}) collective-permute-start(bf16[2,4,48,768]{3,2,1,0:T(8,128)(2,1)S(1)} %get-tuple-element.87), channel_id=1, source_target_pairs={{0,16},{2,18},{4,20},{6,22},{8,24},{10,26},{12,28},{14,30},{16,0},... | collective-permute-start | bytes 1769480 | tf_op jit(solution)/shard_map/ppermute | solution.py:334
  32.4 14.6 %collective-permute-start.8 = (bf16[2,4,48,768]{3,2,1,0:T(8,128)(2,1)S(1)}, bf16[2,4,48,768]{3,2,1,0:T(8,128)(2,1)S(1)}, u32[]{:S(2)}, u32[]{:S(2)}) collective-permute-start(bf16[2,4,48,768]{3,2,1,0:T(8,128)(2,1)S(1)} %get-tuple-element.89), channel_id=1, source_target_pairs={{0,4},{2,6},{4,0},{6,2},{8,12},{10,14},{12,8},{14,10},{16,20},{18,... | collective-permute-start | bytes 1769480 | tf_op jit(solution)/shard_map/ppermute | solution.py:334
  35.9 11.4 %collective-permute-start.5 = (bf16[256,768]{1,0:T(8,128)(2,1)S(1)}, bf16[256,768]{1,0:T(8,128)(2,1)S(1)}, u32[]{:S(2)}, u32[]{:S(2)}) collective-permute-start(bf16[256,768]{1,0:T(8,128)(2,1)S(1)} %get-tuple-element.93), channel_id=1, source_target_pairs={{128,192},{129,193},{130,194},{131,195},{132,196},{133,197},{134,1... | collective-permute-start | bytes 1179656 | tf_op jit(solution)/shard_map/ppermute | solution.py:23
  36.7 10.6 %collective-permute-start.6 = (bf16[256,768]{1,0:T(8,128)(2,1)S(1)}, bf16[256,768]{1,0:T(8,128)(2,1)S(1)}, u32[]{:S(2)}, u32[]{:S(2)}) collective-permute-start(bf16[256,768]{1,0:T(8,128)(2,1)S(1)} %get-tuple-element.93), channel_id=1, source_target_pairs={{128,193},{129,192},{130,195},{131,194},{132,197},{133,196},{134,1... | collective-permute-start | bytes 1179656 | tf_op jit(solution)/shard_map/ppermute | solution.py:26
  50.2 11.2 %collective-permute-start.10 = (bf16[256,768]{1,0:T(8,128)(2,1)S(1)}, bf16[256,768]{1,0:T(8,128)(2,1)S(1)}, u32[]{:S(2)}, u32[]{:S(2)}) collective-permute-start(bf16[256,768]{1,0:T(8,128)(2,1)S(1)} %get-tuple-element.107), channel_id=1, source_target_pairs={{192,128},{193,129},{194,130},{195,131},{196,132},{197,133},{198,1... | collective-permute-start | bytes 1179656 | tf_op jit(solution)/shard_map/ppermute | solution.py:23
  50.9 10.5 %collective-permute-start.11 = (bf16[256,768]{1,0:T(8,128)(2,1)S(1)}, bf16[256,768]{1,0:T(8,128)(2,1)S(1)}, u32[]{:S(2)}, u32[]{:S(2)}) collective-permute-start(bf16[256,768]{1,0:T(8,128)(2,1)S(1)} %get-tuple-element.107), channel_id=1, source_target_pairs={{192,129},{193,128},{194,131},{195,130},{196,133},{197,132},{198,1... | collective-permute-start | bytes 1179656 | tf_op jit(solution)/shard_map/ppermute | solution.py:26
  51.6 8.7 %collective-permute-start.12 = (bf16[4,48,768]{2,1,0:T(8,128)(2,1)S(1)}, bf16[4,48,768]{2,1,0:T(8,128)(2,1)S(1)}, u32[]{:S(2)}, u32[]{:S(2)}) collective-permute-start(bf16[4,48,768]{2,1,0:T(8,128)(2,1)S(1)} %get-tuple-element.99), channel_id=1, source_target_pairs={{0,48},{2,50},{4,52},{6,54},{8,56},{10,58},{12,60},{14,62},{16,32}... | collective-permute-start | bytes 884744 | tf_op jit(solution)/shard_map/ppermute | solution.py:334
  52.8 8.4 %collective-permute-start.13 = (bf16[4,48,768]{2,1,0:T(8,128)(2,1)S(1)}, bf16[4,48,768]{2,1,0:T(8,128)(2,1)S(1)}, u32[]{:S(2)}, u32[]{:S(2)}) collective-permute-start(bf16[4,48,768]{2,1,0:T(8,128)(2,1)S(1)} %get-tuple-element.101), channel_id=1, source_target_pairs={{0,12},{2,14},{4,8},{6,10},{8,4},{10,6},{12,0},{14,2},{16,28},{18,... | collective-permute-start | bytes 884744 | tf_op jit(solution)/shard_map/ppermute | solution.py:334
  63.3 7.4 %collective-permute-start.15 = (bf16[256,768]{1,0:T(8,128)(2,1)S(1)}, bf16[256,768]{1,0:T(8,128)(2,1)S(1)}, u32[]{:S(2)}, u32[]{:S(2)}) collective-permute-start(bf16[256,768]{1,0:T(8,128)(2,1)S(1)} %get-tuple-element.120), channel_id=1, source_target_pairs={{128,64},{129,65},{130,66},{131,67},{132,68},{133,69},{134,70},{13... | collective-permute-start | bytes 1179656 | tf_op jit(solution)/shard_map/ppermute | solution.py:23
  64.0 6.7 %collective-permute-start.16 = (bf16[256,768]{1,0:T(8,128)(2,1)S(1)}, bf16[256,768]{1,0:T(8,128)(2,1)S(1)}, u32[]{:S(2)}, u32[]{:S(2)}) collective-permute-start(bf16[256,768]{1,0:T(8,128)(2,1)S(1)} %get-tuple-element.120), channel_id=1, source_target_pairs={{128,65},{129,64},{130,67},{131,66},{132,69},{133,68},{134,71},{13... | collective-permute-start | bytes 1179656 | tf_op jit(solution)/shard_map/ppermute | solution.py:26
  64.6 5.2 %collective-permute-start.17 = (bf16[2,48,768]{2,1,0:T(8,128)(2,1)S(1)}, bf16[2,48,768]{2,1,0:T(8,128)(2,1)S(1)}, u32[]{:S(2)}, u32[]{:S(2)}) collective-permute-start(bf16[2,48,768]{2,1,0:T(8,128)(2,1)S(1)} %get-tuple-element.113), channel_id=1, source_target_pairs={{0,4},{2,6},{4,0},{6,2},{8,12},{10,14},{12,8},{14,10},{16,20},{18,... | collective-permute-start | bytes 442376 | tf_op jit(solution)/shard_map/ppermute | solution.py:334
  65.4 5.1 %collective-permute-start.18 = (bf16[2,48,768]{2,1,0:T(8,128)(2,1)S(1)}, bf16[2,48,768]{2,1,0:T(8,128)(2,1)S(1)}, u32[]{:S(2)}, u32[]{:S(2)}) collective-permute-start(bf16[2,48,768]{2,1,0:T(8,128)(2,1)S(1)} %get-tuple-element.115), channel_id=1, source_target_pairs={{0,16},{2,18},{4,20},{6,22},{8,24},{10,26},{12,28},{14,30},{16,0},... | collective-permute-start | bytes 442376 | tf_op jit(solution)/shard_map/ppermute | solution.py:334
  72.5 39.7 %collective-permute-start.19 = (bf16[256,768]{1,0:T(8,128)(2,1)S(1)}, bf16[256,768]{1,0:T(8,128)(2,1)S(1)}, u32[]{:S(2)}, u32[]{:S(2)}) collective-permute-start(bf16[256,768]{1,0:T(8,128)(2,1)S(1)} %get-tuple-element.132), channel_id=1, source_target_pairs={{64,0},{65,1},{66,2},{67,3},{68,4},{69,5},{70,6},{71,7},{72,8},{73... | collective-permute-start | bytes 1179656 | tf_op jit(solution)/shard_map/ppermute | solution.py:23
  73.9 38.3 %collective-permute-start.20 = (bf16[256,768]{1,0:T(8,128)(2,1)S(1)}, bf16[256,768]{1,0:T(8,128)(2,1)S(1)}, u32[]{:S(2)}, u32[]{:S(2)}) collective-permute-start(bf16[256,768]{1,0:T(8,128)(2,1)S(1)} %get-tuple-element.132), channel_id=1, source_target_pairs={{64,1},{65,0},{66,3},{67,2},{68,5},{69,4},{70,7},{71,6},{72,9},{73... | collective-permute-start | bytes 1179656 | tf_op jit(solution)/shard_map/ppermute | solution.py:26
  75.2 6.7 %collective-permute-start.21 = (bf16[48,768]{1,0:T(8,128)(2,1)S(1)}, bf16[48,768]{1,0:T(8,128)(2,1)S(1)}, u32[]{:S(2)}, u32[]{:S(2)}) collective-permute-start(bf16[48,768]{1,0:T(8,128)(2,1)S(1)} %get-tuple-element.126), channel_id=1, source_target_pairs={{0,12},{2,14},{4,8},{6,10},{8,4},{10,6},{12,0},{14,2},{16,28},{18,... | collective-permute-start | bytes 221192 | tf_op jit(solution)/shard_map/ppermute | solution.py:334
  77.7 5.6 %collective-permute-start.22 = (bf16[48,768]{1,0:T(8,128)(2,1)S(1)}, bf16[48,768]{1,0:T(8,128)(2,1)S(1)}, u32[]{:S(2)}, u32[]{:S(2)}) collective-permute-start(bf16[48,768]{1,0:T(8,128)(2,1)S(1)} %get-tuple-element.128), channel_id=1, source_target_pairs={{0,48},{2,50},{4,52},{6,54},{8,56},{10,58},{12,60},{14,62},{16,32}... | collective-permute-start | bytes 221192 | tf_op jit(solution)/shard_map/ppermute | solution.py:334
  80.6 48.5 %collective-permute-start.9 = (bf16[256,768]{1,0:T(8,128)(2,1)S(1)}, bf16[256,768]{1,0:T(8,128)(2,1)S(1)}, u32[]{:S(2)}, u32[]{:S(2)}) collective-permute-start(bf16[256,768]{1,0:T(8,128)(2,1)S(1)} %shard_map.127.mixed), channel_id=1, source_target_pairs={{192,193},{193,192},{64,0},{65,1},{128,64},{129,65},{194,195},{195... | collective-permute-start | bytes 1179656 | tf_op jit(solution)/shard_map/ppermute | solution.py:34
  81.9 47.2 %collective-permute-start.14 = (bf16[256,768]{1,0:T(8,128)(2,1)S(1)}, bf16[256,768]{1,0:T(8,128)(2,1)S(1)}, u32[]{:S(2)}, u32[]{:S(2)}) collective-permute-start(bf16[256,768]{1,0:T(8,128)(2,1)S(1)} %get-tuple-element.119), channel_id=1, source_target_pairs={{192,128},{193,129},{129,192},{128,193},{194,130},{195,131},{131,1... | collective-permute-start | bytes 1179656 | tf_op jit(solution)/shard_map/ppermute | solution.py:34
  83.3 46.7 %collective-permute-start.25 = (bf16[256,768]{1,0:T(8,128)(2,1)S(1)}, bf16[256,768]{1,0:T(8,128)(2,1)S(1)}, u32[]{:S(2)}, u32[]{:S(2)}) collective-permute-start(bf16[256,768]{1,0:T(8,128)(2,1)S(1)} %get-tuple-element.141.kept), channel_id=1, source_target_pairs={{65,128},{64,129},{67,130},{66,131},{69,132},{68,133},{71,134},{70... | collective-permute-start | bytes 1179656 | tf_op jit(solution)/shard_map/ppermute | solution.py:34
  114.1 15.9 %collective-permute-start.23 = (bf16[256,768]{1,0:T(8,128)(2,1)S(1)}, bf16[256,768]{1,0:T(8,128)(2,1)S(1)}, u32[]{:S(2)}, u32[]{:S(2)}) collective-permute-start(bf16[256,768]{1,0:T(8,128)(2,1)S(1)} %get-tuple-element.142.part), channel_id=1, source_target_pairs={{0,1},{1,0},{2,3},{3,2},{4,5},{5,4},{6,7},{7,6},{8,9},{9,8},{10,11... | collective-permute-start | bytes 1179656 | tf_op jit(solution)/shard_map/ppermute | solution.py:34
  120.3 19.0 %collective-permute-start.24 = (bf16[256,768]{1,0:T(8,128)(2,1)S(1)}, bf16[256,768]{1,0:T(8,128)(2,1)S(1)}, u32[]{:S(2)}, u32[]{:S(2)}) collective-permute-start(bf16[256,768]{1,0:T(8,128)(2,1)S(1)} %get-tuple-element.143), channel_id=1, source_target_pairs={{1,64},{0,65},{3,66},{2,67},{5,68},{4,69},{7,70},{6,71},{9,72},{8,... | collective-permute-start | bytes 1179656 | tf_op jit(solution)/shard_map/ppermute | solution.py:34
  (8 other events, 47.6 us)

commit v3 on v1

v3 whole, which is shorter than its diff:
```python
from functools import partial

import jax
import jax.numpy as jnp
from jax import lax
from jax.experimental import pallas as pl
from jax.experimental.pallas import tpu as pltpu
from jax.sharding import PartitionSpec as P


eps_norm = 1e-05
gelu_coef = 0.7978845608028654
learning_rate = 0.05
bf16 = jnp.bfloat16
f32 = jnp.float32
side = 4
cores = 2


def hand_over(value, source, target):
    both = range(lax.axis_size("tensor"))
    crossed = handed(value, [((source, t), (target, 1 - t)) for t in both])
    straight = handed(value, [((source, t), (target, t)) for t in both])
    return straight, crossed


def handed(value, moves):
    halves = lax.axis_size("tensor")
    return lax.ppermute(
        value, ("section", "tensor"), [(a * halves + t, b * halves + u) for (a, t), (b, u) in moves]
    )


chunk = 512


def apply_norm(values):
    center = jnp.mean(values, axis=-1, keepdims=True)
    centered = values - center
    spread = jnp.mean(centered * centered, axis=-1, keepdims=True)
    inverse_scale = lax.rsqrt(spread + eps_norm)
    return centered * inverse_scale, inverse_scale


def plus(a, b):
    return (a.astype(f32) + b.astype(f32)).astype(bf16)


def chosen(stage, straight, crossed, kept):
    return jnp.where(lax.axis_index("section") == stage, plus(straight[...], crossed[...]), kept)


def up_of(normed, w_up, at):
    return jnp.dot(normed, w_up[:, at : at + chunk], preferred_element_type=f32)


def curve(upper):
    square = upper * upper
    return jnp.tanh(gelu_coef * (upper + 0.044715 * square * upper)), square


def rows_of(array, micro):
    return array[micro] if len(array.shape) == 3 else array[...]


def down_part(rows, act, w_down):
    part = jnp.dot(act[...], w_down[...], preferred_element_type=f32)
    return (part + 0.5 * rows.astype(f32)).astype(bf16)


def activate(rows, gain, w_up, act, ready=None):
    standardized, _ = apply_norm(rows.astype(f32))
    normed = (standardized * gain[...]).astype(bf16)
    for i, at in enumerate(range(0, act.shape[1], chunk)):
        if ready:
            ready[i].wait()
        upper = up_of(normed, w_up, at)
        inner, _ = curve(upper)
        act[:, at : at + chunk] = (0.5 * upper * (1.0 + inner)).astype(bf16)


def first_body(inputs, gain, w_up, w_down, part_out, inputs_here, gain_here, up_here, down_here, act, came):
    pairs = [(inputs, inputs_here), (gain, gain_here)]
    for at in range(0, act.shape[1], chunk):
        here = pl.ds(at, chunk)
        pairs.append((w_up.at[:, here], up_here.at[:, here]))
    pairs.append((w_down, down_here))
    loads = [pltpu.make_async_copy(a, b, came.at[i]) for i, (a, b) in enumerate(pairs)]
    for load in loads:
        load.start()
    loads[0].wait()
    loads[1].wait()
    rows = inputs_here[0]
    activate(rows, gain_here, up_here, act, loads[2:-1])
    loads[-1].wait()
    part_out[...] = down_part(rows, act, down_here)


def at_section(stage):
    return pl.when(lax.axis_index("section") == stage)


def opening_body(micro, inputs, gain, w_up, w_down, part_out, act):
    @at_section(0)
    def _():
        rows = inputs[micro]
        activate(rows, gain, w_up, act)
        part_out[...] = down_part(rows, act, w_down)


def forward_body(stage, micro, straight, crossed, kept, gain, w_up, w_down, rows_out, part_out, act):
    rows = chosen(stage, straight, crossed, rows_of(kept, micro))
    rows_out[...] = rows

    @at_section(stage)
    def _():
        activate(rows, gain, w_up, act)
        part_out[...] = down_part(rows, act, w_down)


def grad_part(grad, pushed, standardized, inverse_scale, gain, w_up):
    part = lax.dot_general(pushed[...], w_up[...], across, preferred_element_type=f32) * gain
    leading = jnp.mean(part, axis=-1, keepdims=True)
    trailing = jnp.mean(part * standardized, axis=-1, keepdims=True)
    moved = inverse_scale * (part - leading - standardized * trailing)
    return (moved + 0.5 * grad.astype(f32)).astype(bf16)


across = (((1,), (1,)), ((), ()))


def slope_of(upper, inner, square):
    return 0.5 * (1.0 + inner) + 0.5 * upper * (1.0 - inner * inner) * gelu_coef * (1.0 + 3.0 * 0.044715 * square)


def turn_body(stage, micro, straight, crossed, kept, grad_in, gain, w_up, w_down, rows_out, act, part_out, pushed):
    rows = chosen(stage, straight, crossed, rows_of(kept, micro))
    rows_out[...] = rows

    @at_section(stage)
    def _():
        standardized, inverse_scale = apply_norm(rows.astype(f32))
        normed = (standardized * gain[...]).astype(bf16)
        grad = grad_in[micro]
        for at in range(0, act.shape[1], chunk):
            here = slice(at, at + chunk)
            upper = up_of(normed, w_up, at)
            inner, square = curve(upper)
            act[:, here] = (0.5 * upper * (1.0 + inner)).astype(bf16)
            grad_act = lax.dot_general(grad, w_down[here, :], across, preferred_element_type=f32)
            pushed[:, here] = (grad_act * slope_of(upper, inner, square)).astype(bf16)
        part_out[...] = grad_part(grad, pushed, standardized, inverse_scale, gain[...], w_up)


def slope_body(last, *refs):
    count = (len(refs) - 2) // 2
    gain, w_up = refs[count : count + 2]

    @pl.when(lax.axis_index("section") < last)
    def _():
        for rows, slope in zip(refs[:count], refs[count + 2 :]):
            standardized, _ = apply_norm(rows[...].astype(f32))
            normed = (standardized * gain[...]).astype(bf16)
            for at in range(0, slope.shape[1], chunk):
                upper = up_of(normed, w_up, at)
                inner, square = curve(upper)
                slope[:, at : at + chunk] = slope_of(upper, inner, square)


def backward_body(stage, micro, straight, crossed, kept, rows, slope, gain, w_up, w_down, grad_out, part_out, pushed):
    grad = chosen(stage, straight, crossed, rows_of(kept, micro))
    grad_out[...] = grad

    @at_section(stage)
    def _():
        for at in range(0, pushed.shape[1], chunk):
            here = slice(at, at + chunk)
            grad_act = lax.dot_general(grad, w_down[here, :], across, preferred_element_type=f32)
            pushed[:, here] = (grad_act * slope[:, here]).astype(bf16)
        standardized, inverse_scale = apply_norm(rows[...].astype(f32))
        part_out[...] = grad_part(grad, pushed, standardized, inverse_scale, gain[...], w_up)


def stacked(parts):
    return jnp.concatenate([part[...] for part in parts], axis=0)


def mix_body(last, *refs):
    *pairs, w_down, out = refs
    count = pairs[0].shape[0]

    @at_section(last)
    def _():
        for at in range(len(pairs) // 2):
            out[at * count : (at + 1) * count, :] = down_part(pairs[2 * at][...], pairs[2 * at + 1], w_down)


def pack_body(*refs):
    *parts, out = refs
    out[...] = stacked(parts)


def produced_body(mixed, other, *refs):
    *backs, out = refs
    section = lax.axis_index("section")
    value = plus(mixed[...], other[...])
    for at, back in enumerate(backs):
        value = jnp.where(section == at, back[...], value)
    out[...] = value


def grads_body(micros, early, late, *refs):
    *ends, out = refs
    section = lax.axis_index("section")
    mine = jnp.concatenate([plus(ends[2 * at][...], ends[2 * at + 1][...]) for at in range(micros)], axis=0)
    back = jnp.where(lax.rem(section, 2) == 1, late[...], early[...])
    out[...] = jnp.where(section == 0, mine, back)


def held(*arrays):
    return [(array, "held") for array in arrays]


def kernel(body, outs, operands, scratch=(), plain=False):
    spaces = {"held": pltpu.VMEM, "copied": pltpu.VMEM, "far": pltpu.HBM}
    in_vmem = pl.BlockSpec(memory_space=pltpu.VMEM)
    return pl.pallas_call(
        body,
        out_shape=[(jax.ShapeDtypeStruct if plain else pltpu.VMEM)(shape, dtype) for shape, dtype in outs],
        in_specs=[pl.BlockSpec(memory_space=spaces[where]) for _, where in operands],
        out_specs=[in_vmem] * len(outs),
        scratch_shapes=list(scratch),
        compiler_params=pltpu.CompilerParams(vmem_limit_bytes=16 * 2**20),
    )(
        *(
            pltpu.with_memory_space_constraint(array, spaces[where]) if where in ("held", "far") else array
            for array, where in operands
        )
    )


def by_position(axis, move):
    pairs = []
    for x in range(side):
        for y in range(side):
            for core in range(cores):
                place = [x, y, core]
                place[axis] = move(place[axis])
                pairs.append(((x * side + y) * cores + core, (place[0] * side + place[1]) * cores + place[2]))
    return pairs


def near(position):
    return position ^ 1


def wrapped(position):
    return side - 1 - position


def my_core():
    return lax.rem(lax.axis_index("dp"), cores)


def my_places(axis):
    chip = lax.div(lax.axis_index("dp"), cores)
    own = lax.rem(chip, side) if axis else lax.div(chip, side)
    beside = near(own)
    return own, wrapped(own), beside, wrapped(beside)


def split_body(up, down, own, other, came):
    mine = my_core()
    rows, columns = up.shape[3], own.shape[-1]
    copies = []
    for to, core in ((own, mine), (other, cores - 1 - mine)):
        for part in range(up.shape[4] // columns):
            source = up.at[:, :, core, :, pl.ds(part * columns, columns)]
            copies.append((source, to.at[0, :, :, pl.ds(part * rows, rows), :]))
        copies.append((down.at[:, :, core], to.at[1]))
    copies = [pltpu.make_async_copy(a, b, came.at[i]) for i, (a, b) in enumerate(copies)]
    for copy in copies:
        copy.start()
    for copy in copies:
        copy.wait()


def halved_body(own, got, kept, sent):
    places = my_places(0)
    for slot in range(4):
        to = kept if slot < 2 else sent
        for weight in range(2):
            for line in range(side):
                block = (weight, places[slot], line)
                to[slot % 2, weight, line] = plus(own[block], got[block])


def paired_body(kept, got, mine, sent):
    mine[...] = plus(kept[0], got[0])
    sent[...] = plus(kept[1], got[1])


def crossing_body(mine, got, kept, sent):
    places = my_places(1)
    for slot in range(4):
        to = kept if slot < 2 else sent
        for weight in range(2):
            block = (weight, places[slot])
            to[slot % 2, weight] = plus(mine[block], got[block])


def settled_body(mine, got, master_up, master_down, new_up, new_down):
    rows, columns = master_up.shape[0], mine.shape[2]
    for part in range(master_up.shape[1] // columns):
        here, there = slice(part * rows, (part + 1) * rows), slice(part * columns, (part + 1) * columns)
        total = mine[0, here, :].astype(f32) + got[0, here, :].astype(f32)
        new_up[:, there] = master_up[:, there] - learning_rate * total
    total = mine[1].astype(f32) + got[1].astype(f32)
    new_down[...] = master_down[...] - learning_rate * total


def local(
    inputs,
    out_grads,
    norm_gain,
    up_weight,
    down_weight,
    prior_up_grad,
    prior_down_grad,
    master_up,
    master_down,
):
    columns = down_weight.shape[2]
    shape = (down_weight.shape[1] // (side * side * cores), columns)
    whole, line = (2, side, side, *shape), (2, side, *shape)
    turn, state, gots = 0, None, None

    def sum_turn():
        nonlocal turn, state, gots
        if turn == 0:
            up = prior_up_grad.reshape(side, side, cores, -1, prior_up_grad.shape[-1])
            down = prior_down_grad.reshape(side, side, cores, *shape)
            loads = pltpu.SemaphoreType.DMA((2 * (up.shape[-1] // columns + 1),))
            own, other = kernel(split_body, [(whole, bf16)] * 2, [(up, "far"), (down, "far")], [loads])
            state = own
            gots = lax.ppermute(other, "dp", by_position(2, lambda c: 1 - c))
        elif turn < 5:
            body = (halved_body, paired_body, crossing_body, paired_body)[turn - 1]
            out = ((2, *line), line, (2, 2, *shape), (2, *shape))[turn - 1]
            state, sent = kernel(body, [(out, bf16)] * 2, held(state, gots))
            gots = lax.ppermute(sent, "dp", by_position((turn - 1) // 2, near if turn % 2 else wrapped))
        else:
            masters = [(master_up[0], "copied"), (master_down[0], "copied")]
            outs = [(master_up.shape[1:], f32), (master_down.shape[1:], f32)]
            state = kernel(settled_body, outs, [*held(state, gots), *masters], plain=True)
        turn += 1

    sections = lax.axis_size("section")
    last, both, micros = sections - 1, range(lax.axis_size("tensor")), range(inputs.shape[0])
    count, width = inputs.shape[1:]
    w_up, w_down = up_weight[0], down_weight[0]
    hidden = w_up.shape[1]
    narrow, wide, broad = ((count, width), bf16), ((count, hidden), bf16), ((count, hidden), f32)
    packed = ((len(micros) * count, width), bf16)
    scratch = [pltpu.VMEM((count, hidden), bf16)]
    loads = pltpu.SemaphoreType.DMA((hidden // chunk + 3,))
    parts = [None for _ in micros]
    parts[0], inputs_here, gain_here, up_here, down_here = kernel(
        first_body,
        [narrow, (inputs.shape, bf16), (norm_gain.shape, f32), (w_up.shape, bf16), (w_down.shape, bf16)],
        [(inputs, "far"), (norm_gain, "far"), (w_up, "far"), (w_down, "far")],
        [*scratch, loads],
    )
    weights = held(gain_here, up_here, down_here)
    kept = [held(inputs_here)[0] for _ in micros]
    seeds = (out_grads, "copied")
    acts, slopes = [None for _ in micros], None
    rows, grads = [None for _ in micros], [None for _ in micros]
    stages = [*range(1, sections), *range(last - 1, -1, -1)]
    with_sum = (0, 1, 4, 5)
    backs = {}

    def opened(micro):
        (parts[micro],) = kernel(partial(opening_body, micro), [narrow], [*held(inputs_here), *weights], scratch)

    def stepped(at, micro, fresh):
        stage, down = stages[at], at >= last
        arrays = [*held(*fresh), kept[micro]]
        if at < last - 1:
            rows[micro], parts[micro] = kernel(
                partial(forward_body, stage, micro), [narrow, narrow], [*arrays, *weights], scratch
            )
            kept[micro] = (rows[micro], "held")
        elif not down:
            rows[micro], acts[micro], parts[micro] = kernel(
                partial(turn_body, stage, micro), [narrow, wide, narrow], [*arrays, seeds, *weights], scratch
            )
            kept[micro] = seeds
        else:
            grads[micro], parts[micro] = kernel(
                partial(backward_body, stage, micro),
                [narrow, narrow],
                [*arrays, *held(rows[micro], slopes[micro]), *weights],
                scratch,
            )
            kept[micro] = (grads[micro], "held")

    fresh = [None for _ in micros]
    for layer, stage in enumerate(stages):
        source = 0 if layer == 0 else stages[layer - 1]
        for micro in micros:
            if micro:
                opened(micro) if layer == 0 else stepped(layer - 1, micro, fresh[micro])
            fresh[micro] = hand_over(parts[micro], source, stage)
        if layer in with_sum:
            sum_turn()
        if layer == last:
            (mixed,) = kernel(
                partial(mix_body, last),
                [packed],
                held(*(array for both_of in zip(rows, acts) for array in both_of), down_here),
            )
            other = handed(mixed, [((last, t), (last, 1 - t)) for t in both])
            slopes = kernel(partial(slope_body, last), [broad for _ in micros], held(*rows, gain_here, up_here))
            (packed_rows,) = kernel(pack_body, [packed], held(*rows))
            backs[0] = handed(packed_rows, [((s + 1, t), (s, t)) for s in range(0, last, 2) for t in both])
        elif layer == last + 1:
            backs[1] = handed(packed_rows, [((s + 1, t), (s, t)) for s in range(1, last, 2) for t in both])
        elif layer == len(stages) - 1:
            (sent,) = kernel(pack_body, [packed], held(*grads))
            early = handed(sent, [((s, t), (s + 1, t)) for s in range(1, last, 2) for t in both])
        stepped(layer, 0, fresh[0])
    layer = len(stages)
    others = [None for _ in micros]
    for micro in micros:
        if micro:
            stepped(layer - 1, micro, fresh[micro])
        others[micro] = handed(parts[micro], [((0, t), (0, 1 - t)) for t in both])
    (sent,) = kernel(pack_body, [packed], held(*grads))
    late = handed(sent, [((s, t), (s + 1, t)) for s in range(0, last, 2) for t in both])
    sum_turn()
    sum_turn()
    returned = [backs[s % 2] for s in range(last)]
    (produced,) = kernel(produced_body, [packed], held(mixed, other, *returned), plain=True)
    ends = [array for both_halves in zip(parts, others) for array in both_halves]
    (grads_done,) = kernel(partial(grads_body, len(micros)), [packed], held(early, late, *ends), plain=True)
    new_up, new_down = state[0][None], state[1][None]
    whole_shape = (1, *inputs.shape)
    return (produced.reshape(whole_shape), grads_done.reshape(whole_shape), new_up, new_down)


def solution(mesh):
    placed = (
        P(None, "dp", None),
        P(None, "dp", None),
        P("section", None),
        P("section", None, "tensor"),
        P("section", "tensor", None),
        P("dp", "section", None, "tensor"),
        P("dp", "section", "tensor", None),
        P("section", "dp", "tensor"),
        P("section", ("tensor", "dp"), None),
    )
    return jax.shard_map(
        local,
        mesh=mesh,
        in_specs=placed,
        out_specs=(
            P("section", None, "dp", None),
            P("section", None, "dp", None),
            P("section", "dp", "tensor"),
            P("section", ("tensor", "dp"), None),
        ),
        check_vma=False,
    )
```

time: 180 us -> 133 us (0.74)
  matrix products: 35.4 us -> 0 us
  other arithmetic: 33.3 us -> 0 us
  Pallas kernels: 0 us -> 16.7 us
  starting transfers between devices: 43.6 us -> 49.4 us
  local copies, waits for them, and re-layouts: 4.11 us -> 0.02 us
  waiting for transfers between devices: 61 us -> 64.3 us
    dot_general x9 -> x0, matrix products: 35.4 us -> none  [the longest x4 19.5 us: backward_part(): lax.dot_general(grad_up, w_up, across, preferred_element_type=f32) * gain]
    convert_element_type x20 -> x0, other arithmetic: 19.4 us -> none  [the longest x13 9.4 us: plus(): return (a.astype(f32) + b.astype(f32)).astype(bf16)]
    pallas_call x0 -> x27, Pallas kernels: none -> 16.7 us  [kernel(): pl.pallas_call(body, out_shape=[(jax.ShapeDtypeStruct if plain else pltpu...]
    reduce_sum x8 -> x0, other arithmetic: 6.99 us -> none  [the longest x4 5.02 us: apply_norm(): center = jnp.mean(values, axis=-1, keepdims=True)]
    ppermute x32 -> x36, starting transfers between devices: 43.6 us -> 49.4 us  [the longest x31 42.5 us: handed(): lax.ppermute(value, ('section', 'tensor'), [(a * halves + t, b * halves +...]
    squeeze x2 -> x0, local copies, waits for them, and re-layouts: 3.5 us -> none  [summed_shards(): other = lax.dynamic_index_in_dim(value, 1 - core, 2, keepdims=False)]
    ppermute x32 -> x36, waiting for transfers between devices: 61 us -> 64.3 us  [the longest x31 59.8 us: handed(): lax.ppermute(value, ('section', 'tensor'), [(a * halves + t, b * halves +...]
    concatenate x4 -> x0, other arithmetic: 2.15 us -> none  [summed_shards(): totals.append(jnp.concatenate(parts, axis=0))]
  transfers between devices with their start and end apart: 32 -> 36, of which waited for: 10 -> 8; matrix products, arithmetic and copies ran while one was open for 26% -> 0% of each run, Pallas kernels for 0% -> 10%
where the time goes in v3:
time: 133 us; the launch traced here: 132 us
  waiting for transfers between devices  64.3 us (48%)
  starting transfers between devices  49.4 us (37%)
  Pallas kernels  16.7 us (13%)
    ppermute x31, waiting for transfers between devices, handed(): lax.ppermute(value, ('section', 'tensor'), [(a * halves + t, b * halves +...  59.8 us
    ppermute x31, starting transfers between devices, handed(): lax.ppermute(value, ('section', 'tensor'), [(a * halves + t, b * halves +...  42.5 us
    pallas_call x27, Pallas kernels, kernel(): pl.pallas_call(body, out_shape=[(jax.ShapeDtypeStruct if plain else pltpu...  16.7 us
    ppermute x4, starting transfers between devices, sum_turn(): lax.ppermute(sent, 'dp', by_position((turn - 1) // 2, near if turn % 2 el...  6.84 us
    ppermute x1, waiting for transfers between devices, sum_turn(): gots = lax.ppermute(other, 'dp', by_position(2, lambda c: 1 - c))  4.52 us
  transfers between devices with their start and end apart: 36, of which 8 were waited for; matrix products, arithmetic and copies ran while one was open for 0% of the time, Pallas kernels for 10%

profile of v3, /device:TPU:6, one launch (start us, length us, event | category | flops | bytes accessed | tf_op | source)
XLA Modules:
  0.0 131.7 jit_solution(3026535292559511051)
XLA Ops:
  0.6 2.4 %shard_map.141 = (bf16[2,4,4,48,768]{4,3,2,1,0:T(8,128)(2,1)S(1)}, bf16[2,4,4,48,768]{4,3,2,1,0:T(8,128)(2,1)S(1)}) custom-call(bf16[4,4,2,24,1536]{4,3,2,1,0:T(8,128)(2,1)} %bitcast.12, bf16[4,4,2,48,768]{4,3,2,1,0:T(8,128)(2,1)} %bitcast.13), custom_call_target="tpu_custom_call" | custom-call | tf_op jit(solution)/shard_map/pallas_call | solution.py:227
  3.2 4.5 %collective-permute-done.31.got = bf16[2,4,4,48,768]{4,3,2,1,0:T(8,128)(2,1)S(1)} collective-permute-done((bf16[2,4,4,48,768]{4,3,2,1,0:T(8,128)(2,1)S(1)}, bf16[2,4,4,48,768]{4,3,2,1,0:T(8,128)(2,1)S(1)}, u32[]{:S(2)}, u32[]{:S(2)}) %collective-permute-start.31) | collective-permute-done | bytes 2359328 | tf_op jit(solution)/shard_map/ppermute | solution.py:346
  9.1 3.2 %shard_map.120 = (bf16[128,768]{1,0:T(8,128)(2,1)S(1)}, bf16[2,128,768]{2,1,0:T(8,128)(2,1)S(1)}, f32[1,768]{1,0:T(1,128)S(1)}, bf16[768,1536]{1,0:T(8,128)(2,1)S(1)}, bf16[1536,768]{1,0:T(8,128)(2,1)S(1)}) custom-call(bf16[2,128,768]{2,1,0:T(8,128)(2,1)} %inputs.1, f32[1,768]{1,0:T(1,128)} %gain.1, bf16[768,1536]{1,0:T(8,128)(2,1)} %bitcast.14, ...), custom_call_target="tpu_custom_call" | custom-call | tf_op jit(solution)/shard_map/pallas_call | solution.py:227
  13.5 2.7 %collective-permute-start.6 = (bf16[128,768]{1,0:T(8,128)(2,1)S(1)}, bf16[128,768]{1,0:T(8,128)(2,1)S(1)}, u32[]{:S(2)}, u32[]{:S(2)}) collective-permute-start(bf16[128,768]{1,0:T(8,128)(2,1)S(1)} %shard_map.124), channel_id=1, source_target_pairs={{0,64},{1,65},{2,66},{3,67},{4,68},{5,69},{6,70},{7,71},{8,72},{9,... | collective-permute-start | bytes 589832 | tf_op jit(solution)/shard_map/ppermute | solution.py:29
  16.2 6.1 %collective-permute-start.7 = (bf16[128,768]{1,0:T(8,128)(2,1)S(1)}, bf16[128,768]{1,0:T(8,128)(2,1)S(1)}, u32[]{:S(2)}, u32[]{:S(2)}) collective-permute-start(bf16[128,768]{1,0:T(8,128)(2,1)S(1)} %shard_map.124), channel_id=1, source_target_pairs={{0,65},{1,64},{2,67},{3,66},{4,69},{5,68},{6,71},{7,70},{8,73},{9,... | collective-permute-start | bytes 589832 | tf_op jit(solution)/shard_map/ppermute | solution.py:29
  22.3 1.3 collective-permute-start
  23.6 1.3 collective-permute-start.1
  25.0 2.6 %collective-permute-done.7.crossed = bf16[128,768]{1,0:T(8,128)(2,1)S(1)} collective-permute-done((bf16[128,768]{1,0:T(8,128)(2,1)S(1)}, bf16[128,768]{1,0:T(8,128)(2,1)S(1)}, u32[]{:S(2)}, u32[]{:S(2)}) %collective-permute-start.7) | collective-permute-done | bytes 196640 | tf_op jit(solution)/shard_map/ppermute | solution.py:29
  29.0 1.7 %collective-permute-done.1.crossed = bf16[128,768]{1,0:T(8,128)(2,1)S(1)} collective-permute-done((bf16[128,768]{1,0:T(8,128)(2,1)S(1)}, bf16[128,768]{1,0:T(8,128)(2,1)S(1)}, u32[]{:S(2)}, u32[]{:S(2)}) %collective-permute-start.1) | collective-permute-done | bytes 196640 | tf_op jit(solution)/shard_map/ppermute | solution.py:29
  39.8 1.5 %shard_map.131 = (f32[128,1536]{1,0:T(8,128)S(1)}, f32[128,1536]{1,0:T(8,128)S(1)}) custom-call(bf16[128,768]{1,0:T(8,128)(2,1)S(1)} %get-tuple-element.58.refs_0_.rows, bf16[128,768]{1,0:T(8,128)(2,1)S(1)} %get-tuple-element.64.refs_2_.refs_1_.rows, f32[1,768]{1,0:T(1,128)S(1)} %get-tuple-element.51.gain.refs_2_, ...), custom_call_target="tpu_custom_call" | custom-call | tf_op jit(solution)/shard_map/pallas_call | solution.py:227
  44.3 1.3 collective-permute-start.26
  45.6 1.3 collective-permute-start.27
  49.6 37.0 %collective-permute-done.26.straight = bf16[128,768]{1,0:T(8,128)(2,1)S(1)} collective-permute-done((bf16[128,768]{1,0:T(8,128)(2,1)S(1)}, bf16[128,768]{1,0:T(8,128)(2,1)S(1)}, u32[]{:S(2)}, u32[]{:S(2)}) %collective-permute-start.26) | collective-permute-done | bytes 196640 | tf_op jit(solution)/shard_map/ppermute | solution.py:29
  87.4 5.1 %collective-permute-done.27.crossed = bf16[128,768]{1,0:T(8,128)(2,1)S(1)} collective-permute-done((bf16[128,768]{1,0:T(8,128)(2,1)S(1)}, bf16[128,768]{1,0:T(8,128)(2,1)S(1)}, u32[]{:S(2)}, u32[]{:S(2)}) %collective-permute-start.27) | collective-permute-done | bytes 196640 | tf_op jit(solution)/shard_map/ppermute | solution.py:29
  94.7 8.2 %collective-permute-done.24.straight = bf16[128,768]{1,0:T(8,128)(2,1)S(1)} collective-permute-done((bf16[128,768]{1,0:T(8,128)(2,1)S(1)}, bf16[128,768]{1,0:T(8,128)(2,1)S(1)}, u32[]{:S(2)}, u32[]{:S(2)}) %collective-permute-start.24) | collective-permute-done | bytes 196640 | tf_op jit(solution)/shard_map/ppermute | solution.py:29
  102.9 1.6 %collective-permute-start.34 = (bf16[2,2,48,768]{3,2,1,0:T(8,128)(2,1)S(1)}, bf16[2,2,48,768]{3,2,1,0:T(8,128)(2,1)S(1)}, u32[]{:S(2)}, u32[]{:S(2)}) collective-permute-start(bf16[2,2,48,768]{3,2,1,0:T(8,128)(2,1)S(1)} %get-tuple-element.89), channel_id=1, source_target_pairs={{0,4},{2,6},{4,0},{6,2},{8,12},{10,14},{12,8},{14,10},{16,20},{18,... | collective-permute-start | bytes 884744 | tf_op jit(solution)/shard_map/ppermute | solution.py:351
  104.5 2.1 %shard_map.138 = (bf16[128,768]{1,0:T(8,128)(2,1)S(1)}, bf16[128,768]{1,0:T(8,128)(2,1)S(1)}) custom-call(bf16[128,768]{1,0:T(8,128)(2,1)S(1)} %collective-permute-done.26.straight, bf16[128,768]{1,0:T(8,128)(2,1)S(1)} %collective-permute-done.27.crossed, bf16[128,768]{1,0:T(8,128)(2,1)S(1)} %get-tuple-element.75.refs_1_.kept, ...), custom_call_target="tpu_custom_call" | custom-call | tf_op jit(solution)/shard_map/pallas_call | solution.py:227
  107.3 1.9 %shard_map.137 = (bf16[128,768]{1,0:T(8,128)(2,1)S(1)}, bf16[128,768]{1,0:T(8,128)(2,1)S(1)}) custom-call(bf16[128,768]{1,0:T(8,128)(2,1)S(1)} %collective-permute-done.24.straight, bf16[128,768]{1,0:T(8,128)(2,1)S(1)} %collective-permute-done.25.crossed, bf16[128,768]{1,0:T(8,128)(2,1)S(1)} %get-tuple-element.70.refs_0_.kept, ...), custom_call_target="tpu_custom_call" | custom-call | tf_op jit(solution)/shard_map/pallas_call | solution.py:227
  109.2 1.9 %collective-permute-start.28 = (bf16[256,768]{1,0:T(8,128)(2,1)S(1)}, bf16[256,768]{1,0:T(8,128)(2,1)S(1)}, u32[]{:S(2)}, u32[]{:S(2)}) collective-permute-start(bf16[256,768]{1,0:T(8,128)(2,1)S(1)} %shard_map.139), channel_id=1, source_target_pairs={{0,64},{1,65},{128,192},{129,193},{2,66},{3,67},{130,194},{131,195... | collective-permute-start | bytes 1179656 | tf_op jit(solution)/shard_map/ppermute | solution.py:29
  111.2 7.4 %collective-permute-start.30 = (bf16[128,768]{1,0:T(8,128)(2,1)S(1)}, bf16[128,768]{1,0:T(8,128)(2,1)S(1)}, u32[]{:S(2)}, u32[]{:S(2)}) collective-permute-start(bf16[128,768]{1,0:T(8,128)(2,1)S(1)} %get-tuple-element.81.refs_2_), channel_id=1, source_target_pairs={{0,1},{1,0},{2,3},{3,2},{4,5},{5,4},{6,7},{7,6},{8,9},{9,8},{10,11... | collective-permute-start | bytes 589832 | tf_op jit(solution)/shard_map/ppermute | solution.py:29
  118.6 2.4 %collective-permute-start.29 = (bf16[128,768]{1,0:T(8,128)(2,1)S(1)}, bf16[128,768]{1,0:T(8,128)(2,1)S(1)}, u32[]{:S(2)}, u32[]{:S(2)}) collective-permute-start(bf16[128,768]{1,0:T(8,128)(2,1)S(1)} %get-tuple-element.80.refs_0_), channel_id=1, source_target_pairs={{0,1},{1,0},{2,3},{3,2},{4,5},{5,4},{6,7},{7,6},{8,9},{9,8},{10,11... | collective-permute-start | bytes 589832 | tf_op jit(solution)/shard_map/ppermute | solution.py:29
  121.1 3.1 %collective-permute-start.35 = (bf16[2,48,768]{2,1,0:T(8,128)(2,1)S(1)}, bf16[2,48,768]{2,1,0:T(8,128)(2,1)S(1)}, u32[]{:S(2)}, u32[]{:S(2)}) collective-permute-start(bf16[2,48,768]{2,1,0:T(8,128)(2,1)S(1)} %get-tuple-element.91), channel_id=1, source_target_pairs={{0,12},{2,14},{4,8},{6,10},{8,4},{10,6},{12,0},{14,2},{16,28},{18,... | collective-permute-start | bytes 442376 | tf_op jit(solution)/shard_map/ppermute | solution.py:351
  125.1 1.5 %collective-permute-done.30.refs_3_ = bf16[128,768]{1,0:T(8,128)(2,1)S(1)} collective-permute-done((bf16[128,768]{1,0:T(8,128)(2,1)S(1)}, bf16[128,768]{1,0:T(8,128)(2,1)S(1)}, u32[]{:S(2)}, u32[]{:S(2)}) %collective-permute-start.30) | collective-permute-done | bytes 196640 | tf_op jit(solution)/shard_map/ppermute | solution.py:29
  126.6 3.5 %collective-permute-done.29.refs_1_ = bf16[128,768]{1,0:T(8,128)(2,1)S(1)} collective-permute-done((bf16[128,768]{1,0:T(8,128)(2,1)S(1)}, bf16[128,768]{1,0:T(8,128)(2,1)S(1)}, u32[]{:S(2)}, u32[]{:S(2)}) %collective-permute-start.29) | collective-permute-done | bytes 196640 | tf_op jit(solution)/shard_map/ppermute | solution.py:29
  (81 shorter events, 24.8 us)
Async XLA Ops:
  8.2 30.1 %collective-permute-start.32 = (bf16[2,2,4,48,768]{4,3,2,1,0:T(8,128)(2,1)S(1)}, bf16[2,2,4,48,768]{4,3,2,1,0:T(8,128)(2,1)S(1)}, u32[]{:S(2)}, u32[]{:S(2)}) collective-permute-start(bf16[2,2,4,48,768]{4,3,2,1,0:T(8,128)(2,1)S(1)} %get-tuple-element.85), channel_id=1, source_target_pairs={{0,16},{2,18},{4,20},{6,22},{8,24},{10,26},{12,28},{14,30},{16,0},... | collective-permute-start | bytes 3538952 | tf_op jit(solution)/shard_map/ppermute | solution.py:351
  13.5 11.5 %collective-permute-start.6 = (bf16[128,768]{1,0:T(8,128)(2,1)S(1)}, bf16[128,768]{1,0:T(8,128)(2,1)S(1)}, u32[]{:S(2)}, u32[]{:S(2)}) collective-permute-start(bf16[128,768]{1,0:T(8,128)(2,1)S(1)} %shard_map.124), channel_id=1, source_target_pairs={{0,64},{1,65},{2,66},{3,67},{4,68},{5,69},{6,70},{7,71},{8,72},{9,... | collective-permute-start | bytes 589832 | tf_op jit(solution)/shard_map/ppermute | solution.py:29
  16.2 11.4 %collective-permute-start.7 = (bf16[128,768]{1,0:T(8,128)(2,1)S(1)}, bf16[128,768]{1,0:T(8,128)(2,1)S(1)}, u32[]{:S(2)}, u32[]{:S(2)}) collective-permute-start(bf16[128,768]{1,0:T(8,128)(2,1)S(1)} %shard_map.124), channel_id=1, source_target_pairs={{0,65},{1,64},{2,67},{3,66},{4,69},{5,68},{6,71},{7,70},{8,73},{9,... | collective-permute-start | bytes 589832 | tf_op jit(solution)/shard_map/ppermute | solution.py:29
  22.3 6.7 %collective-permute-start = (bf16[128,768]{1,0:T(8,128)(2,1)S(1)}, bf16[128,768]{1,0:T(8,128)(2,1)S(1)}, u32[]{:S(2)}, u32[]{:S(2)}) collective-permute-start(bf16[128,768]{1,0:T(8,128)(2,1)S(1)} %get-tuple-element.49), channel_id=1, source_target_pairs={{0,64},{1,65},{2,66},{3,67},{4,68},{5,69},{6,70},{7,71},{8,72},{9,... | collective-permute-start | bytes 589832 | tf_op jit(solution)/shard_map/ppermute | solution.py:29
  23.6 7.1 %collective-permute-start.1 = (bf16[128,768]{1,0:T(8,128)(2,1)S(1)}, bf16[128,768]{1,0:T(8,128)(2,1)S(1)}, u32[]{:S(2)}, u32[]{:S(2)}) collective-permute-start(bf16[128,768]{1,0:T(8,128)(2,1)S(1)} %get-tuple-element.49), channel_id=1, source_target_pairs={{0,65},{1,64},{2,67},{3,66},{4,69},{5,68},{6,71},{7,70},{8,73},{9,... | collective-permute-start | bytes 589832 | tf_op jit(solution)/shard_map/ppermute | solution.py:29
  35.3 6.0 %collective-permute-start.19 = (bf16[128,768]{1,0:T(8,128)(2,1)S(1)}, bf16[128,768]{1,0:T(8,128)(2,1)S(1)}, u32[]{:S(2)}, u32[]{:S(2)}) collective-permute-start(bf16[128,768]{1,0:T(8,128)(2,1)S(1)} %get-tuple-element.71), channel_id=1, source_target_pairs={{192,128},{193,129},{194,130},{195,131},{196,132},{197,133},{198,1... | collective-permute-start | bytes 589832 | tf_op jit(solution)/shard_map/ppermute | solution.py:29
  36.0 5.4 %collective-permute-start.20 = (bf16[128,768]{1,0:T(8,128)(2,1)S(1)}, bf16[128,768]{1,0:T(8,128)(2,1)S(1)}, u32[]{:S(2)}, u32[]{:S(2)}) collective-permute-start(bf16[128,768]{1,0:T(8,128)(2,1)S(1)} %get-tuple-element.71), channel_id=1, source_target_pairs={{192,129},{193,128},{194,131},{195,130},{196,133},{197,132},{198,1... | collective-permute-start | bytes 589832 | tf_op jit(solution)/shard_map/ppermute | solution.py:29
  36.9 5.8 %collective-permute-start.15 = (bf16[128,768]{1,0:T(8,128)(2,1)S(1)}, bf16[128,768]{1,0:T(8,128)(2,1)S(1)}, u32[]{:S(2)}, u32[]{:S(2)}) collective-permute-start(bf16[128,768]{1,0:T(8,128)(2,1)S(1)} %get-tuple-element.66), channel_id=1, source_target_pairs={{192,128},{193,129},{194,130},{195,131},{196,132},{197,133},{198,1... | collective-permute-start | bytes 589832 | tf_op jit(solution)/shard_map/ppermute | solution.py:29
  37.6 5.2 %collective-permute-start.16 = (bf16[128,768]{1,0:T(8,128)(2,1)S(1)}, bf16[128,768]{1,0:T(8,128)(2,1)S(1)}, u32[]{:S(2)}, u32[]{:S(2)}) collective-permute-start(bf16[128,768]{1,0:T(8,128)(2,1)S(1)} %get-tuple-element.66), channel_id=1, source_target_pairs={{192,129},{193,128},{194,131},{195,130},{196,133},{197,132},{198,1... | collective-permute-start | bytes 589832 | tf_op jit(solution)/shard_map/ppermute | solution.py:29
  38.6 55.3 %collective-permute-start.33 = (bf16[2,4,48,768]{3,2,1,0:T(8,128)(2,1)S(1)}, bf16[2,4,48,768]{3,2,1,0:T(8,128)(2,1)S(1)}, u32[]{:S(2)}, u32[]{:S(2)}) collective-permute-start(bf16[2,4,48,768]{3,2,1,0:T(8,128)(2,1)S(1)} %get-tuple-element.87), channel_id=1, source_target_pairs={{0,48},{2,50},{4,52},{6,54},{8,56},{10,58},{12,60},{14,62},{16,32}... | collective-permute-start | bytes 1769480 | tf_op jit(solution)/shard_map/ppermute | solution.py:351
  43.5 4.7 %collective-permute-start.18 = (bf16[128,768]{1,0:T(8,128)(2,1)S(1)}, bf16[128,768]{1,0:T(8,128)(2,1)S(1)}, u32[]{:S(2)}, u32[]{:S(2)}) collective-permute-start(bf16[128,768]{1,0:T(8,128)(2,1)S(1)} %get-tuple-element.68), channel_id=1, source_target_pairs={{128,65},{129,64},{130,67},{131,66},{132,69},{133,68},{134,71},{13... | collective-permute-start | bytes 589832 | tf_op jit(solution)/shard_map/ppermute | solution.py:29
  44.3 42.4 %collective-permute-start.26 = (bf16[128,768]{1,0:T(8,128)(2,1)S(1)}, bf16[128,768]{1,0:T(8,128)(2,1)S(1)}, u32[]{:S(2)}, u32[]{:S(2)}) collective-permute-start(bf16[128,768]{1,0:T(8,128)(2,1)S(1)} %get-tuple-element.78), channel_id=1, source_target_pairs={{64,0},{65,1},{66,2},{67,3},{68,4},{69,5},{70,6},{71,7},{72,8},{73... | collective-permute-start | bytes 589832 | tf_op jit(solution)/shard_map/ppermute | solution.py:29
  45.6 46.9 %collective-permute-start.27 = (bf16[128,768]{1,0:T(8,128)(2,1)S(1)}, bf16[128,768]{1,0:T(8,128)(2,1)S(1)}, u32[]{:S(2)}, u32[]{:S(2)}) collective-permute-start(bf16[128,768]{1,0:T(8,128)(2,1)S(1)} %get-tuple-element.78), channel_id=1, source_target_pairs={{64,1},{65,0},{66,3},{67,2},{68,5},{69,4},{70,7},{71,6},{72,9},{73... | collective-permute-start | bytes 589832 | tf_op jit(solution)/shard_map/ppermute | solution.py:29
  47.0 62.3 %collective-permute-start.13 = (bf16[256,768]{1,0:T(8,128)(2,1)S(1)}, bf16[256,768]{1,0:T(8,128)(2,1)S(1)}, u32[]{:S(2)}, u32[]{:S(2)}) collective-permute-start(bf16[256,768]{1,0:T(8,128)(2,1)S(1)} %shard_map.129), channel_id=1, source_target_pairs={{64,0},{65,1},{192,128},{193,129},{66,2},{67,3},{194,130},{195,131... | collective-permute-start | bytes 1179656 | tf_op jit(solution)/shard_map/ppermute | solution.py:29
  48.3 54.6 %collective-permute-start.24 = (bf16[128,768]{1,0:T(8,128)(2,1)S(1)}, bf16[128,768]{1,0:T(8,128)(2,1)S(1)}, u32[]{:S(2)}, u32[]{:S(2)}) collective-permute-start(bf16[128,768]{1,0:T(8,128)(2,1)S(1)} %get-tuple-element.76), channel_id=1, source_target_pairs={{64,0},{65,1},{66,2},{67,3},{68,4},{69,5},{70,6},{71,7},{72,8},{73... | collective-permute-start | bytes 589832 | tf_op jit(solution)/shard_map/ppermute | solution.py:29
  86.7 24.5 %collective-permute-start.14 = (bf16[256,768]{1,0:T(8,128)(2,1)S(1)}, bf16[256,768]{1,0:T(8,128)(2,1)S(1)}, u32[]{:S(2)}, u32[]{:S(2)}) collective-permute-start(bf16[256,768]{1,0:T(8,128)(2,1)S(1)} %shard_map.129), channel_id=1, source_target_pairs={{128,64},{129,65},{130,66},{131,67},{132,68},{133,69},{134,70},{13... | collective-permute-start | bytes 1179656 | tf_op jit(solution)/shard_map/ppermute | solution.py:29
  92.5 14.1 %collective-permute-start.25 = (bf16[128,768]{1,0:T(8,128)(2,1)S(1)}, bf16[128,768]{1,0:T(8,128)(2,1)S(1)}, u32[]{:S(2)}, u32[]{:S(2)}) collective-permute-start(bf16[128,768]{1,0:T(8,128)(2,1)S(1)} %get-tuple-element.76), channel_id=1, source_target_pairs={{64,1},{65,0},{66,3},{67,2},{68,5},{69,4},{70,7},{71,6},{72,9},{73... | collective-permute-start | bytes 589832 | tf_op jit(solution)/shard_map/ppermute | solution.py:29
  93.8 27.2 %collective-permute-start.12 = (bf16[256,768]{1,0:T(8,128)(2,1)S(1)}, bf16[256,768]{1,0:T(8,128)(2,1)S(1)}, u32[]{:S(2)}, u32[]{:S(2)}) collective-permute-start(bf16[256,768]{1,0:T(8,128)(2,1)S(1)} %shard_map.128.mixed), channel_id=1, source_target_pairs={{192,193},{193,192},{194,195},{195,194},{196,197},{197,196},{198,1... | collective-permute-start | bytes 1179656 | tf_op jit(solution)/shard_map/ppermute | solution.py:29
  102.9 15.7 %collective-permute-start.34 = (bf16[2,2,48,768]{3,2,1,0:T(8,128)(2,1)S(1)}, bf16[2,2,48,768]{3,2,1,0:T(8,128)(2,1)S(1)}, u32[]{:S(2)}, u32[]{:S(2)}) collective-permute-start(bf16[2,2,48,768]{3,2,1,0:T(8,128)(2,1)S(1)} %get-tuple-element.89), channel_id=1, source_target_pairs={{0,4},{2,6},{4,0},{6,2},{8,12},{10,14},{12,8},{14,10},{16,20},{18,... | collective-permute-start | bytes 884744 | tf_op jit(solution)/shard_map/ppermute | solution.py:351
  106.6 23.5 %collective-permute-start.23 = (bf16[256,768]{1,0:T(8,128)(2,1)S(1)}, bf16[256,768]{1,0:T(8,128)(2,1)S(1)}, u32[]{:S(2)}, u32[]{:S(2)}) collective-permute-start(bf16[256,768]{1,0:T(8,128)(2,1)S(1)} %shard_map.136), channel_id=1, source_target_pairs={{64,128},{65,129},{66,130},{67,131},{68,132},{69,133},{70,134},{71... | collective-permute-start | bytes 1179656 | tf_op jit(solution)/shard_map/ppermute | solution.py:29
  109.2 20.8 %collective-permute-start.28 = (bf16[256,768]{1,0:T(8,128)(2,1)S(1)}, bf16[256,768]{1,0:T(8,128)(2,1)S(1)}, u32[]{:S(2)}, u32[]{:S(2)}) collective-permute-start(bf16[256,768]{1,0:T(8,128)(2,1)S(1)} %shard_map.139), channel_id=1, source_target_pairs={{0,64},{1,65},{128,192},{129,193},{2,66},{3,67},{130,194},{131,195... | collective-permute-start | bytes 1179656 | tf_op jit(solution)/shard_map/ppermute | solution.py:29
  111.2 15.4 %collective-permute-start.30 = (bf16[128,768]{1,0:T(8,128)(2,1)S(1)}, bf16[128,768]{1,0:T(8,128)(2,1)S(1)}, u32[]{:S(2)}, u32[]{:S(2)}) collective-permute-start(bf16[128,768]{1,0:T(8,128)(2,1)S(1)} %get-tuple-element.81.refs_2_), channel_id=1, source_target_pairs={{0,1},{1,0},{2,3},{3,2},{4,5},{5,4},{6,7},{7,6},{8,9},{9,8},{10,11... | collective-permute-start | bytes 589832 | tf_op jit(solution)/shard_map/ppermute | solution.py:29
  118.6 11.5 %collective-permute-start.29 = (bf16[128,768]{1,0:T(8,128)(2,1)S(1)}, bf16[128,768]{1,0:T(8,128)(2,1)S(1)}, u32[]{:S(2)}, u32[]{:S(2)}) collective-permute-start(bf16[128,768]{1,0:T(8,128)(2,1)S(1)} %get-tuple-element.80.refs_0_), channel_id=1, source_target_pairs={{0,1},{1,0},{2,3},{3,2},{4,5},{5,4},{6,7},{7,6},{8,9},{9,8},{10,11... | collective-permute-start | bytes 589832 | tf_op jit(solution)/shard_map/ppermute | solution.py:29
  121.1 9.9 %collective-permute-start.35 = (bf16[2,48,768]{2,1,0:T(8,128)(2,1)S(1)}, bf16[2,48,768]{2,1,0:T(8,128)(2,1)S(1)}, u32[]{:S(2)}, u32[]{:S(2)}) collective-permute-start(bf16[2,48,768]{2,1,0:T(8,128)(2,1)S(1)} %get-tuple-element.91), channel_id=1, source_target_pairs={{0,12},{2,14},{4,8},{6,10},{8,4},{10,6},{12,0},{14,2},{16,28},{18,... | collective-permute-start | bytes 442376 | tf_op jit(solution)/shard_map/ppermute | solution.py:351
  (15 other events, 59.0 us)

commit v4 on v3

--- a/solution.py
+++ b/solution.py
@@ -86,14 +86,38 @@
         pairs.append((w_up.at[:, here], up_here.at[:, here]))
     pairs.append((w_down, down_here))
     loads = [pltpu.make_async_copy(a, b, came.at[i]) for i, (a, b) in enumerate(pairs)]
-    for load in loads:
-        load.start()
+    first = lax.axis_index("section") == 0
+    loads[0].start()
+    loads[1].start()
+
+    @pl.when(first)
+    def _():
+        for load in loads[2:]:
+            load.start()
+
     loads[0].wait()
     loads[1].wait()
-    rows = inputs_here[0]
-    activate(rows, gain_here, up_here, act, loads[2:-1])
-    loads[-1].wait()
-    part_out[...] = down_part(rows, act, down_here)
+
+    @pl.when(first)
+    def _():
+        rows = inputs_here[0]
+        activate(rows, gain_here, up_here, act, loads[2:-1])
+        loads[-1].wait()
+        part_out[...] = down_part(rows, act, down_here)
+
+
+def fetch_body(after, w_up, w_down, up_in, down_in, up_here, down_here, came):
+    loads = [
+        pltpu.make_async_copy(w_up, up_here, came.at[0]),
+        pltpu.make_async_copy(w_down, down_here, came.at[1]),
+    ]
+
+    @pl.when(lax.axis_index("section") > 0)
+    def _():
+        for load in loads:
+            load.start()
+        for load in loads:
+            load.wait()
 
 
 def at_section(stage):
@@ -185,7 +209,7 @@
     return jnp.concatenate([part[...] for part in parts], axis=0)
 
 
-def mix_body(last, *refs):
+def mix_body(last, token, *refs):
     *pairs, w_down, out = refs
     count = pairs[0].shape[0]
 
@@ -200,20 +224,19 @@
     out[...] = stacked(parts)
 
 
-def produced_body(mixed, other, *refs):
-    *backs, out = refs
-    section = lax.axis_index("section")
-    value = plus(mixed[...], other[...])
-    for at, back in enumerate(backs):
-        value = jnp.where(section == at, back[...], value)
-    out[...] = value
-
-
-def grads_body(micros, early, late, *refs):
+def token_body(part, out):
+    out[...] = part[: out.shape[0], : out.shape[1]]
+
+
+def produced_body(last, mixed, other, back, out):
+    out[...] = jnp.where(lax.axis_index("section") == last, plus(mixed[...], other[...]), back[...])
+
+
+def grads_body(early, *refs):
     *ends, out = refs
     section = lax.axis_index("section")
-    mine = jnp.concatenate([plus(ends[2 * at][...], ends[2 * at + 1][...]) for at in range(micros)], axis=0)
-    back = jnp.where(lax.rem(section, 2) == 1, late[...], early[...])
+    mine = jnp.concatenate([plus(a[...], b[...]) for a, b in zip(ends[::3], ends[1::3])], axis=0)
+    back = jnp.where(lax.rem(section, 2) == 1, stacked(ends[2::3]), early[...])
     out[...] = jnp.where(section == 0, mine, back)
 
 
@@ -221,7 +244,7 @@
     return [(array, "held") for array in arrays]
 
 
-def kernel(body, outs, operands, scratch=(), plain=False):
+def kernel(body, outs, operands, scratch=(), plain=False, aliases={}):
     spaces = {"held": pltpu.VMEM, "copied": pltpu.VMEM, "far": pltpu.HBM}
     in_vmem = pl.BlockSpec(memory_space=pltpu.VMEM)
     return pl.pallas_call(
@@ -230,6 +253,7 @@
         in_specs=[pl.BlockSpec(memory_space=spaces[where]) for _, where in operands],
         out_specs=[in_vmem] * len(outs),
         scratch_shapes=list(scratch),
+        input_output_aliases=aliases,
         compiler_params=pltpu.CompilerParams(vmem_limit_bytes=16 * 2**20),
     )(
         *(
@@ -378,7 +402,6 @@
     rows, grads = [None for _ in micros], [None for _ in micros]
     stages = [*range(1, sections), *range(last - 1, -1, -1)]
     with_sum = (0, 1, 4, 5)
-    backs = {}
 
     def opened(micro):
         (parts[micro],) = kernel(partial(opening_body, micro), [narrow], [*held(inputs_here), *weights], scratch)
@@ -414,36 +437,44 @@
             fresh[micro] = hand_over(parts[micro], source, stage)
         if layer in with_sum:
             sum_turn()
+        if layer == 0:
+            up_here, down_here = kernel(
+                fetch_body,
+                [(w_up.shape, bf16), (w_down.shape, bf16)],
+                [*held(parts[-1]), (w_up, "far"), (w_down, "far"), *held(up_here, down_here)],
+                [pltpu.SemaphoreType.DMA((2,))],
+                aliases={3: 0, 4: 1},
+            )
+            weights = held(gain_here, up_here, down_here)
         if layer == last:
-            (mixed,) = kernel(
-                partial(mix_body, last),
-                [packed],
-                held(*(array for both_of in zip(rows, acts) for array in both_of), down_here),
-            )
-            other = handed(mixed, [((last, t), (last, 1 - t)) for t in both])
             slopes = kernel(partial(slope_body, last), [broad for _ in micros], held(*rows, gain_here, up_here))
             (packed_rows,) = kernel(pack_body, [packed], held(*rows))
-            backs[0] = handed(packed_rows, [((s + 1, t), (s, t)) for s in range(0, last, 2) for t in both])
         elif layer == last + 1:
-            backs[1] = handed(packed_rows, [((s + 1, t), (s, t)) for s in range(1, last, 2) for t in both])
+            back = handed(packed_rows, [((s + 1, t), (s, t)) for s in range(last) for t in both])
         elif layer == len(stages) - 1:
+            (token,) = kernel(token_body, [((16, 128), bf16)], held(parts[-1]))
+            token = handed(token, [((1, t), (last, t)) for t in both])
             (sent,) = kernel(pack_body, [packed], held(*grads))
             early = handed(sent, [((s, t), (s + 1, t)) for s in range(1, last, 2) for t in both])
         stepped(layer, 0, fresh[0])
     layer = len(stages)
-    others = [None for _ in micros]
+    others, lates = [None for _ in micros], [None for _ in micros]
     for micro in micros:
         if micro:
             stepped(layer - 1, micro, fresh[micro])
         others[micro] = handed(parts[micro], [((0, t), (0, 1 - t)) for t in both])
-    (sent,) = kernel(pack_body, [packed], held(*grads))
-    late = handed(sent, [((s, t), (s + 1, t)) for s in range(0, last, 2) for t in both])
+        lates[micro] = handed(grads[micro], [((s, t), (s + 1, t)) for s in range(0, last, 2) for t in both])
+    (mixed,) = kernel(
+        partial(mix_body, last),
+        [packed],
+        held(token, *(array for both_of in zip(rows, acts) for array in both_of), down_here),
+    )
+    other = handed(mixed, [((last, t), (last, 1 - t)) for t in both])
     sum_turn()
     sum_turn()
-    returned = [backs[s % 2] for s in range(last)]
-    (produced,) = kernel(produced_body, [packed], held(mixed, other, *returned), plain=True)
-    ends = [array for both_halves in zip(parts, others) for array in both_halves]
-    (grads_done,) = kernel(partial(grads_body, len(micros)), [packed], held(early, late, *ends), plain=True)
+    (produced,) = kernel(partial(produced_body, last), [packed], held(mixed, other, back), plain=True)
+    ends = [array for one_micro in zip(parts, others, lates) for array in one_micro]
+    (grads_done,) = kernel(grads_body, [packed], held(early, *ends), plain=True)
     new_up, new_down = state[0][None], state[1][None]
     whole_shape = (1, *inputs.shape)
     return (produced.reshape(whole_shape), grads_done.reshape(whole_shape), new_up, new_down)

time: 133 us -> 128 us (0.962)
  starting transfers between devices: 49.4 us -> 44.2 us
    ppermute x31 -> x32, starting transfers between devices: 42.5 us -> 36.3 us  [handed(): lax.ppermute(value, ('section', 'tensor'), [(a * halves + t, b * halves +...]
    ppermute x4, waiting for transfers between devices: 0.01 us -> 3.44 us  [sum_turn(): lax.ppermute(sent, 'dp', by_position((turn - 1) // 2, near if turn % 2 el...]
    ppermute x31 -> x32, waiting for transfers between devices: 59.8 us -> 57.3 us  [handed(): lax.ppermute(value, ('section', 'tensor'), [(a * halves + t, b * halves +...]
    pallas_call x27 -> x28, Pallas kernels: 16.7 us -> 16.5 us  [kernel(): pl.pallas_call(body, out_shape=[(jax.ShapeDtypeStruct if plain else pltpu...]
  transfers between devices with their start and end apart: 36 -> 37, of which waited for: 8 -> 9; matrix products, arithmetic and copies ran while one was open for 0% -> 0% of each run, Pallas kernels for 10% -> 10%
where the time goes in v4:
time: 128 us; the launch traced here: 127 us
  waiting for transfers between devices  65.3 us (51%)
  starting transfers between devices  44.2 us (35%)
  Pallas kernels  16.5 us (13%)
    ppermute x32, waiting for transfers between devices, handed(): lax.ppermute(value, ('section', 'tensor'), [(a * halves + t, b * halves +...  57.3 us
    ppermute x32, starting transfers between devices, handed(): lax.ppermute(value, ('section', 'tensor'), [(a * halves + t, b * halves +...  36.3 us
    pallas_call x28, Pallas kernels, kernel(): pl.pallas_call(body, out_shape=[(jax.ShapeDtypeStruct if plain else pltpu...  16.5 us
    ppermute x4, starting transfers between devices, sum_turn(): lax.ppermute(sent, 'dp', by_position((turn - 1) // 2, near if turn % 2 el...  7.85 us
    ppermute x1, waiting for transfers between devices, sum_turn(): gots = lax.ppermute(other, 'dp', by_position(2, lambda c: 1 - c))  4.52 us
    ppermute x4, waiting for transfers between devices, sum_turn(): lax.ppermute(sent, 'dp', by_position((turn - 1) // 2, near if turn % 2 el...  3.44 us
  transfers between devices with their start and end apart: 37, of which 9 were waited for; matrix products, arithmetic and copies ran while one was open for 0% of the time, Pallas kernels for 10%

profile of v4, /device:TPU:6, one launch (start us, length us, event | category | flops | bytes accessed | tf_op | source)
XLA Modules:
  0.0 127.3 jit_solution(649319158503608651)
XLA Ops:
  0.6 2.4 %shard_map.142 = (bf16[2,4,4,48,768]{4,3,2,1,0:T(8,128)(2,1)S(1)}, bf16[2,4,4,48,768]{4,3,2,1,0:T(8,128)(2,1)S(1)}) custom-call(bf16[4,4,2,24,1536]{4,3,2,1,0:T(8,128)(2,1)} %bitcast.16, bf16[4,4,2,48,768]{4,3,2,1,0:T(8,128)(2,1)} %bitcast.17), custom_call_target="tpu_custom_call" | custom-call | tf_op jit(solution)/shard_map/pallas_call | solution.py:250
  3.2 4.5 %collective-permute-done.32.got = bf16[2,4,4,48,768]{4,3,2,1,0:T(8,128)(2,1)S(1)} collective-permute-done((bf16[2,4,4,48,768]{4,3,2,1,0:T(8,128)(2,1)S(1)}, bf16[2,4,4,48,768]{4,3,2,1,0:T(8,128)(2,1)S(1)}, u32[]{:S(2)}, u32[]{:S(2)}) %collective-permute-start.32) | collective-permute-done | bytes 2359328 | tf_op jit(solution)/shard_map/ppermute | solution.py:370
  9.1 3.2 %shard_map.120 = (bf16[128,768]{1,0:T(8,128)(2,1)S(1)}, bf16[2,128,768]{2,1,0:T(8,128)(2,1)S(1)}, f32[1,768]{1,0:T(1,128)S(1)}, bf16[768,1536]{1,0:T(8,128)(2,1)S(1)}, bf16[1536,768]{1,0:T(8,128)(2,1)S(1)}) custom-call(bf16[2,128,768]{2,1,0:T(8,128)(2,1)} %inputs.1, f32[1,768]{1,0:T(1,128)} %gain.1, bf16[768,1536]{1,0:T(8,128)(2,1)} %bitcast.12, ...), custom_call_target="tpu_custom_call" | custom-call | tf_op jit(solution)/shard_map/pallas_call | solution.py:250
  13.5 1.3 %collective-permute-start = (bf16[128,768]{1,0:T(8,128)(2,1)S(1)}, bf16[128,768]{1,0:T(8,128)(2,1)S(1)}, u32[]{:S(2)}, u32[]{:S(2)}) collective-permute-start(bf16[128,768]{1,0:T(8,128)(2,1)S(1)} %shard_map.121.after), channel_id=1, source_target_pairs={{0,64},{1,65},{2,66},{3,67},{4,68},{5,69},{6,70},{7,71},{8,72},{9,... | collective-permute-start | bytes 589832 | tf_op jit(solution)/shard_map/ppermute | solution.py:29
  14.8 5.4 %collective-permute-start.1 = (bf16[128,768]{1,0:T(8,128)(2,1)S(1)}, bf16[128,768]{1,0:T(8,128)(2,1)S(1)}, u32[]{:S(2)}, u32[]{:S(2)}) collective-permute-start(bf16[128,768]{1,0:T(8,128)(2,1)S(1)} %shard_map.121.after), channel_id=1, source_target_pairs={{0,65},{1,64},{2,67},{3,66},{4,69},{5,68},{6,71},{7,70},{8,73},{9,... | collective-permute-start | bytes 589832 | tf_op jit(solution)/shard_map/ppermute | solution.py:29
  20.2 1.3 %collective-permute-start.8 = (bf16[128,768]{1,0:T(8,128)(2,1)S(1)}, bf16[128,768]{1,0:T(8,128)(2,1)S(1)}, u32[]{:S(2)}, u32[]{:S(2)}) collective-permute-start(bf16[128,768]{1,0:T(8,128)(2,1)S(1)} %get-tuple-element.63), channel_id=1, source_target_pairs={{0,64},{1,65},{2,66},{3,67},{4,68},{5,69},{6,70},{7,71},{8,72},{9,... | collective-permute-start | bytes 589832 | tf_op jit(solution)/shard_map/ppermute | solution.py:29
  21.5 1.3 %collective-permute-start.9 = (bf16[128,768]{1,0:T(8,128)(2,1)S(1)}, bf16[128,768]{1,0:T(8,128)(2,1)S(1)}, u32[]{:S(2)}, u32[]{:S(2)}) collective-permute-start(bf16[128,768]{1,0:T(8,128)(2,1)S(1)} %get-tuple-element.63), channel_id=1, source_target_pairs={{0,65},{1,64},{2,67},{3,66},{4,69},{5,68},{6,71},{7,70},{8,73},{9,... | collective-permute-start | bytes 589832 | tf_op jit(solution)/shard_map/ppermute | solution.py:29
  22.9 2.6 %collective-permute-done.1.crossed = bf16[128,768]{1,0:T(8,128)(2,1)S(1)} collective-permute-done((bf16[128,768]{1,0:T(8,128)(2,1)S(1)}, bf16[128,768]{1,0:T(8,128)(2,1)S(1)}, u32[]{:S(2)}, u32[]{:S(2)}) %collective-permute-start.1) | collective-permute-done | bytes 196640 | tf_op jit(solution)/shard_map/ppermute | solution.py:29
  26.9 1.7 %collective-permute-done.9.crossed = bf16[128,768]{1,0:T(8,128)(2,1)S(1)} collective-permute-done((bf16[128,768]{1,0:T(8,128)(2,1)S(1)}, bf16[128,768]{1,0:T(8,128)(2,1)S(1)}, u32[]{:S(2)}, u32[]{:S(2)}) %collective-permute-start.9) | collective-permute-done | bytes 196640 | tf_op jit(solution)/shard_map/ppermute | solution.py:29
  34.5 1.8 %collective-permute-done.33.got = bf16[2,2,4,48,768]{4,3,2,1,0:T(8,128)(2,1)S(1)} collective-permute-done((bf16[2,2,4,48,768]{4,3,2,1,0:T(8,128)(2,1)S(1)}, bf16[2,2,4,48,768]{4,3,2,1,0:T(8,128)(2,1)S(1)}, u32[]{:S(2)}, u32[]{:S(2)}) %collective-permute-start.33) | collective-permute-done | bytes 1179680 | tf_op jit(solution)/shard_map/ppermute | solution.py:375
  36.6 2.3 %collective-permute-start.34 = (bf16[2,4,48,768]{3,2,1,0:T(8,128)(2,1)S(1)}, bf16[2,4,48,768]{3,2,1,0:T(8,128)(2,1)S(1)}, u32[]{:S(2)}, u32[]{:S(2)}) collective-permute-start(bf16[2,4,48,768]{3,2,1,0:T(8,128)(2,1)S(1)} %get-tuple-element.91), channel_id=1, source_target_pairs={{0,48},{2,50},{4,52},{6,54},{8,56},{10,58},{12,60},{14,62},{16,32}... | collective-permute-start | bytes 1769480 | tf_op jit(solution)/shard_map/ppermute | solution.py:375
  40.5 1.5 %shard_map.129 = (f32[128,1536]{1,0:T(8,128)S(1)}, f32[128,1536]{1,0:T(8,128)S(1)}) custom-call(bf16[128,768]{1,0:T(8,128)(2,1)S(1)} %get-tuple-element.68.refs_0_.rows, bf16[128,768]{1,0:T(8,128)(2,1)S(1)} %get-tuple-element.62.refs_1_.rows.refs_2_, f32[1,768]{1,0:T(1,128)S(1)} %get-tuple-element.52.gain.refs_2_, ...), custom_call_target="tpu_custom_call" | custom-call | tf_op jit(solution)/shard_map/pallas_call | solution.py:250
  50.3 30.9 %collective-permute-done.28.straight = bf16[128,768]{1,0:T(8,128)(2,1)S(1)} collective-permute-done((bf16[128,768]{1,0:T(8,128)(2,1)S(1)}, bf16[128,768]{1,0:T(8,128)(2,1)S(1)}, u32[]{:S(2)}, u32[]{:S(2)}) %collective-permute-start.28) | collective-permute-done | bytes 196640 | tf_op jit(solution)/shard_map/ppermute | solution.py:29
  81.2 10.2 %collective-permute-done.29.crossed = bf16[128,768]{1,0:T(8,128)(2,1)S(1)} collective-permute-done((bf16[128,768]{1,0:T(8,128)(2,1)S(1)}, bf16[128,768]{1,0:T(8,128)(2,1)S(1)}, u32[]{:S(2)}, u32[]{:S(2)}) %collective-permute-start.29) | collective-permute-done | bytes 196640 | tf_op jit(solution)/shard_map/ppermute | solution.py:29
  91.4 1.9 %shard_map.140 = (bf16[128,768]{1,0:T(8,128)(2,1)S(1)}, bf16[128,768]{1,0:T(8,128)(2,1)S(1)}) custom-call(bf16[128,768]{1,0:T(8,128)(2,1)S(1)} %collective-permute-done.28.straight, bf16[128,768]{1,0:T(8,128)(2,1)S(1)} %collective-permute-done.29.crossed, bf16[128,768]{1,0:T(8,128)(2,1)S(1)} %get-tuple-element.80.refs_1_.kept, ...), custom_call_target="tpu_custom_call" | custom-call | tf_op jit(solution)/shard_map/pallas_call | solution.py:250
  93.2 1.9 %collective-permute-start.30 = (bf16[128,768]{1,0:T(8,128)(2,1)S(1)}, bf16[128,768]{1,0:T(8,128)(2,1)S(1)}, u32[]{:S(2)}, u32[]{:S(2)}) collective-permute-start(bf16[128,768]{1,0:T(8,128)(2,1)S(1)} %get-tuple-element.84.refs_3_), channel_id=1, source_target_pairs={{0,1},{1,0},{2,3},{3,2},{4,5},{5,4},{6,7},{7,6},{8,9},{9,8},{10,11... | collective-permute-start | bytes 589832 | tf_op jit(solution)/shard_map/ppermute | solution.py:29
  95.2 1.3 %collective-permute-start.31 = (bf16[128,768]{1,0:T(8,128)(2,1)S(1)}, bf16[128,768]{1,0:T(8,128)(2,1)S(1)}, u32[]{:S(2)}, u32[]{:S(2)}) collective-permute-start(bf16[128,768]{1,0:T(8,128)(2,1)S(1)} %get-tuple-element.85), channel_id=1, source_target_pairs={{0,64},{1,65},{128,192},{129,193},{2,66},{3,67},{130,194},{131,195... | collective-permute-start | bytes 589832 | tf_op jit(solution)/shard_map/ppermute | solution.py:29
  97.3 1.7 %collective-permute-start.35 = (bf16[2,2,48,768]{3,2,1,0:T(8,128)(2,1)S(1)}, bf16[2,2,48,768]{3,2,1,0:T(8,128)(2,1)S(1)}, u32[]{:S(2)}, u32[]{:S(2)}) collective-permute-start(bf16[2,2,48,768]{3,2,1,0:T(8,128)(2,1)S(1)} %get-tuple-element.93), channel_id=1, source_target_pairs={{0,4},{2,6},{4,0},{6,2},{8,12},{10,14},{12,8},{14,10},{16,20},{18,... | collective-permute-start | bytes 884744 | tf_op jit(solution)/shard_map/ppermute | solution.py:375
  101.1 4.9 %collective-permute-done.30.refs_4_ = bf16[128,768]{1,0:T(8,128)(2,1)S(1)} collective-permute-done((bf16[128,768]{1,0:T(8,128)(2,1)S(1)}, bf16[128,768]{1,0:T(8,128)(2,1)S(1)}, u32[]{:S(2)}, u32[]{:S(2)}) %collective-permute-start.30) | collective-permute-done | bytes 196640 | tf_op jit(solution)/shard_map/ppermute | solution.py:29
  106.7 1.9 %shard_map.139 = (bf16[128,768]{1,0:T(8,128)(2,1)S(1)}, bf16[128,768]{1,0:T(8,128)(2,1)S(1)}) custom-call(bf16[128,768]{1,0:T(8,128)(2,1)S(1)} %collective-permute-done.24.straight, bf16[128,768]{1,0:T(8,128)(2,1)S(1)} %collective-permute-done.25.crossed, bf16[128,768]{1,0:T(8,128)(2,1)S(1)} %get-tuple-element.79.refs_0_.kept, ...), custom_call_target="tpu_custom_call" | custom-call | tf_op jit(solution)/shard_map/pallas_call | solution.py:250
  108.6 3.1 %collective-permute-start.26 = (bf16[128,768]{1,0:T(8,128)(2,1)S(1)}, bf16[128,768]{1,0:T(8,128)(2,1)S(1)}, u32[]{:S(2)}, u32[]{:S(2)}) collective-permute-start(bf16[128,768]{1,0:T(8,128)(2,1)S(1)} %get-tuple-element.82.refs_0_), channel_id=1, source_target_pairs={{0,1},{1,0},{2,3},{3,2},{4,5},{5,4},{6,7},{7,6},{8,9},{9,8},{10,11... | collective-permute-start | bytes 589832 | tf_op jit(solution)/shard_map/ppermute | solution.py:29
  113.1 7.1 %collective-permute-done.26.refs_1_ = bf16[128,768]{1,0:T(8,128)(2,1)S(1)} collective-permute-done((bf16[128,768]{1,0:T(8,128)(2,1)S(1)}, bf16[128,768]{1,0:T(8,128)(2,1)S(1)}, u32[]{:S(2)}, u32[]{:S(2)}) %collective-permute-start.26) | collective-permute-done | bytes 196640 | tf_op jit(solution)/shard_map/ppermute | solution.py:29
  120.2 3.0 %collective-permute-start.36 = (bf16[2,48,768]{2,1,0:T(8,128)(2,1)S(1)}, bf16[2,48,768]{2,1,0:T(8,128)(2,1)S(1)}, u32[]{:S(2)}, u32[]{:S(2)}) collective-permute-start(bf16[2,48,768]{2,1,0:T(8,128)(2,1)S(1)} %get-tuple-element.95), channel_id=1, source_target_pairs={{0,12},{2,14},{4,8},{6,10},{8,4},{10,6},{12,0},{14,2},{16,28},{18,... | collective-permute-start | bytes 442376 | tf_op jit(solution)/shard_map/ppermute | solution.py:375
  124.9 1.6 %collective-permute-done.36.got = bf16[2,48,768]{2,1,0:T(8,128)(2,1)S(1)} collective-permute-done((bf16[2,48,768]{2,1,0:T(8,128)(2,1)S(1)}, bf16[2,48,768]{2,1,0:T(8,128)(2,1)S(1)}, u32[]{:S(2)}, u32[]{:S(2)}) %collective-permute-start.36) | collective-permute-done | bytes 147488 | tf_op jit(solution)/shard_map/ppermute | solution.py:375
  (84 shorter events, 27.4 us)
Async XLA Ops:
  3.1 4.6 %collective-permute-start.32 = (bf16[2,4,4,48,768]{4,3,2,1,0:T(8,128)(2,1)S(1)}, bf16[2,4,4,48,768]{4,3,2,1,0:T(8,128)(2,1)S(1)}, u32[]{:S(2)}, u32[]{:S(2)}) collective-permute-start(bf16[2,4,4,48,768]{4,3,2,1,0:T(8,128)(2,1)S(1)} %get-tuple-element.87), channel_id=1, source_target_pairs={{0,2},{2,0},{4,6},{6,4},{8,10},{10,8},{12,14},{14,12},{16,18},{18,... | collective-permute-start | bytes 7077896 | tf_op jit(solution)/shard_map/ppermute | solution.py:370
  8.2 28.1 %collective-permute-start.33 = (bf16[2,2,4,48,768]{4,3,2,1,0:T(8,128)(2,1)S(1)}, bf16[2,2,4,48,768]{4,3,2,1,0:T(8,128)(2,1)S(1)}, u32[]{:S(2)}, u32[]{:S(2)}) collective-permute-start(bf16[2,2,4,48,768]{4,3,2,1,0:T(8,128)(2,1)S(1)} %get-tuple-element.89), channel_id=1, source_target_pairs={{0,16},{2,18},{4,20},{6,22},{8,24},{10,26},{12,28},{14,30},{16,0},... | collective-permute-start | bytes 3538952 | tf_op jit(solution)/shard_map/ppermute | solution.py:375
  13.5 9.4 %collective-permute-start = (bf16[128,768]{1,0:T(8,128)(2,1)S(1)}, bf16[128,768]{1,0:T(8,128)(2,1)S(1)}, u32[]{:S(2)}, u32[]{:S(2)}) collective-permute-start(bf16[128,768]{1,0:T(8,128)(2,1)S(1)} %shard_map.121.after), channel_id=1, source_target_pairs={{0,64},{1,65},{2,66},{3,67},{4,68},{5,69},{6,70},{7,71},{8,72},{9,... | collective-permute-start | bytes 589832 | tf_op jit(solution)/shard_map/ppermute | solution.py:29
  14.8 10.6 %collective-permute-start.1 = (bf16[128,768]{1,0:T(8,128)(2,1)S(1)}, bf16[128,768]{1,0:T(8,128)(2,1)S(1)}, u32[]{:S(2)}, u32[]{:S(2)}) collective-permute-start(bf16[128,768]{1,0:T(8,128)(2,1)S(1)} %shard_map.121.after), channel_id=1, source_target_pairs={{0,65},{1,64},{2,67},{3,66},{4,69},{5,68},{6,71},{7,70},{8,73},{9,... | collective-permute-start | bytes 589832 | tf_op jit(solution)/shard_map/ppermute | solution.py:29
  20.2 6.7 %collective-permute-start.8 = (bf16[128,768]{1,0:T(8,128)(2,1)S(1)}, bf16[128,768]{1,0:T(8,128)(2,1)S(1)}, u32[]{:S(2)}, u32[]{:S(2)}) collective-permute-start(bf16[128,768]{1,0:T(8,128)(2,1)S(1)} %get-tuple-element.63), channel_id=1, source_target_pairs={{0,64},{1,65},{2,66},{3,67},{4,68},{5,69},{6,70},{7,71},{8,72},{9,... | collective-permute-start | bytes 589832 | tf_op jit(solution)/shard_map/ppermute | solution.py:29
  21.5 7.1 %collective-permute-start.9 = (bf16[128,768]{1,0:T(8,128)(2,1)S(1)}, bf16[128,768]{1,0:T(8,128)(2,1)S(1)}, u32[]{:S(2)}, u32[]{:S(2)}) collective-permute-start(bf16[128,768]{1,0:T(8,128)(2,1)S(1)} %get-tuple-element.63), channel_id=1, source_target_pairs={{0,65},{1,64},{2,67},{3,66},{4,69},{5,68},{6,71},{7,70},{8,73},{9,... | collective-permute-start | bytes 589832 | tf_op jit(solution)/shard_map/ppermute | solution.py:29
  31.5 7.3 %collective-permute-start.12 = (bf16[128,768]{1,0:T(8,128)(2,1)S(1)}, bf16[128,768]{1,0:T(8,128)(2,1)S(1)}, u32[]{:S(2)}, u32[]{:S(2)}) collective-permute-start(bf16[128,768]{1,0:T(8,128)(2,1)S(1)} %get-tuple-element.66), channel_id=1, source_target_pairs={{128,192},{129,193},{130,194},{131,195},{132,196},{133,197},{134,1... | collective-permute-start | bytes 589832 | tf_op jit(solution)/shard_map/ppermute | solution.py:29
  32.4 6.5 %collective-permute-start.13 = (bf16[128,768]{1,0:T(8,128)(2,1)S(1)}, bf16[128,768]{1,0:T(8,128)(2,1)S(1)}, u32[]{:S(2)}, u32[]{:S(2)}) collective-permute-start(bf16[128,768]{1,0:T(8,128)(2,1)S(1)} %get-tuple-element.66), channel_id=1, source_target_pairs={{128,193},{129,192},{130,195},{131,194},{132,197},{133,196},{134,1... | collective-permute-start | bytes 589832 | tf_op jit(solution)/shard_map/ppermute | solution.py:29
  33.1 8.9 %collective-permute-start.6 = (bf16[128,768]{1,0:T(8,128)(2,1)S(1)}, bf16[128,768]{1,0:T(8,128)(2,1)S(1)}, u32[]{:S(2)}, u32[]{:S(2)}) collective-permute-start(bf16[128,768]{1,0:T(8,128)(2,1)S(1)} %get-tuple-element.61), channel_id=1, source_target_pairs={{192,128},{193,129},{194,130},{195,131},{196,132},{197,133},{198,1... | collective-permute-start | bytes 589832 | tf_op jit(solution)/shard_map/ppermute | solution.py:29
  33.8 8.2 %collective-permute-start.7 = (bf16[128,768]{1,0:T(8,128)(2,1)S(1)}, bf16[128,768]{1,0:T(8,128)(2,1)S(1)}, u32[]{:S(2)}, u32[]{:S(2)}) collective-permute-start(bf16[128,768]{1,0:T(8,128)(2,1)S(1)} %get-tuple-element.61), channel_id=1, source_target_pairs={{192,129},{193,128},{194,131},{195,130},{196,133},{197,132},{198,1... | collective-permute-start | bytes 589832 | tf_op jit(solution)/shard_map/ppermute | solution.py:29
  36.6 59.9 %collective-permute-start.34 = (bf16[2,4,48,768]{3,2,1,0:T(8,128)(2,1)S(1)}, bf16[2,4,48,768]{3,2,1,0:T(8,128)(2,1)S(1)}, u32[]{:S(2)}, u32[]{:S(2)}) collective-permute-start(bf16[2,4,48,768]{3,2,1,0:T(8,128)(2,1)S(1)} %get-tuple-element.91), channel_id=1, source_target_pairs={{0,48},{2,50},{4,52},{6,54},{8,56},{10,58},{12,60},{14,62},{16,32}... | collective-permute-start | bytes 1769480 | tf_op jit(solution)/shard_map/ppermute | solution.py:375
  45.0 36.2 %collective-permute-start.28 = (bf16[128,768]{1,0:T(8,128)(2,1)S(1)}, bf16[128,768]{1,0:T(8,128)(2,1)S(1)}, u32[]{:S(2)}, u32[]{:S(2)}) collective-permute-start(bf16[128,768]{1,0:T(8,128)(2,1)S(1)} %get-tuple-element.72.part), channel_id=1, source_target_pairs={{64,0},{65,1},{66,2},{67,3},{68,4},{69,5},{70,6},{71,7},{72,8},{73... | collective-permute-start | bytes 589832 | tf_op jit(solution)/shard_map/ppermute | solution.py:29
  46.3 45.1 %collective-permute-start.29 = (bf16[128,768]{1,0:T(8,128)(2,1)S(1)}, bf16[128,768]{1,0:T(8,128)(2,1)S(1)}, u32[]{:S(2)}, u32[]{:S(2)}) collective-permute-start(bf16[128,768]{1,0:T(8,128)(2,1)S(1)} %get-tuple-element.72.part), channel_id=1, source_target_pairs={{64,1},{65,0},{66,3},{67,2},{68,5},{69,4},{70,7},{71,6},{72,9},{73... | collective-permute-start | bytes 589832 | tf_op jit(solution)/shard_map/ppermute | solution.py:29
  47.7 51.4 %collective-permute-start.24 = (bf16[128,768]{1,0:T(8,128)(2,1)S(1)}, bf16[128,768]{1,0:T(8,128)(2,1)S(1)}, u32[]{:S(2)}, u32[]{:S(2)}) collective-permute-start(bf16[128,768]{1,0:T(8,128)(2,1)S(1)} %get-tuple-element.81), channel_id=1, source_target_pairs={{64,0},{65,1},{66,2},{67,3},{68,4},{69,5},{70,6},{71,7},{72,8},{73... | collective-permute-start | bytes 589832 | tf_op jit(solution)/shard_map/ppermute | solution.py:29
  49.0 50.8 %collective-permute-start.25 = (bf16[128,768]{1,0:T(8,128)(2,1)S(1)}, bf16[128,768]{1,0:T(8,128)(2,1)S(1)}, u32[]{:S(2)}, u32[]{:S(2)}) collective-permute-start(bf16[128,768]{1,0:T(8,128)(2,1)S(1)} %get-tuple-element.81), channel_id=1, source_target_pairs={{64,1},{65,0},{66,3},{67,2},{68,5},{69,4},{70,7},{71,6},{72,9},{73... | collective-permute-start | bytes 589832 | tf_op jit(solution)/shard_map/ppermute | solution.py:29
  93.2 12.8 %collective-permute-start.30 = (bf16[128,768]{1,0:T(8,128)(2,1)S(1)}, bf16[128,768]{1,0:T(8,128)(2,1)S(1)}, u32[]{:S(2)}, u32[]{:S(2)}) collective-permute-start(bf16[128,768]{1,0:T(8,128)(2,1)S(1)} %get-tuple-element.84.refs_3_), channel_id=1, source_target_pairs={{0,1},{1,0},{2,3},{3,2},{4,5},{5,4},{6,7},{7,6},{8,9},{9,8},{10,11... | collective-permute-start | bytes 589832 | tf_op jit(solution)/shard_map/ppermute | solution.py:29
  95.2 13.4 %collective-permute-start.31 = (bf16[128,768]{1,0:T(8,128)(2,1)S(1)}, bf16[128,768]{1,0:T(8,128)(2,1)S(1)}, u32[]{:S(2)}, u32[]{:S(2)}) collective-permute-start(bf16[128,768]{1,0:T(8,128)(2,1)S(1)} %get-tuple-element.85), channel_id=1, source_target_pairs={{0,64},{1,65},{128,192},{129,193},{2,66},{3,67},{130,194},{131,195... | collective-permute-start | bytes 589832 | tf_op jit(solution)/shard_map/ppermute | solution.py:29
  97.3 14.4 %collective-permute-start.35 = (bf16[2,2,48,768]{3,2,1,0:T(8,128)(2,1)S(1)}, bf16[2,2,48,768]{3,2,1,0:T(8,128)(2,1)S(1)}, u32[]{:S(2)}, u32[]{:S(2)}) collective-permute-start(bf16[2,2,48,768]{3,2,1,0:T(8,128)(2,1)S(1)} %get-tuple-element.93), channel_id=1, source_target_pairs={{0,4},{2,6},{4,0},{6,2},{8,12},{10,14},{12,8},{14,10},{16,20},{18,... | collective-permute-start | bytes 884744 | tf_op jit(solution)/shard_map/ppermute | solution.py:375
  99.1 24.0 %collective-permute-start.23 = (bf16[256,768]{1,0:T(8,128)(2,1)S(1)}, bf16[256,768]{1,0:T(8,128)(2,1)S(1)}, u32[]{:S(2)}, u32[]{:S(2)}) collective-permute-start(bf16[256,768]{1,0:T(8,128)(2,1)S(1)} %shard_map.138), channel_id=1, source_target_pairs={{64,128},{65,129},{66,130},{67,131},{68,132},{69,133},{70,134},{71... | collective-permute-start | bytes 1179656 | tf_op jit(solution)/shard_map/ppermute | solution.py:29
  99.8 24.2 %collective-permute-start.18 = (bf16[256,768]{1,0:T(8,128)(2,1)S(1)}, bf16[256,768]{1,0:T(8,128)(2,1)S(1)}, u32[]{:S(2)}, u32[]{:S(2)}) collective-permute-start(bf16[256,768]{1,0:T(8,128)(2,1)S(1)} %shard_map.134), channel_id=1, source_target_pairs={{64,0},{65,1},{128,64},{129,65},{192,128},{193,129},{66,2},{67,3},... | collective-permute-start | bytes 1179656 | tf_op jit(solution)/shard_map/ppermute | solution.py:29
  106.0 18.1 %collective-permute-start.17 = (bf16[256,768]{1,0:T(8,128)(2,1)S(1)}, bf16[256,768]{1,0:T(8,128)(2,1)S(1)}, u32[]{:S(2)}, u32[]{:S(2)}) collective-permute-start(bf16[256,768]{1,0:T(8,128)(2,1)S(1)} %shard_map.133.mixed), channel_id=1, source_target_pairs={{192,193},{193,192},{194,195},{195,194},{196,197},{197,196},{198,1... | collective-permute-start | bytes 1179656 | tf_op jit(solution)/shard_map/ppermute | solution.py:29
  108.6 11.6 %collective-permute-start.26 = (bf16[128,768]{1,0:T(8,128)(2,1)S(1)}, bf16[128,768]{1,0:T(8,128)(2,1)S(1)}, u32[]{:S(2)}, u32[]{:S(2)}) collective-permute-start(bf16[128,768]{1,0:T(8,128)(2,1)S(1)} %get-tuple-element.82.refs_0_), channel_id=1, source_target_pairs={{0,1},{1,0},{2,3},{3,2},{4,5},{5,4},{6,7},{7,6},{8,9},{9,8},{10,11... | collective-permute-start | bytes 589832 | tf_op jit(solution)/shard_map/ppermute | solution.py:29
  111.7 11.4 %collective-permute-start.27 = (bf16[128,768]{1,0:T(8,128)(2,1)S(1)}, bf16[128,768]{1,0:T(8,128)(2,1)S(1)}, u32[]{:S(2)}, u32[]{:S(2)}) collective-permute-start(bf16[128,768]{1,0:T(8,128)(2,1)S(1)} %get-tuple-element.83), channel_id=1, source_target_pairs={{0,64},{1,65},{128,192},{129,193},{2,66},{3,67},{130,194},{131,195... | collective-permute-start | bytes 589832 | tf_op jit(solution)/shard_map/ppermute | solution.py:29
  120.2 6.4 %collective-permute-start.36 = (bf16[2,48,768]{2,1,0:T(8,128)(2,1)S(1)}, bf16[2,48,768]{2,1,0:T(8,128)(2,1)S(1)}, u32[]{:S(2)}, u32[]{:S(2)}) collective-permute-start(bf16[2,48,768]{2,1,0:T(8,128)(2,1)S(1)} %get-tuple-element.95), channel_id=1, source_target_pairs={{0,12},{2,14},{4,8},{6,10},{8,4},{10,6},{12,0},{14,2},{16,28},{18,... | collective-permute-start | bytes 442376 | tf_op jit(solution)/shard_map/ppermute | solution.py:375
  (16 other events, 77.3 us)

commit v5 on v4

--- a/solution.py
+++ b/solution.py
@@ -32,6 +32,7 @@
 
 
 chunk = 512
+tile = 256
 
 
 def apply_norm(values):
@@ -86,31 +87,22 @@
         pairs.append((w_up.at[:, here], up_here.at[:, here]))
     pairs.append((w_down, down_here))
     loads = [pltpu.make_async_copy(a, b, came.at[i]) for i, (a, b) in enumerate(pairs)]
-    first = lax.axis_index("section") == 0
-    loads[0].start()
-    loads[1].start()
-
-    @pl.when(first)
-    def _():
-        for load in loads[2:]:
+
+    @pl.when(lax.axis_index("section") == 0)
+    def _():
+        for load in loads:
             load.start()
-
-    loads[0].wait()
-    loads[1].wait()
-
-    @pl.when(first)
-    def _():
+        loads[0].wait()
+        loads[1].wait()
         rows = inputs_here[0]
         activate(rows, gain_here, up_here, act, loads[2:-1])
         loads[-1].wait()
         part_out[...] = down_part(rows, act, down_here)
 
 
-def fetch_body(after, w_up, w_down, up_in, down_in, up_here, down_here, came):
-    loads = [
-        pltpu.make_async_copy(w_up, up_here, came.at[0]),
-        pltpu.make_async_copy(w_down, down_here, came.at[1]),
-    ]
+def fetch_body(after, gain, w_up, w_down, gain_in, up_in, down_in, gain_here, up_here, down_here, came):
+    pairs = ((gain, gain_here), (w_up, up_here), (w_down, down_here))
+    loads = [pltpu.make_async_copy(a, b, came.at[i]) for i, (a, b) in enumerate(pairs)]
 
     @pl.when(lax.axis_index("section") > 0)
     def _():
@@ -120,6 +112,13 @@
             load.wait()
 
 
+def flip_body(w_up, w_down, up_flip, down_flip):
+    for weight, flip in ((w_up, up_flip), (w_down, down_flip)):
+        for row in range(0, weight.shape[0], tile):
+            for column in range(0, weight.shape[1], tile):
+                flip[column : column + tile, row : row + tile] = weight[row : row + tile, column : column + tile].T
+
+
 def at_section(stage):
     return pl.when(lax.axis_index("section") == stage)
 
@@ -142,22 +141,19 @@
         part_out[...] = down_part(rows, act, w_down)
 
 
-def grad_part(grad, pushed, standardized, inverse_scale, gain, w_up):
-    part = lax.dot_general(pushed[...], w_up[...], across, preferred_element_type=f32) * gain
+def grad_part(grad, pushed, standardized, inverse_scale, gain, up_flip):
+    part = jnp.dot(pushed[...], up_flip[...], preferred_element_type=f32) * gain
     leading = jnp.mean(part, axis=-1, keepdims=True)
     trailing = jnp.mean(part * standardized, axis=-1, keepdims=True)
     moved = inverse_scale * (part - leading - standardized * trailing)
     return (moved + 0.5 * grad.astype(f32)).astype(bf16)
 
 
-across = (((1,), (1,)), ((), ()))
-
-
 def slope_of(upper, inner, square):
     return 0.5 * (1.0 + inner) + 0.5 * upper * (1.0 - inner * inner) * gelu_coef * (1.0 + 3.0 * 0.044715 * square)
 
 
-def turn_body(stage, micro, straight, crossed, kept, grad_in, gain, w_up, w_down, rows_out, act, part_out, pushed):
+def turn_body(stage, micro, straight, crossed, kept, grad_in, gain, w_up, up_flip, down_flip, rows_out, act, part_out, pushed):
     rows = chosen(stage, straight, crossed, rows_of(kept, micro))
     rows_out[...] = rows
 
@@ -171,9 +167,9 @@
             upper = up_of(normed, w_up, at)
             inner, square = curve(upper)
             act[:, here] = (0.5 * upper * (1.0 + inner)).astype(bf16)
-            grad_act = lax.dot_general(grad, w_down[here, :], across, preferred_element_type=f32)
+            grad_act = jnp.dot(grad, down_flip[:, here], preferred_element_type=f32)
             pushed[:, here] = (grad_act * slope_of(upper, inner, square)).astype(bf16)
-        part_out[...] = grad_part(grad, pushed, standardized, inverse_scale, gain[...], w_up)
+        part_out[...] = grad_part(grad, pushed, standardized, inverse_scale, gain[...], up_flip)
 
 
 def slope_body(last, *refs):
@@ -191,7 +187,7 @@
                 slope[:, at : at + chunk] = slope_of(upper, inner, square)
 
 
-def backward_body(stage, micro, straight, crossed, kept, rows, slope, gain, w_up, w_down, grad_out, part_out, pushed):
+def backward_body(stage, micro, straight, crossed, kept, rows, slope, gain, up_flip, down_flip, grad_out, part_out, pushed):
     grad = chosen(stage, straight, crossed, rows_of(kept, micro))
     grad_out[...] = grad
 
@@ -199,10 +195,10 @@
     def _():
         for at in range(0, pushed.shape[1], chunk):
             here = slice(at, at + chunk)
-            grad_act = lax.dot_general(grad, w_down[here, :], across, preferred_element_type=f32)
+            grad_act = jnp.dot(grad, down_flip[:, here], preferred_element_type=f32)
             pushed[:, here] = (grad_act * slope[:, here]).astype(bf16)
         standardized, inverse_scale = apply_norm(rows[...].astype(f32))
-        part_out[...] = grad_part(grad, pushed, standardized, inverse_scale, gain[...], w_up)
+        part_out[...] = grad_part(grad, pushed, standardized, inverse_scale, gain[...], up_flip)
 
 
 def stacked(parts):
@@ -395,7 +391,7 @@
         [(inputs, "far"), (norm_gain, "far"), (w_up, "far"), (w_down, "far")],
         [*scratch, loads],
     )
-    weights = held(gain_here, up_here, down_here)
+    weights, flips = held(gain_here, up_here, down_here), None
     kept = [held(inputs_here)[0] for _ in micros]
     seeds = (out_grads, "copied")
     acts, slopes = [None for _ in micros], None
@@ -416,14 +412,17 @@
             kept[micro] = (rows[micro], "held")
         elif not down:
             rows[micro], acts[micro], parts[micro] = kernel(
-                partial(turn_body, stage, micro), [narrow, wide, narrow], [*arrays, seeds, *weights], scratch
+                partial(turn_body, stage, micro),
+                [narrow, wide, narrow],
+                [*arrays, seeds, *weights[:2], *flips],
+                scratch,
             )
             kept[micro] = seeds
         else:
             grads[micro], parts[micro] = kernel(
                 partial(backward_body, stage, micro),
                 [narrow, narrow],
-                [*arrays, *held(rows[micro], slopes[micro]), *weights],
+                [*arrays, *held(rows[micro], slopes[micro]), weights[0], *flips],
                 scratch,
             )
             kept[micro] = (grads[micro], "held")
@@ -438,23 +437,29 @@
         if layer in with_sum:
             sum_turn()
         if layer == 0:
-            up_here, down_here = kernel(
+            gain_here, up_here, down_here = kernel(
                 fetch_body,
-                [(w_up.shape, bf16), (w_down.shape, bf16)],
-                [*held(parts[-1]), (w_up, "far"), (w_down, "far"), *held(up_here, down_here)],
-                [pltpu.SemaphoreType.DMA((2,))],
-                aliases={3: 0, 4: 1},
+                [(norm_gain.shape, f32), (w_up.shape, bf16), (w_down.shape, bf16)],
+                [
+                    *held(parts[-1]),
+                    *((array, "far") for array in (norm_gain, w_up, w_down)),
+                    *held(gain_here, up_here, down_here),
+                ],
+                [pltpu.SemaphoreType.DMA((3,))],
+                aliases={4: 0, 5: 1, 6: 2},
             )
             weights = held(gain_here, up_here, down_here)
+            flips = held(
+                *kernel(flip_body, [(w_up.shape[::-1], bf16), (w_down.shape[::-1], bf16)], held(up_here, down_here))
+            )
         if layer == last:
             slopes = kernel(partial(slope_body, last), [broad for _ in micros], held(*rows, gain_here, up_here))
             (packed_rows,) = kernel(pack_body, [packed], held(*rows))
-        elif layer == last + 1:
-            back = handed(packed_rows, [((s + 1, t), (s, t)) for s in range(last) for t in both])
         elif layer == len(stages) - 1:
             (token,) = kernel(token_body, [((16, 128), bf16)], held(parts[-1]))
             token = handed(token, [((1, t), (last, t)) for t in both])
             (sent,) = kernel(pack_body, [packed], held(*grads))
+            back = handed(packed_rows, [((s + 1, t), (s, t)) for s in range(last) for t in both])
             early = handed(sent, [((s, t), (s + 1, t)) for s in range(1, last, 2) for t in both])
         stepped(layer, 0, fresh[0])
     layer = len(stages)

time: 128 us -> 124 us (0.969)
  the two profiles are of different devices: /device:TPU:6 before, /device:TPU:28 now
where the time goes in v5:
time: 124 us; the launch traced here: 123 us
  waiting for transfers between devices  58.7 us (47%)
  starting transfers between devices  47.3 us (38%)
  Pallas kernels  16 us (13%)
  between operations  1.27 us (1%)
    ppermute x32, waiting for transfers between devices, handed(): lax.ppermute(value, ('section', 'tensor'), [(a * halves + t, b * halves +...  48.6 us
    ppermute x32, starting transfers between devices, handed(): lax.ppermute(value, ('section', 'tensor'), [(a * halves + t, b * halves +...  44.2 us
    pallas_call x29, Pallas kernels, kernel(): pl.pallas_call(body, out_shape=[(jax.ShapeDtypeStruct if plain else pltpu...  16 us
    ppermute x4, waiting for transfers between devices, sum_turn(): lax.ppermute(sent, 'dp', by_position((turn - 1) // 2, near if turn % 2 el...  5.59 us
    ppermute x1, waiting for transfers between devices, sum_turn(): gots = lax.ppermute(other, 'dp', by_position(2, lambda c: 1 - c))  4.52 us
    ppermute x4, starting transfers between devices, sum_turn(): lax.ppermute(sent, 'dp', by_position((turn - 1) // 2, near if turn % 2 el...  3.09 us
  transfers between devices with their start and end apart: 37, of which 9 were waited for; matrix products, arithmetic and copies ran while one was open for 0% of the time, Pallas kernels for 10%

profile of v5, /device:TPU:28, one launch (start us, length us, event | category | flops | bytes accessed | tf_op | source)
XLA Modules:
  0.0 123.4 jit_solution(2953808045801774433)
XLA Ops:
  0.6 2.4 %shard_map.143 = (bf16[2,4,4,48,768]{4,3,2,1,0:T(8,128)(2,1)S(1)}, bf16[2,4,4,48,768]{4,3,2,1,0:T(8,128)(2,1)S(1)}) custom-call(bf16[4,4,2,24,1536]{4,3,2,1,0:T(8,128)(2,1)} %bitcast.16, bf16[4,4,2,48,768]{4,3,2,1,0:T(8,128)(2,1)} %bitcast.17), custom_call_target="tpu_custom_call" | custom-call | tf_op jit(solution)/shard_map/pallas_call | solution.py:246
  3.2 4.5 %collective-permute-done.32.got = bf16[2,4,4,48,768]{4,3,2,1,0:T(8,128)(2,1)S(1)} collective-permute-done((bf16[2,4,4,48,768]{4,3,2,1,0:T(8,128)(2,1)S(1)}, bf16[2,4,4,48,768]{4,3,2,1,0:T(8,128)(2,1)S(1)}, u32[]{:S(2)}, u32[]{:S(2)}) %collective-permute-start.32) | collective-permute-done | bytes 2359328 | tf_op jit(solution)/shard_map/ppermute | solution.py:366
  8.2 1.3 %collective-permute-start.33 = (bf16[2,2,4,48,768]{4,3,2,1,0:T(8,128)(2,1)S(1)}, bf16[2,2,4,48,768]{4,3,2,1,0:T(8,128)(2,1)S(1)}, u32[]{:S(2)}, u32[]{:S(2)}) collective-permute-start(bf16[2,2,4,48,768]{4,3,2,1,0:T(8,128)(2,1)S(1)} %get-tuple-element.95), channel_id=1, source_target_pairs={{0,16},{2,18},{4,20},{6,22},{8,24},{10,26},{12,28},{14,30},{16,0},... | collective-permute-start | bytes 3538952 | tf_op jit(solution)/shard_map/ppermute | solution.py:371
  9.5 3.2 %shard_map.120 = (bf16[128,768]{1,0:T(8,128)(2,1)S(1)}, bf16[2,128,768]{2,1,0:T(8,128)(2,1)S(1)}, f32[1,768]{1,0:T(1,128)S(1)}, bf16[768,1536]{1,0:T(8,128)(2,1)S(1)}, bf16[1536,768]{1,0:T(8,128)(2,1)S(1)}) custom-call(bf16[2,128,768]{2,1,0:T(8,128)(2,1)} %inputs.1, f32[1,768]{1,0:T(1,128)} %gain.3, bf16[768,1536]{1,0:T(8,128)(2,1)} %bitcast.12, ...), custom_call_target="tpu_custom_call" | custom-call | tf_op jit(solution)/shard_map/pallas_call | solution.py:246
  13.8 1.3 %collective-permute-start = (bf16[128,768]{1,0:T(8,128)(2,1)S(1)}, bf16[128,768]{1,0:T(8,128)(2,1)S(1)}, u32[]{:S(2)}, u32[]{:S(2)}) collective-permute-start(bf16[128,768]{1,0:T(8,128)(2,1)S(1)} %shard_map.121.after), channel_id=1, source_target_pairs={{0,64},{1,65},{2,66},{3,67},{4,68},{5,69},{6,70},{7,71},{8,72},{9,... | collective-permute-start | bytes 589832 | tf_op jit(solution)/shard_map/ppermute | solution.py:29
  15.1 4.4 %collective-permute-start.1 = (bf16[128,768]{1,0:T(8,128)(2,1)S(1)}, bf16[128,768]{1,0:T(8,128)(2,1)S(1)}, u32[]{:S(2)}, u32[]{:S(2)}) collective-permute-start(bf16[128,768]{1,0:T(8,128)(2,1)S(1)} %shard_map.121.after), channel_id=1, source_target_pairs={{0,65},{1,64},{2,67},{3,66},{4,69},{5,68},{6,71},{7,70},{8,73},{9,... | collective-permute-start | bytes 589832 | tf_op jit(solution)/shard_map/ppermute | solution.py:29
  19.6 1.3 %collective-permute-start.8 = (bf16[128,768]{1,0:T(8,128)(2,1)S(1)}, bf16[128,768]{1,0:T(8,128)(2,1)S(1)}, u32[]{:S(2)}, u32[]{:S(2)}) collective-permute-start(bf16[128,768]{1,0:T(8,128)(2,1)S(1)} %get-tuple-element.69), channel_id=1, source_target_pairs={{0,64},{1,65},{2,66},{3,67},{4,68},{5,69},{6,70},{7,71},{8,72},{9,... | collective-permute-start | bytes 589832 | tf_op jit(solution)/shard_map/ppermute | solution.py:29
  20.9 1.3 %collective-permute-start.9 = (bf16[128,768]{1,0:T(8,128)(2,1)S(1)}, bf16[128,768]{1,0:T(8,128)(2,1)S(1)}, u32[]{:S(2)}, u32[]{:S(2)}) collective-permute-start(bf16[128,768]{1,0:T(8,128)(2,1)S(1)} %get-tuple-element.69), channel_id=1, source_target_pairs={{0,65},{1,64},{2,67},{3,66},{4,69},{5,68},{6,71},{7,70},{8,73},{9,... | collective-permute-start | bytes 589832 | tf_op jit(solution)/shard_map/ppermute | solution.py:29
  22.2 2.6 %collective-permute-done.1.crossed = bf16[128,768]{1,0:T(8,128)(2,1)S(1)} collective-permute-done((bf16[128,768]{1,0:T(8,128)(2,1)S(1)}, bf16[128,768]{1,0:T(8,128)(2,1)S(1)}, u32[]{:S(2)}, u32[]{:S(2)}) %collective-permute-start.1) | collective-permute-done | bytes 196640 | tf_op jit(solution)/shard_map/ppermute | solution.py:29
  26.3 1.7 %collective-permute-done.9.crossed = bf16[128,768]{1,0:T(8,128)(2,1)S(1)} collective-permute-done((bf16[128,768]{1,0:T(8,128)(2,1)S(1)}, bf16[128,768]{1,0:T(8,128)(2,1)S(1)}, u32[]{:S(2)}, u32[]{:S(2)}) %collective-permute-start.9) | collective-permute-done | bytes 196640 | tf_op jit(solution)/shard_map/ppermute | solution.py:29
  38.8 1.5 %shard_map.130 = (f32[128,1536]{1,0:T(8,128)S(1)}, f32[128,1536]{1,0:T(8,128)S(1)}) custom-call(bf16[128,768]{1,0:T(8,128)(2,1)S(1)} %get-tuple-element.74.refs_0_.rows, bf16[128,768]{1,0:T(8,128)(2,1)S(1)} %get-tuple-element.68.refs_1_.rows.refs_2_, f32[1,768]{1,0:T(1,128)S(1)} %get-tuple-element.58.gain.refs_2_, ...), custom_call_target="tpu_custom_call" | custom-call | tf_op jit(solution)/shard_map/pallas_call | solution.py:246
  43.3 1.3 %collective-permute-start.28 = (bf16[128,768]{1,0:T(8,128)(2,1)S(1)}, bf16[128,768]{1,0:T(8,128)(2,1)S(1)}, u32[]{:S(2)}, u32[]{:S(2)}) collective-permute-start(bf16[128,768]{1,0:T(8,128)(2,1)S(1)} %get-tuple-element.78.part), channel_id=1, source_target_pairs={{64,0},{65,1},{66,2},{67,3},{68,4},{69,5},{70,6},{71,7},{72,8},{73... | collective-permute-start | bytes 589832 | tf_op jit(solution)/shard_map/ppermute | solution.py:29
  44.6 1.3 %collective-permute-start.29 = (bf16[128,768]{1,0:T(8,128)(2,1)S(1)}, bf16[128,768]{1,0:T(8,128)(2,1)S(1)}, u32[]{:S(2)}, u32[]{:S(2)}) collective-permute-start(bf16[128,768]{1,0:T(8,128)(2,1)S(1)} %get-tuple-element.78.part), channel_id=1, source_target_pairs={{64,1},{65,0},{66,3},{67,2},{68,5},{69,4},{70,7},{71,6},{72,9},{73... | collective-permute-start | bytes 589832 | tf_op jit(solution)/shard_map/ppermute | solution.py:29
  46.0 1.3 %collective-permute-start.24 = (bf16[128,768]{1,0:T(8,128)(2,1)S(1)}, bf16[128,768]{1,0:T(8,128)(2,1)S(1)}, u32[]{:S(2)}, u32[]{:S(2)}) collective-permute-start(bf16[128,768]{1,0:T(8,128)(2,1)S(1)} %get-tuple-element.87), channel_id=1, source_target_pairs={{64,0},{65,1},{66,2},{67,3},{68,4},{69,5},{70,6},{71,7},{72,8},{73... | collective-permute-start | bytes 589832 | tf_op jit(solution)/shard_map/ppermute | solution.py:29
  47.3 1.3 %collective-permute-start.25 = (bf16[128,768]{1,0:T(8,128)(2,1)S(1)}, bf16[128,768]{1,0:T(8,128)(2,1)S(1)}, u32[]{:S(2)}, u32[]{:S(2)}) collective-permute-start(bf16[128,768]{1,0:T(8,128)(2,1)S(1)} %get-tuple-element.87), channel_id=1, source_target_pairs={{64,1},{65,0},{66,3},{67,2},{68,5},{69,4},{70,7},{71,6},{72,9},{73... | collective-permute-start | bytes 589832 | tf_op jit(solution)/shard_map/ppermute | solution.py:29
  48.6 37.9 %collective-permute-done.28.straight = bf16[128,768]{1,0:T(8,128)(2,1)S(1)} collective-permute-done((bf16[128,768]{1,0:T(8,128)(2,1)S(1)}, bf16[128,768]{1,0:T(8,128)(2,1)S(1)}, u32[]{:S(2)}, u32[]{:S(2)}) %collective-permute-start.28) | collective-permute-done | bytes 196640 | tf_op jit(solution)/shard_map/ppermute | solution.py:29
  88.7 7.7 %collective-permute-start.30 = (bf16[128,768]{1,0:T(8,128)(2,1)S(1)}, bf16[128,768]{1,0:T(8,128)(2,1)S(1)}, u32[]{:S(2)}, u32[]{:S(2)}) collective-permute-start(bf16[128,768]{1,0:T(8,128)(2,1)S(1)} %get-tuple-element.90.refs_3_), channel_id=1, source_target_pairs={{0,1},{1,0},{2,3},{3,2},{4,5},{5,4},{6,7},{7,6},{8,9},{9,8},{10,11... | collective-permute-start | bytes 589832 | tf_op jit(solution)/shard_map/ppermute | solution.py:29
  96.3 1.3 %collective-permute-start.31 = (bf16[128,768]{1,0:T(8,128)(2,1)S(1)}, bf16[128,768]{1,0:T(8,128)(2,1)S(1)}, u32[]{:S(2)}, u32[]{:S(2)}) collective-permute-start(bf16[128,768]{1,0:T(8,128)(2,1)S(1)} %get-tuple-element.91), channel_id=1, source_target_pairs={{0,64},{1,65},{128,192},{129,193},{2,66},{3,67},{130,194},{131,195... | collective-permute-start | bytes 589832 | tf_op jit(solution)/shard_map/ppermute | solution.py:29
  100.1 1.3 %collective-permute-start.18 = (bf16[256,768]{1,0:T(8,128)(2,1)S(1)}, bf16[256,768]{1,0:T(8,128)(2,1)S(1)}, u32[]{:S(2)}, u32[]{:S(2)}) collective-permute-start(bf16[256,768]{1,0:T(8,128)(2,1)S(1)} %shard_map.135), channel_id=1, source_target_pairs={{64,0},{65,1},{128,64},{129,65},{192,128},{193,129},{66,2},{67,3},... | collective-permute-start | bytes 1179656 | tf_op jit(solution)/shard_map/ppermute | solution.py:29
  103.3 1.5 %collective-permute-done.31.refs_5_ = bf16[128,768]{1,0:T(8,128)(2,1)S(1)} collective-permute-done((bf16[128,768]{1,0:T(8,128)(2,1)S(1)}, bf16[128,768]{1,0:T(8,128)(2,1)S(1)}, u32[]{:S(2)}, u32[]{:S(2)}) %collective-permute-start.31) | collective-permute-done | bytes 196640 | tf_op jit(solution)/shard_map/ppermute | solution.py:29
  104.8 6.2 %collective-permute-start.26 = (bf16[128,768]{1,0:T(8,128)(2,1)S(1)}, bf16[128,768]{1,0:T(8,128)(2,1)S(1)}, u32[]{:S(2)}, u32[]{:S(2)}) collective-permute-start(bf16[128,768]{1,0:T(8,128)(2,1)S(1)} %get-tuple-element.88.refs_0_), channel_id=1, source_target_pairs={{0,1},{1,0},{2,3},{3,2},{4,5},{5,4},{6,7},{7,6},{8,9},{9,8},{10,11... | collective-permute-start | bytes 589832 | tf_op jit(solution)/shard_map/ppermute | solution.py:29
  111.0 1.3 %collective-permute-start.27 = (bf16[128,768]{1,0:T(8,128)(2,1)S(1)}, bf16[128,768]{1,0:T(8,128)(2,1)S(1)}, u32[]{:S(2)}, u32[]{:S(2)}) collective-permute-start(bf16[128,768]{1,0:T(8,128)(2,1)S(1)} %get-tuple-element.89), channel_id=1, source_target_pairs={{0,64},{1,65},{128,192},{129,193},{2,66},{3,67},{130,194},{131,195... | collective-permute-start | bytes 589832 | tf_op jit(solution)/shard_map/ppermute | solution.py:29
  112.4 3.9 %collective-permute-done.26.refs_1_ = bf16[128,768]{1,0:T(8,128)(2,1)S(1)} collective-permute-done((bf16[128,768]{1,0:T(8,128)(2,1)S(1)}, bf16[128,768]{1,0:T(8,128)(2,1)S(1)}, u32[]{:S(2)}, u32[]{:S(2)}) %collective-permute-start.26) | collective-permute-done | bytes 196640 | tf_op jit(solution)/shard_map/ppermute | solution.py:29
  118.2 4.4 %collective-permute-done.36.got = bf16[2,48,768]{2,1,0:T(8,128)(2,1)S(1)} collective-permute-done((bf16[2,48,768]{2,1,0:T(8,128)(2,1)S(1)}, bf16[2,48,768]{2,1,0:T(8,128)(2,1)S(1)}, u32[]{:S(2)}, u32[]{:S(2)}) %collective-permute-start.36) | collective-permute-done | bytes 147488 | tf_op jit(solution)/shard_map/ppermute | solution.py:371
  (85 shorter events, 26.0 us)
Async XLA Ops:
  3.1 4.6 %collective-permute-start.32 = (bf16[2,4,4,48,768]{4,3,2,1,0:T(8,128)(2,1)S(1)}, bf16[2,4,4,48,768]{4,3,2,1,0:T(8,128)(2,1)S(1)}, u32[]{:S(2)}, u32[]{:S(2)}) collective-permute-start(bf16[2,4,4,48,768]{4,3,2,1,0:T(8,128)(2,1)S(1)} %get-tuple-element.93), channel_id=1, source_target_pairs={{0,2},{2,0},{4,6},{6,4},{8,10},{10,8},{12,14},{14,12},{16,18},{18,... | collective-permute-start | bytes 7077896 | tf_op jit(solution)/shard_map/ppermute | solution.py:366
  8.2 28.1 %collective-permute-start.33 = (bf16[2,2,4,48,768]{4,3,2,1,0:T(8,128)(2,1)S(1)}, bf16[2,2,4,48,768]{4,3,2,1,0:T(8,128)(2,1)S(1)}, u32[]{:S(2)}, u32[]{:S(2)}) collective-permute-start(bf16[2,2,4,48,768]{4,3,2,1,0:T(8,128)(2,1)S(1)} %get-tuple-element.95), channel_id=1, source_target_pairs={{0,16},{2,18},{4,20},{6,22},{8,24},{10,26},{12,28},{14,30},{16,0},... | collective-permute-start | bytes 3538952 | tf_op jit(solution)/shard_map/ppermute | solution.py:371
  13.8 8.4 %collective-permute-start = (bf16[128,768]{1,0:T(8,128)(2,1)S(1)}, bf16[128,768]{1,0:T(8,128)(2,1)S(1)}, u32[]{:S(2)}, u32[]{:S(2)}) collective-permute-start(bf16[128,768]{1,0:T(8,128)(2,1)S(1)} %shard_map.121.after), channel_id=1, source_target_pairs={{0,64},{1,65},{2,66},{3,67},{4,68},{5,69},{6,70},{7,71},{8,72},{9,... | collective-permute-start | bytes 589832 | tf_op jit(solution)/shard_map/ppermute | solution.py:29
  15.1 9.7 %collective-permute-start.1 = (bf16[128,768]{1,0:T(8,128)(2,1)S(1)}, bf16[128,768]{1,0:T(8,128)(2,1)S(1)}, u32[]{:S(2)}, u32[]{:S(2)}) collective-permute-start(bf16[128,768]{1,0:T(8,128)(2,1)S(1)} %shard_map.121.after), channel_id=1, source_target_pairs={{0,65},{1,64},{2,67},{3,66},{4,69},{5,68},{6,71},{7,70},{8,73},{9,... | collective-permute-start | bytes 589832 | tf_op jit(solution)/shard_map/ppermute | solution.py:29
  19.6 6.7 %collective-permute-start.8 = (bf16[128,768]{1,0:T(8,128)(2,1)S(1)}, bf16[128,768]{1,0:T(8,128)(2,1)S(1)}, u32[]{:S(2)}, u32[]{:S(2)}) collective-permute-start(bf16[128,768]{1,0:T(8,128)(2,1)S(1)} %get-tuple-element.69), channel_id=1, source_target_pairs={{0,64},{1,65},{2,66},{3,67},{4,68},{5,69},{6,70},{7,71},{8,72},{9,... | collective-permute-start | bytes 589832 | tf_op jit(solution)/shard_map/ppermute | solution.py:29
  20.9 7.1 %collective-permute-start.9 = (bf16[128,768]{1,0:T(8,128)(2,1)S(1)}, bf16[128,768]{1,0:T(8,128)(2,1)S(1)}, u32[]{:S(2)}, u32[]{:S(2)}) collective-permute-start(bf16[128,768]{1,0:T(8,128)(2,1)S(1)} %get-tuple-element.69), channel_id=1, source_target_pairs={{0,65},{1,64},{2,67},{3,66},{4,69},{5,68},{6,71},{7,70},{8,73},{9,... | collective-permute-start | bytes 589832 | tf_op jit(solution)/shard_map/ppermute | solution.py:29
  24.9 4.5 %collective-permute-start.2 = (bf16[128,768]{1,0:T(8,128)(2,1)S(1)}, bf16[128,768]{1,0:T(8,128)(2,1)S(1)}, u32[]{:S(2)}, u32[]{:S(2)}) collective-permute-start(bf16[128,768]{1,0:T(8,128)(2,1)S(1)} %get-tuple-element.61), channel_id=1, source_target_pairs={{64,128},{65,129},{66,130},{67,131},{68,132},{69,133},{70,134},{71... | collective-permute-start | bytes 589832 | tf_op jit(solution)/shard_map/ppermute | solution.py:29
  32.2 5.2 %collective-permute-start.12 = (bf16[128,768]{1,0:T(8,128)(2,1)S(1)}, bf16[128,768]{1,0:T(8,128)(2,1)S(1)}, u32[]{:S(2)}, u32[]{:S(2)}) collective-permute-start(bf16[128,768]{1,0:T(8,128)(2,1)S(1)} %get-tuple-element.72), channel_id=1, source_target_pairs={{128,192},{129,193},{130,194},{131,195},{132,196},{133,197},{134,1... | collective-permute-start | bytes 589832 | tf_op jit(solution)/shard_map/ppermute | solution.py:29
  33.8 6.5 %collective-permute-start.6 = (bf16[128,768]{1,0:T(8,128)(2,1)S(1)}, bf16[128,768]{1,0:T(8,128)(2,1)S(1)}, u32[]{:S(2)}, u32[]{:S(2)}) collective-permute-start(bf16[128,768]{1,0:T(8,128)(2,1)S(1)} %get-tuple-element.67), channel_id=1, source_target_pairs={{192,128},{193,129},{194,130},{195,131},{196,132},{197,133},{198,1... | collective-permute-start | bytes 589832 | tf_op jit(solution)/shard_map/ppermute | solution.py:29
  34.5 5.9 %collective-permute-start.7 = (bf16[128,768]{1,0:T(8,128)(2,1)S(1)}, bf16[128,768]{1,0:T(8,128)(2,1)S(1)}, u32[]{:S(2)}, u32[]{:S(2)}) collective-permute-start(bf16[128,768]{1,0:T(8,128)(2,1)S(1)} %get-tuple-element.67), channel_id=1, source_target_pairs={{192,129},{193,128},{194,131},{195,130},{196,133},{197,132},{198,1... | collective-permute-start | bytes 589832 | tf_op jit(solution)/shard_map/ppermute | solution.py:29
  36.6 61.0 %collective-permute-start.34 = (bf16[2,4,48,768]{3,2,1,0:T(8,128)(2,1)S(1)}, bf16[2,4,48,768]{3,2,1,0:T(8,128)(2,1)S(1)}, u32[]{:S(2)}, u32[]{:S(2)}) collective-permute-start(bf16[2,4,48,768]{3,2,1,0:T(8,128)(2,1)S(1)} %get-tuple-element.97), channel_id=1, source_target_pairs={{0,48},{2,50},{4,52},{6,54},{8,56},{10,58},{12,60},{14,62},{16,32}... | collective-permute-start | bytes 1769480 | tf_op jit(solution)/shard_map/ppermute | solution.py:371
  43.3 43.2 %collective-permute-start.28 = (bf16[128,768]{1,0:T(8,128)(2,1)S(1)}, bf16[128,768]{1,0:T(8,128)(2,1)S(1)}, u32[]{:S(2)}, u32[]{:S(2)}) collective-permute-start(bf16[128,768]{1,0:T(8,128)(2,1)S(1)} %get-tuple-element.78.part), channel_id=1, source_target_pairs={{64,0},{65,1},{66,2},{67,3},{68,4},{69,5},{70,6},{71,7},{72,8},{73... | collective-permute-start | bytes 589832 | tf_op jit(solution)/shard_map/ppermute | solution.py:29
  44.6 42.9 %collective-permute-start.29 = (bf16[128,768]{1,0:T(8,128)(2,1)S(1)}, bf16[128,768]{1,0:T(8,128)(2,1)S(1)}, u32[]{:S(2)}, u32[]{:S(2)}) collective-permute-start(bf16[128,768]{1,0:T(8,128)(2,1)S(1)} %get-tuple-element.78.part), channel_id=1, source_target_pairs={{64,1},{65,0},{66,3},{67,2},{68,5},{69,4},{70,7},{71,6},{72,9},{73... | collective-permute-start | bytes 589832 | tf_op jit(solution)/shard_map/ppermute | solution.py:29
  46.0 53.4 %collective-permute-start.24 = (bf16[128,768]{1,0:T(8,128)(2,1)S(1)}, bf16[128,768]{1,0:T(8,128)(2,1)S(1)}, u32[]{:S(2)}, u32[]{:S(2)}) collective-permute-start(bf16[128,768]{1,0:T(8,128)(2,1)S(1)} %get-tuple-element.87), channel_id=1, source_target_pairs={{64,0},{65,1},{66,2},{67,3},{68,4},{69,5},{70,6},{71,7},{72,8},{73... | collective-permute-start | bytes 589832 | tf_op jit(solution)/shard_map/ppermute | solution.py:29
  47.3 52.8 %collective-permute-start.25 = (bf16[128,768]{1,0:T(8,128)(2,1)S(1)}, bf16[128,768]{1,0:T(8,128)(2,1)S(1)}, u32[]{:S(2)}, u32[]{:S(2)}) collective-permute-start(bf16[128,768]{1,0:T(8,128)(2,1)S(1)} %get-tuple-element.87), channel_id=1, source_target_pairs={{64,1},{65,0},{66,3},{67,2},{68,5},{69,4},{70,7},{71,6},{72,9},{73... | collective-permute-start | bytes 589832 | tf_op jit(solution)/shard_map/ppermute | solution.py:29
  88.7 12.8 %collective-permute-start.30 = (bf16[128,768]{1,0:T(8,128)(2,1)S(1)}, bf16[128,768]{1,0:T(8,128)(2,1)S(1)}, u32[]{:S(2)}, u32[]{:S(2)}) collective-permute-start(bf16[128,768]{1,0:T(8,128)(2,1)S(1)} %get-tuple-element.90.refs_3_), channel_id=1, source_target_pairs={{0,1},{1,0},{2,3},{3,2},{4,5},{5,4},{6,7},{7,6},{8,9},{9,8},{10,11... | collective-permute-start | bytes 589832 | tf_op jit(solution)/shard_map/ppermute | solution.py:29
  96.3 8.5 %collective-permute-start.31 = (bf16[128,768]{1,0:T(8,128)(2,1)S(1)}, bf16[128,768]{1,0:T(8,128)(2,1)S(1)}, u32[]{:S(2)}, u32[]{:S(2)}) collective-permute-start(bf16[128,768]{1,0:T(8,128)(2,1)S(1)} %get-tuple-element.91), channel_id=1, source_target_pairs={{0,64},{1,65},{128,192},{129,193},{2,66},{3,67},{130,194},{131,195... | collective-permute-start | bytes 589832 | tf_op jit(solution)/shard_map/ppermute | solution.py:29
  98.5 12.5 %collective-permute-start.35 = (bf16[2,2,48,768]{3,2,1,0:T(8,128)(2,1)S(1)}, bf16[2,2,48,768]{3,2,1,0:T(8,128)(2,1)S(1)}, u32[]{:S(2)}, u32[]{:S(2)}) collective-permute-start(bf16[2,2,48,768]{3,2,1,0:T(8,128)(2,1)S(1)} %get-tuple-element.99), channel_id=1, source_target_pairs={{0,4},{2,6},{4,0},{6,2},{8,12},{10,14},{12,8},{14,10},{16,20},{18,... | collective-permute-start | bytes 884744 | tf_op jit(solution)/shard_map/ppermute | solution.py:371
  99.4 17.0 %collective-permute-start.23 = (bf16[256,768]{1,0:T(8,128)(2,1)S(1)}, bf16[256,768]{1,0:T(8,128)(2,1)S(1)}, u32[]{:S(2)}, u32[]{:S(2)}) collective-permute-start(bf16[256,768]{1,0:T(8,128)(2,1)S(1)} %shard_map.139), channel_id=1, source_target_pairs={{64,128},{65,129},{66,130},{67,131},{68,132},{69,133},{70,134},{71... | collective-permute-start | bytes 1179656 | tf_op jit(solution)/shard_map/ppermute | solution.py:29
  100.1 17.2 %collective-permute-start.18 = (bf16[256,768]{1,0:T(8,128)(2,1)S(1)}, bf16[256,768]{1,0:T(8,128)(2,1)S(1)}, u32[]{:S(2)}, u32[]{:S(2)}) collective-permute-start(bf16[256,768]{1,0:T(8,128)(2,1)S(1)} %shard_map.135), channel_id=1, source_target_pairs={{64,0},{65,1},{128,64},{129,65},{192,128},{193,129},{66,2},{67,3},... | collective-permute-start | bytes 1179656 | tf_op jit(solution)/shard_map/ppermute | solution.py:29
  101.4 15.9 %collective-permute-start.17 = (bf16[256,768]{1,0:T(8,128)(2,1)S(1)}, bf16[256,768]{1,0:T(8,128)(2,1)S(1)}, u32[]{:S(2)}, u32[]{:S(2)}) collective-permute-start(bf16[256,768]{1,0:T(8,128)(2,1)S(1)} %shard_map.134.mixed), channel_id=1, source_target_pairs={{192,193},{193,192},{194,195},{195,194},{196,197},{197,196},{198,1... | collective-permute-start | bytes 1179656 | tf_op jit(solution)/shard_map/ppermute | solution.py:29
  104.8 11.5 %collective-permute-start.26 = (bf16[128,768]{1,0:T(8,128)(2,1)S(1)}, bf16[128,768]{1,0:T(8,128)(2,1)S(1)}, u32[]{:S(2)}, u32[]{:S(2)}) collective-permute-start(bf16[128,768]{1,0:T(8,128)(2,1)S(1)} %get-tuple-element.88.refs_0_), channel_id=1, source_target_pairs={{0,1},{1,0},{2,3},{3,2},{4,5},{5,4},{6,7},{7,6},{8,9},{9,8},{10,11... | collective-permute-start | bytes 589832 | tf_op jit(solution)/shard_map/ppermute | solution.py:29
  111.0 5.4 %collective-permute-start.27 = (bf16[128,768]{1,0:T(8,128)(2,1)S(1)}, bf16[128,768]{1,0:T(8,128)(2,1)S(1)}, u32[]{:S(2)}, u32[]{:S(2)}) collective-permute-start(bf16[128,768]{1,0:T(8,128)(2,1)S(1)} %get-tuple-element.89), channel_id=1, source_target_pairs={{0,64},{1,65},{128,192},{129,193},{2,66},{3,67},{130,194},{131,195... | collective-permute-start | bytes 589832 | tf_op jit(solution)/shard_map/ppermute | solution.py:29
  116.3 6.4 %collective-permute-start.36 = (bf16[2,48,768]{2,1,0:T(8,128)(2,1)S(1)}, bf16[2,48,768]{2,1,0:T(8,128)(2,1)S(1)}, u32[]{:S(2)}, u32[]{:S(2)}) collective-permute-start(bf16[2,48,768]{2,1,0:T(8,128)(2,1)S(1)} %get-tuple-element.101), channel_id=1, source_target_pairs={{0,12},{2,14},{4,8},{6,10},{8,4},{10,6},{12,0},{14,2},{16,28},{18,... | collective-permute-start | bytes 442376 | tf_op jit(solution)/shard_map/ppermute | solution.py:371
  (16 other events, 85.0 us)
